TPU v7x, 32 devices: a 4x4x1 block of a 4x4x8 slice. The times are simulated.
32 devices in a mesh: sweep: 1 (over z), data: 4 (over y), ent: 8 (over x, core).
Axes of the slice: x: 4, y: 4, z: 1, core: 2. Of those that a mesh axis runs over, the one named last changes fastest.
The devices are a block of a 4x4x8 slice.
Arguments:
- ent_table: float32 [32768, 400], P(('sweep', 'ent'))
- ent_state: float32 [32768], P(('sweep', 'ent'))
- rel_table: float32 [107, 400], P('sweep')
- head_idx: int32 [8, 8, 8192], P(('sweep', 'ent'), None, 'data')
- tail_idx: int32 [8, 8, 8192], P(('sweep', 'ent'), None, 'data')
- rel_idx: int32 [8, 8, 8192], P(('sweep', 'ent'), None, 'data')
- edge_mask: int32 [8, 8, 8192], P(('sweep', 'ent'), None, 'data')
- neg_idx: int32 [8, 8, 1024], P(('sweep', 'ent'))
Outputs:
- output 1: float32 [32768, 400], P(('sweep', 'ent'))
- output 2: float32 [32768], P(('sweep', 'ent'))
- output 3: float32 [107, 400], P('sweep')
- output 4: float32 [8, 8], P(('sweep', 'ent'))
All inputs are finite; a program needn't handle non-finite values.
Results may differ from a plain program's by a relative error of at most 0.001.
Values are sent between devices in bfloat16 or wider.
A program may use at most 768 MiB of HBM per device.

v0:
```python
import jax
import jax.numpy as jnp
from jax import lax
from jax.sharding import PartitionSpec as P

LR_SCALE = 0.2
EPSILON = 1e-8


def adagrad(param_rows, accum_rows, grad_rows, learn_rate):
    accum_new = accum_rows + jnp.mean(grad_rows * grad_rows, axis=-1)
    step_rows = grad_rows / jnp.sqrt(accum_new + EPSILON)[..., None]
    return param_rows - learn_rate * step_rows, accum_new


def bucket_terms(head_rows, rel_rows, tail_bf, neg_bf, weight):
    half_dim = head_rows.shape[-1] // 2
    re_h = head_rows[..., :half_dim]
    im_h = head_rows[..., half_dim:]
    re_r = rel_rows[..., :half_dim]
    im_r = rel_rows[..., half_dim:]
    query_vec = jnp.concatenate([re_h * re_r - im_h * im_r, re_h * im_r + im_h * re_r], axis=-1)
    query_bf = query_vec.astype(jnp.bfloat16)
    pos_score = jnp.einsum('...bd,...bd->...b', query_bf, tail_bf, preferred_element_type=jnp.float32)
    neg_score = jnp.einsum('...bd,...nd->...bn', query_bf, neg_bf, preferred_element_type=jnp.float32)
    top_score = jnp.maximum(jnp.max(neg_score, axis=-1), pos_score)
    pos_exp = jnp.exp(pos_score - top_score)
    neg_exp = jnp.exp(neg_score - top_score[..., None])
    exp_total = pos_exp + jnp.sum(neg_exp, axis=-1)
    log_total = top_score + jnp.log(exp_total)
    loss_sum = jnp.sum(weight * (log_total - pos_score), axis=-1)
    d_pos = weight * (pos_exp / exp_total - 1.0)
    d_neg = ((weight / exp_total)[..., None] * neg_exp).astype(jnp.bfloat16)
    grad_query = d_pos[..., None] * tail_bf + jnp.einsum('...bn,...nd->...bd', d_neg, neg_bf, preferred_element_type=jnp.float32)
    grad_tail = d_pos[..., None] * query_bf
    grad_neg = jnp.einsum('...bn,...bd->...nd', d_neg, query_bf, preferred_element_type=jnp.float32)
    re_g = grad_query[..., :half_dim]
    im_g = grad_query[..., half_dim:]
    grad_head = jnp.concatenate([re_g * re_r + im_g * im_r, im_g * re_r - re_g * im_r], axis=-1)
    grad_rel = jnp.concatenate([re_g * re_h + im_g * im_h, im_g * re_h - re_g * im_h], axis=-1)
    return loss_sum, grad_head, grad_rel, grad_tail, grad_neg


def solution(mesh):
    groups = mesh.shape['ent']
    data_reps = mesh.shape['data']
    row_spec = P(('sweep', 'ent'), None)
    edge_spec = P(('sweep', 'ent'), None, 'data')

    def device_fn(ent_table, ent_state, rel_table, head_idx, tail_idx, rel_idx, edge_mask, neg_idx):
        part_rows, emb_width = ent_table.shape
        rel_rows = rel_table.shape[0]
        bucket_edges = head_idx.shape[2] * data_reps
        learn_rate = LR_SCALE * emb_width ** -0.25
        table_now = ent_table
        state_now = ent_state
        rel_now = rel_table
        rel_state = jnp.zeros((rel_rows,), jnp.float32)
        loss_list = []
        for step_idx in range(groups):
            fetch_perm = [(source, (source - step_idx) % groups) for source in range(groups)]
            return_perm = [(source, (source + step_idx) % groups) for source in range(groups)]
            table_bf = table_now.astype(jnp.bfloat16)
            tail_table = table_bf if step_idx == 0 else lax.ppermute(table_bf, 'ent', fetch_perm)
            h_ids = head_idx[0, step_idx]
            t_ids = tail_idx[0, step_idx]
            r_ids = rel_idx[0, step_idx]
            n_ids = neg_idx[0, step_idx]
            weight = edge_mask[0, step_idx].astype(jnp.float32)
            head_rows = jnp.take(table_now, h_ids, axis=0)
            rel_rows_now = jnp.take(rel_now, r_ids, axis=0)
            tail_bf = jnp.take(tail_table, t_ids, axis=0)
            neg_bf = jnp.take(tail_table, n_ids, axis=0)
            loss_sum, g_head, g_rel, g_tail, g_neg = bucket_terms(head_rows, rel_rows_now, tail_bf, neg_bf, weight)
            sent_rows = jnp.concatenate([g_tail, g_neg], axis=0)
            sent_ids = jnp.concatenate([t_ids, n_ids])
            if step_idx > 0:
                sent_rows = lax.ppermute(sent_rows, 'ent', return_perm)
                sent_ids = lax.ppermute(sent_ids, 'ent', return_perm)
            ent_grad = jax.ops.segment_sum(jnp.concatenate([g_head, sent_rows], axis=0), jnp.concatenate([h_ids, sent_ids]), num_segments=part_rows)
            ent_grad = lax.psum(ent_grad, 'data')
            rel_grad = lax.psum(jax.ops.segment_sum(g_rel, r_ids, num_segments=rel_rows), ('data', 'ent'))
            loss_list.append(lax.psum(loss_sum, 'data') / bucket_edges)
            table_now, state_now = adagrad(table_now, state_now, ent_grad, learn_rate)
            rel_now, rel_state = adagrad(rel_now, rel_state, rel_grad, learn_rate)
        return table_now, state_now, rel_now, jnp.stack(loss_list)[None, :]

    return jax.shard_map(device_fn, mesh=mesh, in_specs=(row_spec, P(('sweep', 'ent')), P('sweep', None), edge_spec, edge_spec, edge_spec, edge_spec, P(('sweep', 'ent'), None, None)), out_specs=(row_spec, P(('sweep', 'ent')), P('sweep', None), row_spec), check_vma=False)
```

profile of v0, /device:TPU:97, one launch (start us, length us, event | category | flops | bytes accessed | tf_op | source)
XLA Modules:
  0.0 4068.9 jit_solution(3416057009412966340)
XLA Ops:
  122.4 35.0 scatter_custom_fusion
  181.8 134.4 %all-reduce.18.cloned.1.call-done = f32[4096,400]{1,0:T(8,128)} async-done(((f32[4096,400]{1,0:T(8,128)}), f32[4096,400]{1,0:T(8,128)}) %all-reduce.18.cloned.1.call-update) | async-done | bytes 6553616 | tf_op jit(solution)/shard_map/psum | solution.py:81
  337.5 74.6 %all-reduce.20.cloned.1.call-done = f32[107,400]{1,0:T(8,128)} async-done(((f32[107,400]{1,0:T(8,128)}), f32[107,400]{1,0:T(8,128)}) %all-reduce.20.cloned.1.call-update) | async-done | bytes 171216 | tf_op jit(solution)/shard_map/psum | solution.py:82
  494.2 53.2 %collective-permute-done = s32[3072]{0:T(1024)S(1)} collective-permute-done((s32[3072]{0:T(1024)S(1)}, s32[3072]{0:T(1024)S(1)}, u32[]{:S(2)}, u32[]{:S(2)}) %collective-permute-start) | collective-permute-done | bytes 12320 | tf_op jit(solution)/shard_map/ppermute | solution.py:79
  573.2 35.2 scatter_custom_fusion.2
  612.1 151.4 %all-reduce.22.cloned.1.call-done = f32[4096,400]{1,0:T(8,128)} async-done(((f32[4096,400]{1,0:T(8,128)}), f32[4096,400]{1,0:T(8,128)}) %all-reduce.22.cloned.1.call-update) | async-done | bytes 6553616 | tf_op jit(solution)/shard_map/psum | solution.py:81
  804.6 91.7 %all-reduce.24.cloned.1.call-done = f32[107,400]{1,0:T(8,128)} async-done(((f32[107,400]{1,0:T(8,128)}), f32[107,400]{1,0:T(8,128)}) %all-reduce.24.cloned.1.call-update) | async-done | bytes 171216 | tf_op jit(solution)/shard_map/psum | solution.py:82
  978.7 106.9 %collective-permute-done.3 = s32[3072]{0:T(1024)S(1)} collective-permute-done((s32[3072]{0:T(1024)S(1)}, s32[3072]{0:T(1024)S(1)}, u32[]{:S(2)}, u32[]{:S(2)}) %collective-permute-start.3) | collective-permute-done | bytes 12320 | tf_op jit(solution)/shard_map/ppermute | solution.py:79
  1110.8 35.0 scatter_custom_fusion.4
  1149.4 149.8 %all-reduce.26.cloned.1.call-done = f32[4096,400]{1,0:T(8,128)} async-done(((f32[4096,400]{1,0:T(8,128)}), f32[4096,400]{1,0:T(8,128)}) %all-reduce.26.cloned.1.call-update) | async-done | bytes 6553616 | tf_op jit(solution)/shard_map/psum | solution.py:81
  1345.5 93.6 %all-reduce.28.cloned.1.call-done = f32[107,400]{1,0:T(8,128)} async-done(((f32[107,400]{1,0:T(8,128)}), f32[107,400]{1,0:T(8,128)}) %all-reduce.28.cloned.1.call-update) | async-done | bytes 171216 | tf_op jit(solution)/shard_map/psum | solution.py:82
  1524.7 106.5 %collective-permute-done.6 = s32[3072]{0:T(1024)S(1)} collective-permute-done((s32[3072]{0:T(1024)S(1)}, s32[3072]{0:T(1024)S(1)}, u32[]{:S(2)}, u32[]{:S(2)}) %collective-permute-start.6) | collective-permute-done | bytes 12320 | tf_op jit(solution)/shard_map/ppermute | solution.py:79
  1657.7 35.0 scatter_custom_fusion.6
  1696.3 149.0 %all-reduce.30.cloned.1.call-done = f32[4096,400]{1,0:T(8,128)} async-done(((f32[4096,400]{1,0:T(8,128)}), f32[4096,400]{1,0:T(8,128)}) %all-reduce.30.cloned.1.call-update) | async-done | bytes 6553616 | tf_op jit(solution)/shard_map/psum | solution.py:81
  1886.8 118.6 %all-reduce.32.cloned.1.call-done = f32[107,400]{1,0:T(8,128)} async-done(((f32[107,400]{1,0:T(8,128)}), f32[107,400]{1,0:T(8,128)}) %all-reduce.32.cloned.1.call-update) | async-done | bytes 171216 | tf_op jit(solution)/shard_map/psum | solution.py:82
  2087.9 106.3 %collective-permute-done.9 = s32[3072]{0:T(1024)S(1)} collective-permute-done((s32[3072]{0:T(1024)S(1)}, s32[3072]{0:T(1024)S(1)}, u32[]{:S(2)}, u32[]{:S(2)}) %collective-permute-start.9) | collective-permute-done | bytes 12320 | tf_op jit(solution)/shard_map/ppermute | solution.py:79
  2219.8 35.0 scatter_custom_fusion.8
  2258.5 150.9 %all-reduce.34.cloned.1.call-done = f32[4096,400]{1,0:T(8,128)} async-done(((f32[4096,400]{1,0:T(8,128)}), f32[4096,400]{1,0:T(8,128)}) %all-reduce.34.cloned.1.call-update) | async-done | bytes 6553616 | tf_op jit(solution)/shard_map/psum | solution.py:81
  2455.7 93.0 %all-reduce.36.cloned.1.call-done = f32[107,400]{1,0:T(8,128)} async-done(((f32[107,400]{1,0:T(8,128)}), f32[107,400]{1,0:T(8,128)}) %all-reduce.36.cloned.1.call-update) | async-done | bytes 171216 | tf_op jit(solution)/shard_map/psum | solution.py:82
  2635.3 103.6 %collective-permute-done.12 = s32[3072]{0:T(1024)S(1)} collective-permute-done((s32[3072]{0:T(1024)S(1)}, s32[3072]{0:T(1024)S(1)}, u32[]{:S(2)}, u32[]{:S(2)}) %collective-permute-start.12) | collective-permute-done | bytes 12320 | tf_op jit(solution)/shard_map/ppermute | solution.py:79
  2765.4 35.0 scatter_custom_fusion.10
  2804.1 151.9 %all-reduce.38.cloned.1.call-done = f32[4096,400]{1,0:T(8,128)} async-done(((f32[4096,400]{1,0:T(8,128)}), f32[4096,400]{1,0:T(8,128)}) %all-reduce.38.cloned.1.call-update) | async-done | bytes 6553616 | tf_op jit(solution)/shard_map/psum | solution.py:81
  2996.1 92.4 %all-reduce.40.cloned.1.call-done = f32[107,400]{1,0:T(8,128)} async-done(((f32[107,400]{1,0:T(8,128)}), f32[107,400]{1,0:T(8,128)}) %all-reduce.40.cloned.1.call-update) | async-done | bytes 171216 | tf_op jit(solution)/shard_map/psum | solution.py:82
  3170.5 105.1 %collective-permute-done.15 = s32[3072]{0:T(1024)S(1)} collective-permute-done((s32[3072]{0:T(1024)S(1)}, s32[3072]{0:T(1024)S(1)}, u32[]{:S(2)}, u32[]{:S(2)}) %collective-permute-start.15) | collective-permute-done | bytes 12320 | tf_op jit(solution)/shard_map/ppermute | solution.py:79
  3300.8 35.0 scatter_custom_fusion.12
  3339.4 152.2 %all-reduce.42.cloned.1.call-done = f32[4096,400]{1,0:T(8,128)} async-done(((f32[4096,400]{1,0:T(8,128)}), f32[4096,400]{1,0:T(8,128)}) %all-reduce.42.cloned.1.call-update) | async-done | bytes 6553616 | tf_op jit(solution)/shard_map/psum | solution.py:81
  3536.4 90.9 %all-reduce.44.cloned.1.call-done = f32[107,400]{1,0:T(8,128)} async-done(((f32[107,400]{1,0:T(8,128)}), f32[107,400]{1,0:T(8,128)}) %all-reduce.44.cloned.1.call-update) | async-done | bytes 171216 | tf_op jit(solution)/shard_map/psum | solution.py:82
  3713.8 54.1 %collective-permute-done.18 = s32[3072]{0:T(1024)S(1)} collective-permute-done((s32[3072]{0:T(1024)S(1)}, s32[3072]{0:T(1024)S(1)}, u32[]{:S(2)}, u32[]{:S(2)}) %collective-permute-start.18) | collective-permute-done | bytes 12320 | tf_op jit(solution)/shard_map/ppermute | solution.py:79
  3777.8 14.1 scatter_custom_fusion.15
  3810.0 35.0 scatter_custom_fusion.14
  3859.7 25.1 all-reduce.48.cloned.1.call-done
  3887.8 153.8 %all-reduce.46.cloned.1.call-done = f32[4096,400]{1,0:T(8,128)} async-done(((f32[4096,400]{1,0:T(8,128)}), f32[4096,400]{1,0:T(8,128)}) %all-reduce.46.cloned.1.call-update) | async-done | bytes 6553616 | tf_op jit(solution)/shard_map/psum | solution.py:81
  (695 shorter events, 1244.5 us)
Async XLA Ops:
  7.2 309.1 %all-reduce.18.cloned.1.call-start = ((), (), s32[]{:S(2)}) async-start(), calls=%async_computation | async-start | bytes 16777216 | tf_op jit(solution)/shard_map/psum | solution.py:81
  157.5 254.6 %all-reduce.20.cloned.1.call-start = ((), (), s32[]{:S(2)}) async-start(), calls=%async_computation.1 | async-start | bytes 458752 | tf_op jit(solution)/shard_map/psum | solution.py:82
  180.1 583.4 %all-reduce.22.cloned.1.call-start = ((), (), s32[]{:S(2)}) async-start(), calls=%async_computation.2 | async-start | bytes 16777216 | tf_op jit(solution)/shard_map/psum | solution.py:81
  335.4 117.7 %collective-permute-start.1 = (bf16[4096,400]{0,1:T(8,128)(2,1)}, bf16[4096,400]{0,1:T(8,128)(2,1)}, u32[]{:S(2)}, u32[]{:S(2)}) collective-permute-start(bf16[4096,400]{0,1:T(8,128)(2,1)} %copy.102), channel_id=1, source_target_pairs={{0,7},{1,0},{2,1},{3,2},{4,3},{5,4},{6,5},{7,6},{8,15},{9,8},{10,9... | collective-permute-start | bytes 9830408 | tf_op jit(solution)/shard_map/ppermute | solution.py:64
  608.5 287.8 %all-reduce.24.cloned.1.call-start = ((), (), s32[]{:S(2)}) async-start(), calls=%async_computation.3 | async-start | bytes 458752 | tf_op jit(solution)/shard_map/psum | solution.py:82
  782.7 158.1 %collective-permute-start.4 = (bf16[4096,400]{0,1:T(8,128)(2,1)}, bf16[4096,400]{0,1:T(8,128)(2,1)}, u32[]{:S(2)}, u32[]{:S(2)}) collective-permute-start(bf16[4096,400]{0,1:T(8,128)(2,1)} %copy.110), channel_id=1, source_target_pairs={{0,6},{1,7},{2,0},{3,1},{4,2},{5,3},{6,4},{7,5},{8,14},{9,15},{10,... | collective-permute-start | bytes 9830408 | tf_op jit(solution)/shard_map/ppermute | solution.py:64
  804.5 494.6 %all-reduce.26.cloned.1.call-start = ((), (), s32[]{:S(2)}) async-start(), calls=%async_computation.4 | async-start | bytes 16777216 | tf_op jit(solution)/shard_map/psum | solution.py:81
  976.6 117.6 %collective-permute-start.5 = (f32[3072,400]{0,1:T(8,128)S(1)}, f32[3072,400]{0,1:T(8,128)}, u32[]{:S(2)}, u32[]{:S(2)}) collective-permute-start(f32[3072,400]{0,1:T(8,128)S(1)} %pad_maximum_fusion.9), channel_id=1, source_target_pairs={{0,2},{1,3},{2,4},{3,5},{4,6},{5,7},{6,0},{7,1},{8,10},{9,11},{10,... | collective-permute-start | bytes 14745608 | tf_op jit(solution)/shard_map/ppermute | solution.py:78
  977.7 107.9 %collective-permute-start.3 = (s32[3072]{0:T(1024)S(1)}, s32[3072]{0:T(1024)S(1)}, u32[]{:S(2)}, u32[]{:S(2)}) collective-permute-start(s32[3072]{0:T(1024)S(1)} %pad_add_fusion.9), channel_id=1, source_target_pairs={{0,2},{1,3},{2,4},{3,5},{4,6},{5,7},{6,0},{7,1},{8,10},{9,11},{10,... | collective-permute-start | bytes 36872 | tf_op jit(solution)/shard_map/ppermute | solution.py:79
  1145.9 293.1 %all-reduce.28.cloned.1.call-start = ((), (), s32[]{:S(2)}) async-start(), calls=%async_computation.5 | async-start | bytes 458752 | tf_op jit(solution)/shard_map/psum | solution.py:82
  1318.3 162.5 %collective-permute-start.7 = (bf16[4096,400]{0,1:T(8,128)(2,1)}, bf16[4096,400]{0,1:T(8,128)(2,1)}, u32[]{:S(2)}, u32[]{:S(2)}) collective-permute-start(bf16[4096,400]{0,1:T(8,128)(2,1)} %copy.118), channel_id=1, source_target_pairs={{0,5},{1,6},{2,7},{3,0},{4,1},{5,2},{6,3},{7,4},{8,13},{9,14},{10,... | collective-permute-start | bytes 9830408 | tf_op jit(solution)/shard_map/ppermute | solution.py:64
  1344.6 500.7 %all-reduce.30.cloned.1.call-start = ((), (), s32[]{:S(2)}) async-start(), calls=%async_computation.6 | async-start | bytes 16777216 | tf_op jit(solution)/shard_map/psum | solution.py:81
  1521.3 119.7 %collective-permute-start.8 = (f32[3072,400]{0,1:T(8,128)S(1)}, f32[3072,400]{0,1:T(8,128)}, u32[]{:S(2)}, u32[]{:S(2)}) collective-permute-start(f32[3072,400]{0,1:T(8,128)S(1)} %pad_maximum_fusion.10), channel_id=1, source_target_pairs={{0,3},{1,4},{2,5},{3,6},{4,7},{5,0},{6,1},{7,2},{8,11},{9,12},{10,... | collective-permute-start | bytes 14745608 | tf_op jit(solution)/shard_map/ppermute | solution.py:78
  1524.2 107.1 %collective-permute-start.6 = (s32[3072]{0:T(1024)S(1)}, s32[3072]{0:T(1024)S(1)}, u32[]{:S(2)}, u32[]{:S(2)}) collective-permute-start(s32[3072]{0:T(1024)S(1)} %pad_add_fusion.10), channel_id=1, source_target_pairs={{0,3},{1,4},{2,5},{3,6},{4,7},{5,0},{6,1},{7,2},{8,11},{9,12},{10,... | collective-permute-start | bytes 36872 | tf_op jit(solution)/shard_map/ppermute | solution.py:79
  1692.8 312.6 %all-reduce.32.cloned.1.call-start = ((), (), s32[]{:S(2)}) async-start(), calls=%async_computation.7 | async-start | bytes 458752 | tf_op jit(solution)/shard_map/psum | solution.py:82
  1864.5 184.3 %collective-permute-start.10 = (bf16[4096,400]{0,1:T(8,128)(2,1)}, bf16[4096,400]{0,1:T(8,128)(2,1)}, u32[]{:S(2)}, u32[]{:S(2)}) collective-permute-start(bf16[4096,400]{0,1:T(8,128)(2,1)} %copy.126), channel_id=1, source_target_pairs={{0,4},{1,5},{2,6},{3,7},{4,0},{5,1},{6,2},{7,3},{8,12},{9,13},{10,... | collective-permute-start | bytes 9830408 | tf_op jit(solution)/shard_map/ppermute | solution.py:64
  1886.7 522.6 %all-reduce.34.cloned.1.call-start = ((), (), s32[]{:S(2)}) async-start(), calls=%async_computation.8 | async-start | bytes 16777216 | tf_op jit(solution)/shard_map/psum | solution.py:81
  2084.9 117.9 %collective-permute-start.11 = (f32[3072,400]{0,1:T(8,128)S(1)}, f32[3072,400]{0,1:T(8,128)}, u32[]{:S(2)}, u32[]{:S(2)}) collective-permute-start(f32[3072,400]{0,1:T(8,128)S(1)} %pad_maximum_fusion.11), channel_id=1, source_target_pairs={{0,4},{1,5},{2,6},{3,7},{4,0},{5,1},{6,2},{7,3},{8,12},{9,13},{10,... | collective-permute-start | bytes 14745608 | tf_op jit(solution)/shard_map/ppermute | solution.py:78
  2087.1 107.1 %collective-permute-start.9 = (s32[3072]{0:T(1024)S(1)}, s32[3072]{0:T(1024)S(1)}, u32[]{:S(2)}, u32[]{:S(2)}) collective-permute-start(s32[3072]{0:T(1024)S(1)} %pad_add_fusion.11), channel_id=1, source_target_pairs={{0,4},{1,5},{2,6},{3,7},{4,0},{5,1},{6,2},{7,3},{8,12},{9,13},{10,... | collective-permute-start | bytes 36872 | tf_op jit(solution)/shard_map/ppermute | solution.py:79
  2254.8 293.8 %all-reduce.36.cloned.1.call-start = ((), (), s32[]{:S(2)}) async-start(), calls=%async_computation.9 | async-start | bytes 458752 | tf_op jit(solution)/shard_map/psum | solution.py:82
  2428.5 162.2 %collective-permute-start.13 = (bf16[4096,400]{0,1:T(8,128)(2,1)}, bf16[4096,400]{0,1:T(8,128)(2,1)}, u32[]{:S(2)}, u32[]{:S(2)}) collective-permute-start(bf16[4096,400]{0,1:T(8,128)(2,1)} %copy.134), channel_id=1, source_target_pairs={{0,3},{1,4},{2,5},{3,6},{4,7},{5,0},{6,1},{7,2},{8,11},{9,12},{10,... | collective-permute-start | bytes 9830408 | tf_op jit(solution)/shard_map/ppermute | solution.py:64
  2455.1 500.9 %all-reduce.38.cloned.1.call-start = ((), (), s32[]{:S(2)}) async-start(), calls=%async_computation.10 | async-start | bytes 16777216 | tf_op jit(solution)/shard_map/psum | solution.py:81
  2631.2 117.6 %collective-permute-start.14 = (f32[3072,400]{0,1:T(8,128)S(1)}, f32[3072,400]{0,1:T(8,128)}, u32[]{:S(2)}, u32[]{:S(2)}) collective-permute-start(f32[3072,400]{0,1:T(8,128)S(1)} %pad_maximum_fusion.12), channel_id=1, source_target_pairs={{0,5},{1,6},{2,7},{3,0},{4,1},{5,2},{6,3},{7,4},{8,13},{9,14},{10,... | collective-permute-start | bytes 14745608 | tf_op jit(solution)/shard_map/ppermute | solution.py:78
  2800.5 288.0 %all-reduce.40.cloned.1.call-start = ((), (), s32[]{:S(2)}) async-start(), calls=%async_computation.11 | async-start | bytes 458752 | tf_op jit(solution)/shard_map/psum | solution.py:82
  2975.2 156.7 %collective-permute-start.16 = (bf16[4096,400]{0,1:T(8,128)(2,1)}, bf16[4096,400]{0,1:T(8,128)(2,1)}, u32[]{:S(2)}, u32[]{:S(2)}) collective-permute-start(bf16[4096,400]{0,1:T(8,128)(2,1)} %copy.142), channel_id=1, source_target_pairs={{0,2},{1,3},{2,4},{3,5},{4,6},{5,7},{6,0},{7,1},{8,10},{9,11},{10,... | collective-permute-start | bytes 9830408 | tf_op jit(solution)/shard_map/ppermute | solution.py:64
  2995.8 495.7 %all-reduce.42.cloned.1.call-start = ((), (), s32[]{:S(2)}) async-start(), calls=%async_computation.12 | async-start | bytes 16777216 | tf_op jit(solution)/shard_map/psum | solution.py:81
  3167.7 116.4 %collective-permute-start.17 = (f32[3072,400]{0,1:T(8,128)S(1)}, f32[3072,400]{0,1:T(8,128)}, u32[]{:S(2)}, u32[]{:S(2)}) collective-permute-start(f32[3072,400]{0,1:T(8,128)S(1)} %pad_maximum_fusion.13), channel_id=1, source_target_pairs={{0,6},{1,7},{2,0},{3,1},{4,2},{5,3},{6,4},{7,5},{8,14},{9,15},{10,... | collective-permute-start | bytes 14745608 | tf_op jit(solution)/shard_map/ppermute | solution.py:78
  3169.1 106.5 %collective-permute-start.15 = (s32[3072]{0:T(1024)S(1)}, s32[3072]{0:T(1024)S(1)}, u32[]{:S(2)}, u32[]{:S(2)}) collective-permute-start(s32[3072]{0:T(1024)S(1)} %pad_add_fusion.13), channel_id=1, source_target_pairs={{0,6},{1,7},{2,0},{3,1},{4,2},{5,3},{6,4},{7,5},{8,14},{9,15},{10,... | collective-permute-start | bytes 36872 | tf_op jit(solution)/shard_map/ppermute | solution.py:79
  3335.8 291.4 %all-reduce.44.cloned.1.call-start = ((), (), s32[]{:S(2)}) async-start(), calls=%async_computation.13 | async-start | bytes 458752 | tf_op jit(solution)/shard_map/psum | solution.py:82
  3510.7 158.4 %collective-permute-start.19 = (bf16[4096,400]{0,1:T(8,128)(2,1)}, bf16[4096,400]{0,1:T(8,128)(2,1)}, u32[]{:S(2)}, u32[]{:S(2)}) collective-permute-start(bf16[4096,400]{0,1:T(8,128)(2,1)} %copy.150), channel_id=1, source_target_pairs={{0,1},{1,2},{2,3},{3,4},{4,5},{5,6},{6,7},{7,0},{8,9},{9,10},{10,1... | collective-permute-start | bytes 9830408 | tf_op jit(solution)/shard_map/ppermute | solution.py:64
  3535.7 349.1 %all-reduce.48.cloned.1.call-start = ((), (), s32[]{:S(2)}) async-start(), calls=%async_computation.15 | async-start | bytes 458752 | tf_op jit(solution)/shard_map/psum | solution.py:82
  3791.9 249.7 %all-reduce.46.cloned.1.call-start = ((), (), s32[]{:S(2)}) async-start(), calls=%async_computation.14 | async-start | bytes 16777216 | tf_op jit(solution)/shard_map/psum | solution.py:81
  (144 other events, 5048.7 us)
Sparse Core Ops, SparseCore 0:
  157.6 158.5 all-reduce.17
  319.6 92.4 all-reduce.19
  608.6 154.8 all-reduce.21
  804.7 91.6 all-reduce.23
  1146.0 153.1 all-reduce.25
  1344.7 94.2 all-reduce.27
  1692.9 152.3 all-reduce.29
  1886.8 118.5 all-reduce.31
  2255.0 154.3 all-reduce.33
  2455.2 93.4 all-reduce.35
  2800.6 155.2 all-reduce.37
  2995.9 92.5 all-reduce.39
  3335.9 155.5 all-reduce.41
  3535.8 91.3 all-reduce.43
  3792.0 92.7 all-reduce.47
  3887.2 154.3 all-reduce.45
where the time goes:
time: 4080 us; the launch traced here: 4070 us
  waiting for transfers between devices  2510 us (62%)
  other arithmetic  737 us (18%)
  local copies, waits for them, and re-layouts  687 us (17%)
  matrix products  69 us (2%)
    psum x8, waiting for transfers between devices, device_fn(): ent_grad = lax.psum(ent_grad, 'data')  1190 us
    psum x8, waiting for transfers between devices, device_fn(): lax.psum(jax.ops.segment_sum(g_rel, r_ids, num_segments=rel_rows), ('data...  680 us
    ppermute x7, waiting for transfers between devices, device_fn(): sent_ids = lax.ppermute(sent_ids, 'ent', return_perm)  636 us
    scatter-add x8, other arithmetic, device_fn(): jax.ops.segment_sum(jnp.concatenate([g_head, sent_rows], axis=0), jnp.con...  280 us
    gather x16, local copies, waits for them, and re-layouts, device_fn(): head_rows = jnp.take(table_now, h_ids, axis=0)  147 us
    gather x16, local copies, waits for them, and re-layouts, device_fn(): tail_bf = jnp.take(tail_table, t_ids, axis=0)  116 us
    gather x16, local copies, waits for them, and re-layouts, device_fn(): rel_rows_now = jnp.take(rel_now, r_ids, axis=0)  113 us
    scatter-add x8, other arithmetic, device_fn(): jax.ops.segment_sum(g_rel, r_ids, num_segments=rel_rows)  111 us
  transfers between devices with their start and end apart: 37, of which 23 were waited for; matrix products, arithmetic and copies ran while one was open for 15% of the time, Pallas kernels for 0%

commit v1 on v0

v1 whole, which is shorter than its diff:
```python
import functools

import jax
import jax.numpy as jnp
from jax import lax
from jax.experimental import pallas as pl
from jax.experimental.pallas import tpu as pltpu
from jax.sharding import PartitionSpec as P

LR_SCALE = 0.2
EPSILON = 1e-8
LANES = 128
HALF = 64
LEFT = 8
BLOCK = 256
CHUNK = 256
UNROLL = 128
REL_PAD = 128
F32 = jnp.float32
BF16 = jnp.bfloat16
VMEM_LIMIT = 60 * 2**20


def wire_rows(rows):
    return 3 * rows + rows // LEFT


def columns_to_tiles(rows):
    half = rows.shape[-1] // 2
    re, im = rows[..., :half], rows[..., half:]
    zero = jnp.zeros((*rows.shape[:-1], HALF - (half - LANES - HALF)), rows.dtype)
    cut = LANES + HALF
    return jnp.concatenate([re[..., :LANES], im[..., :LANES], re[..., LANES:cut], im[..., LANES:cut], re[..., cut:], zero, im[..., cut:], zero], axis=-1)


def tiles_to_wire(rows, size):
    n = rows.shape[0] // size
    blocks = rows.reshape(n, size, 4, LANES)
    main = blocks[:, :, :3].transpose(0, 2, 1, 3).reshape(n, 3 * size, LANES)
    last = blocks[:, :, 3].reshape(n, LEFT, size // LEFT, 2, HALF)[..., :LEFT]
    last = last.transpose(0, 2, 3, 1, 4).reshape(n, size // LEFT, LANES)
    return jnp.concatenate([main, last], axis=1)


def wire_to_columns(wire, size):
    n = wire.shape[0]
    a, b, c = (wire[:, t * size:(t + 1) * size].reshape(n * size, LANES) for t in range(3))
    last = wire[:, 3 * size:wire_rows(size)].reshape(n, size // LEFT, 2, LEFT, LEFT)
    last = last.transpose(0, 3, 1, 2, 4).reshape(n * size, 2, LEFT)
    return jnp.concatenate([a, c[:, :HALF], last[:, 0], b, c[:, HALF:], last[:, 1]], axis=-1)


def each_row(count, body):
    for u in range(count):
        body(u)


def fold_last(tile):
    n = tile.shape[0] // LEFT
    out = tile[:n]
    for k in range(1, LEFT):
        out = out + pltpu.roll(tile[k * n:(k + 1) * n], LEFT * k, 1)
    return out


def unfold_last(packed):
    keep = lax.broadcasted_iota(jnp.int32, packed.shape, 1) % HALF < LEFT
    return [jnp.where(keep, packed if k == 0 else pltpu.roll(packed, LANES - LEFT * k, 1), 0.0) for k in range(LEFT)]


def tiles_of(x):
    return [x[:, t * LANES:(t + 1) * LANES] for t in range(4)]


def times(x, y):
    out = [x[0] * y[0] - x[1] * y[1], x[0] * y[1] + x[1] * y[0]]
    for a, b in zip(x[2:], y[2:]):
        low = lax.broadcasted_iota(jnp.int32, a.shape, 1) < HALF
        a_swap, b_swap = pltpu.roll(a, HALF, 1), pltpu.roll(b, HALF, 1)
        out.append(jnp.where(low, a * b - a_swap * b_swap, a_swap * b + a * b_swap))
    return out


def times_conj(x, y):
    out = [x[0] * y[0] + x[1] * y[1], x[1] * y[0] - x[0] * y[1]]
    for a, b in zip(x[2:], y[2:]):
        low = lax.broadcasted_iota(jnp.int32, a.shape, 1) < HALF
        a_swap, b_swap = pltpu.roll(a, HALF, 1), pltpu.roll(b, HALF, 1)
        out.append(jnp.where(low, a * b + a_swap * b_swap, a * b_swap - a_swap * b))
    return out


def bucket_kernel(bits, edge_ref, count_ref, neg_ref, rel_id_ref, ent_ref, rel_ref, table_ref, tail_out, head_out, rel_out,
                  tail_rows, tail_buf, head_buf, rel_buf, neg_rows, neg_grad, gt_buf, gh_buf, tail_acc0, tail_acc1, head_acc0, head_acc1, rel_acc, loss_acc):
    head_bits, tail_bits = bits
    chunk = CHUNK
    part = chunk // LEFT
    tail_acc, head_acc = (tail_acc0, tail_acc1), (head_acc0, head_acc1)
    count = count_ref[0]
    negs = neg_ref.shape[0]

    def head_of(e):
        return pl.ds(e & (2**head_bits - 1), 1)

    def tail_of(e):
        return pl.ds((e >> head_bits) & (2**tail_bits - 1), 1)

    def widen(n, carry):
        base = pl.multiple_of(n * chunk, chunk)
        for t in range(3):
            tail_rows[pl.ds(base, chunk), t * LANES:(t + 1) * LANES] = table_ref[n, t * chunk:(t + 1) * chunk, :].astype(F32)
        for k, piece in enumerate(unfold_last(table_ref[n, 3 * chunk:, :].astype(F32))):
            tail_rows[pl.ds(base + k * part, part), 3 * LANES:] = piece
        for acc in tail_acc:
            acc[pl.ds(base, chunk), :] = jnp.zeros((chunk, 4 * LANES), F32)
        return carry

    lax.fori_loop(0, table_ref.shape[0], widen, 0)

    def clear(n, carry):
        base = pl.multiple_of(n * UNROLL, UNROLL)
        for acc in head_acc:
            acc[pl.ds(base, UNROLL), :] = jnp.zeros((UNROLL, 4 * LANES), F32)
        return carry

    lax.fori_loop(0, ent_ref.shape[0] // UNROLL, clear, 0)
    neg_grad[...] = jnp.zeros_like(neg_grad)
    rel_acc[...] = jnp.zeros_like(rel_acc)
    loss_acc[...] = jnp.zeros_like(loss_acc)

    def take_negs(n, carry):
        base = pl.multiple_of(n * UNROLL, UNROLL)

        def take(u):
            gt_buf[pl.ds(u, 1), :] = tail_rows[pl.ds(neg_ref[base + u], 1), :]

        each_row(UNROLL, take)
        neg_rows[pl.ds(base, UNROLL), :] = gt_buf[:UNROLL, :].astype(BF16)
        return carry

    lax.fori_loop(0, negs // UNROLL, take_negs, 0)

    def block(n, carry):
        base = n * BLOCK

        def take(u):
            e = edge_ref[base + u]
            head_buf[pl.ds(u, 1), :] = ent_ref[head_of(e), :]
            tail_buf[pl.ds(u, 1), :] = tail_rows[tail_of(e), :]
            rel_buf[pl.ds(u, 1), :] = rel_ref[pl.ds(e >> (head_bits + tail_bits), 1), :]

        each_row(BLOCK, take)
        hot = lax.broadcasted_iota(jnp.int32, (REL_PAD, BLOCK), 0) == rel_id_ref[pl.ds(n, 1), :]
        hot = jnp.where(hot, 1.0, 0.0).astype(BF16)
        weight = jnp.where(lax.broadcasted_iota(jnp.int32, (BLOCK, 1), 0) + base < count, 1.0, 0.0)
        head, rel, tail = tiles_of(head_buf[...]), tiles_of(rel_buf[...]), tiles_of(tail_buf[...])
        query_bf = [t.astype(BF16) for t in times(head, rel)]
        query = [t.astype(F32) for t in query_bf]
        pos = jnp.sum(query[0] * tail[0] + query[1] * tail[1] + query[2] * tail[2] + query[3] * tail[3], axis=1, keepdims=True)
        query_bf = jnp.concatenate(query_bf, axis=1)
        score = lax.dot_general(query_bf, neg_rows[...], (((1,), (1,)), ((), ())), preferred_element_type=F32)
        top = jnp.maximum(jnp.max(score, axis=1, keepdims=True), pos)
        pos_exp = jnp.exp(pos - top)
        neg_exp = jnp.exp(score - top)
        total = pos_exp + jnp.sum(neg_exp, axis=1, keepdims=True)
        loss_acc[...] += jnp.sum(weight * (top + jnp.log(total) - pos), axis=0, keepdims=True)
        d_pos = weight * (pos_exp / total - 1.0)
        d_neg = ((weight / total) * neg_exp).astype(BF16)
        grad_q = lax.dot_general(d_neg, neg_rows[...], (((1,), (0,)), ((), ())), preferred_element_type=F32)
        neg_grad[...] += lax.dot_general(d_neg, query_bf, (((0,), (0,)), ((), ())), preferred_element_type=F32)
        grad_q = [d_pos * a + b for a, b in zip(tail, tiles_of(grad_q))]
        for t in range(4):
            gt_buf[:, t * LANES:(t + 1) * LANES] = d_pos * query[t]
        for t, grad in enumerate(times_conj(grad_q, rel)):
            gh_buf[:, t * LANES:(t + 1) * LANES] = grad
        rest = jnp.concatenate(times_conj(grad_q, head), axis=1)
        rel_sum = rel_acc[...]
        for _ in range(3):
            piece = rest.astype(BF16)
            rest = rest - piece.astype(F32)
            rel_sum = rel_sum + lax.dot_general(hot, piece, (((1,), (0,)), ((), ())), preferred_element_type=F32)
        rel_acc[...] = rel_sum

        def put(pair):
            for lane in range(2):
                u = 2 * pair + lane
                e = edge_ref[base + u]
                head_acc[lane][head_of(e), :] += gh_buf[pl.ds(u, 1), :]
                tail_acc[lane][tail_of(e), :] += gt_buf[pl.ds(u, 1), :]

        each_row(BLOCK // 2, put)
        return carry

    lax.fori_loop(0, pl.cdiv(count, BLOCK), block, 0)

    def put_negs(n, carry):
        base = pl.multiple_of(n * UNROLL, UNROLL)

        def put(pair):
            for lane in range(2):
                u = base + 2 * pair + lane
                tail_acc[lane][pl.ds(neg_ref[u], 1), :] += neg_grad[pl.ds(u, 1), :]

        each_row(UNROLL // 2, put)
        return carry

    lax.fori_loop(0, negs // UNROLL, put_negs, 0)

    def emit(out_ref, acc):
        def one(n, carry):
            base = pl.multiple_of(n * chunk, chunk)
            for t in range(4):
                cols = slice(t * LANES, (t + 1) * LANES)
                rows = acc[0][pl.ds(base, chunk), cols] + acc[1][pl.ds(base, chunk), cols]
                if t < 3:
                    out_ref[n, t * chunk:(t + 1) * chunk, :] = rows
                else:
                    out_ref[n, 3 * chunk:, :] = fold_last(rows)
            return carry

        lax.fori_loop(0, out_ref.shape[0], one, 0)

    emit(tail_out, tail_acc)
    emit(head_out, head_acc)
    group = lax.axis_index('ent') // 2 * 2 + lax.axis_index('data') // 2
    row = lax.broadcasted_iota(jnp.int32, (REL_PAD, LANES), 0)
    lane = lax.broadcasted_iota(jnp.int32, (REL_PAD, LANES), 1)
    loss = jnp.where(lane == group, loss_acc[...], 0.0)
    for t in range(3):
        rows = rel_acc[:, t * LANES:(t + 1) * LANES]
        rel_out[t * REL_PAD:(t + 1) * REL_PAD, :] = jnp.where(row == REL_PAD - 1, loss, rows) if t == 0 else rows
    rel_out[3 * REL_PAD:, :] = fold_last(rel_acc[:, 3 * LANES:])


def bucket_call(bits, edges, count, neg, rel_ids, ent, rel, table):
    smem, vmem = pl.BlockSpec(memory_space=pltpu.SMEM), pl.BlockSpec(memory_space=pltpu.VMEM)
    rows, negs, chunks = ent.shape[0], neg.shape[0], table.shape[0]
    width = 4 * LANES
    wire = wire_rows(CHUNK)
    block = pltpu.VMEM((BLOCK, width), F32)
    return pl.pallas_call(
        functools.partial(bucket_kernel, bits),
        out_shape=(
            jax.ShapeDtypeStruct((chunks, wire, LANES), F32),
            jax.ShapeDtypeStruct((rows // CHUNK, wire, LANES), F32),
            jax.ShapeDtypeStruct((wire_rows(REL_PAD), LANES), F32),
        ),
        in_specs=[smem, smem, smem, vmem, vmem, vmem, vmem],
        out_specs=(vmem, vmem, vmem),
        scratch_shapes=[
            pltpu.VMEM((chunks * CHUNK, width), F32), block, block, block,
            pltpu.VMEM((negs, width), BF16), pltpu.VMEM((negs, width), F32), block, block,
            pltpu.VMEM((chunks * CHUNK, width), F32), pltpu.VMEM((chunks * CHUNK, width), F32),
            pltpu.VMEM((rows, width), F32), pltpu.VMEM((rows, width), F32),
            pltpu.VMEM((REL_PAD, width), F32), pltpu.VMEM((1, 1), F32),
        ],
        compiler_params=pltpu.CompilerParams(vmem_limit_bytes=VMEM_LIMIT),
        name='bucket',
    )(edges, count, neg, rel_ids, ent, rel, table)


def adagrad(rows, state, grad, mean_of, learn_rate):
    square = grad[0] * grad[0] + grad[1] * grad[1] + grad[2] * grad[2] + grad[3] * grad[3]
    state = state + jnp.sum(square, axis=1, keepdims=True) / mean_of
    root = jnp.sqrt(state + EPSILON)
    return [r - learn_rate * (g / root) for r, g in zip(rows, grad)], state


def exchange_kernel(cfg, *refs):
    step, groups, chunks, emb_width, last = cfg
    (tail_ref, head_ref, rel_grad_ref, ent_ref, state_ref, rel_ref, rel_state_ref) = refs[:7]
    if last:
        ent_wire, rel_out, loss_out = refs[7:10]
        rest = refs[10:]
    else:
        ent_out, state_out, rel_out, rel_state_out, loss_out, table = refs[7:13]
        rest = refs[13:]
    (own, from_core, from_y, from_group, rel_sum, rel_from, send_buf,
     own_sem, core_send, core_recv, y_send, y_recv, group_send, group_recv, rel_send, rel_recv, out_send, out_recv) = rest
    learn_rate = LR_SCALE * emb_width ** -0.25
    chunk = CHUNK
    part = chunk // LEFT
    y, ent = lax.axis_index('data'), lax.axis_index('ent')
    x, core = ent // 2, ent % 2
    top, bot = y // 2, y % 2
    mine = 2 * x + top
    x_size = groups // 2

    def place(group, low, c):
        return {'data': 2 * (group % 2) + low, 'ent': 2 * (group // 2) + c}

    def at(dy, dx, c):
        return {'data': dy, 'ent': 2 * dx + c}

    def turned(shift):
        return (bot + shift) % 2

    other_core = at(y, x, 1 - core)
    other_y = at(2 * top + 1 - bot, x, core)
    rel_peers = (other_core, other_y, at(3 - y, x, core), at(y, x + 1 - 2 * (x % 2), core), at(y, x_size - 1 - x, core))
    grad_to = place((mine + step) % groups, turned(step), core)
    grad_from = place((mine + groups - step) % groups, turned(step), core)
    nxt = step + 1
    table_to = place((mine + groups - nxt) % groups, turned(nxt), core)
    table_from = place((mine + nxt) % groups, turned(nxt), core)
    peers = list(rel_peers)
    if step:
        peers += [grad_to, grad_from]
    if last:
        for turn in range(4):
            peers.append(at((y + turn) % 4, x, top))
        senders = [at((2 * core + d), x, c) for d in range(2) for c in range(2)]
        peers += senders
    else:
        peers += [table_to, table_from]
    barrier = pltpu.get_barrier_semaphore()
    for peer in peers:
        pl.semaphore_signal(barrier, inc=1, device_id=peer, device_id_type=pl.DeviceIdType.MESH)
    pl.semaphore_wait(barrier, len(peers))

    def remote(src, dst, send, recv, peer):
        return pltpu.make_async_remote_copy(src_ref=src, dst_ref=dst, send_sem=send, recv_sem=recv, device_id=peer, device_id_type=pl.DeviceIdType.MESH)

    keep = turned(step)
    pending = []

    def start(copy):
        copy.start()
        pending.append(copy)
        return copy

    shards = [(1 - keep, k) for k in range(chunks)] + [(keep, k) for k in range(chunks)]
    loads, cores = [], []
    rel_copies = [start(remote(rel_grad_ref, rel_from.at[0], rel_send.at[0], rel_recv.at[0], rel_peers[0]))]
    for n, (low, k) in enumerate(shards):
        cores.append(start(remote(tail_ref.at[(low * 2 + 1 - core) * chunks + k], from_core.at[n], core_send.at[n], core_recv.at[n], other_core)))
        load = pltpu.make_async_copy(tail_ref.at[(low * 2 + core) * chunks + k], own.at[n], own_sem.at[n])
        load.start()
        loads.append(load)

    def rel_step(n):
        rel_copies[n].wait_recv()
        rel_sum[n] = (rel_grad_ref[...] if n == 0 else rel_sum[n - 1]) + rel_from[n]
        if n + 1 < len(rel_peers):
            rel_copies.append(start(remote(rel_sum.at[n], rel_from.at[n + 1], rel_send.at[n + 1], rel_recv.at[n + 1], rel_peers[n + 1])))

    rel_step(0)
    ys = []
    for k in range(chunks):
        loads[k].wait()
        cores[k].wait_recv()
        own[k] = own[k] + from_core[k]
        ys.append(start(remote(own.at[k], from_y.at[k], y_send.at[k], y_recv.at[k], other_y)))
    rel_step(1)
    for k in range(chunks, 2 * chunks):
        loads[k].wait()
        cores[k].wait_recv()
        own[k] = own[k] + from_core[k]
    rel_step(2)
    gs, outs, forwards, crosses = [], [], [], []

    def stage_group(k):
        ys[k].wait_recv()
        own[chunks + k] = own[chunks + k] + from_y[k]
        if step:
            gs.append(start(remote(own.at[chunks + k], from_group.at[k], group_send.at[k], group_recv.at[k], grad_to)))

    def stage_update(k):
        if step:
            gs[k].wait_recv()
        total = from_group if step else own
        base = k if step else chunks + k
        grad = [total[base, t * chunk:(t + 1) * chunk, :] + head_ref[k, t * chunk:(t + 1) * chunk, :] for t in range(3)]
        grad.append(jnp.concatenate(unfold_last(total[base, 3 * chunk:, :] + head_ref[k, 3 * chunk:, :]), axis=0))
        span = slice(k * chunk, (k + 1) * chunk)
        rows, state = adagrad(tiles_of(ent_ref[span, :]), state_ref[span, :], grad, emb_width, learn_rate)
        wire = rows[:3] + [fold_last(rows[3])]
        if last:
            lane = lax.broadcasted_iota(jnp.int32, (chunk, LANES), 1)
            wire.append(fold_last(jnp.where(lane < 1, state, 0.0)))
        else:
            for t in range(4):
                ent_out[span, t * LANES:(t + 1) * LANES] = rows[t]
            state_out[span, :] = state
        offset = 0
        for piece in wire:
            send_buf[k, offset:offset + piece.shape[0], :] = piece.astype(send_buf.dtype)
            offset += piece.shape[0]
        slot = (bot * 2 + core) * chunks + k
        if last:
            for turn in range(1, 4):
                start(remote(send_buf.at[k], ent_wire.at[slot], out_send.at[turn * chunks + k], out_recv.at[slot], at((y + turn) % 4, x, top)))

            @pl.when(core == top)
            def _():
                pltpu.make_async_copy(send_buf.at[k], ent_wire.at[slot], out_recv.at[slot]).start()

            @pl.when(core != top)
            def _():
                remote(send_buf.at[k], ent_wire.at[slot], out_send.at[k], out_recv.at[slot], other_core).start()
        else:
            outs.append(start(remote(send_buf.at[k], table.at[slot], out_send.at[k], out_recv.at[k], table_to)))

    def forward(n, low, k, peer):
        slot = (low * 2 + core) * chunks + k
        return start(remote(table.at[slot], table.at[slot], out_send.at[n * chunks + k], out_recv.at[n * chunks + k], peer))

    def stage_forward(k):
        if last:
            return
        outs[k].wait_recv()
        forwards.append(forward(1, turned(nxt), k, other_y))
        crosses.append(forward(2, turned(nxt), k, other_core))

    def stage_cross(k):
        if last:
            return
        forwards[k].wait_recv()
        crosses.append(forward(3, 1 - turned(nxt), k, other_core))

    stages = (stage_group, stage_update, stage_forward, stage_cross)
    for tick in range(chunks + len(stages) - 1):
        for lag, stage in enumerate(stages):
            if 0 <= tick - lag < chunks:
                stage(tick - lag)
        if tick in (0, 1):
            rel_step(3 + tick)

    summed = rel_sum[len(rel_peers) - 1]
    rel_grad = [summed[t * REL_PAD:(t + 1) * REL_PAD] for t in range(3)] + [jnp.concatenate(unfold_last(summed[3 * REL_PAD:]), axis=0)]
    loss_out[...] = rel_grad[0][REL_PAD - 1:, :]
    row = lax.broadcasted_iota(jnp.int32, (REL_PAD, LANES), 0)
    rel_grad[0] = jnp.where(row < REL_PAD - 1, rel_grad[0], 0.0)
    rel_rows, rel_state = adagrad(tiles_of(rel_ref[...]), rel_state_ref[...], rel_grad, emb_width, learn_rate)
    for t in range(4):
        rel_out[:, t * LANES:(t + 1) * LANES] = rel_rows[t]
    if not last:
        rel_state_out[...] = rel_state

    if last:
        for slot in range(4 * chunks):
            remote(ent_wire.at[slot], ent_wire.at[slot], out_send.at[0], out_recv.at[slot], other_core).wait_recv()

        @pl.when(core != top)
        def _():
            for k in range(chunks):
                remote(send_buf.at[k], send_buf.at[k], out_send.at[k], out_recv.at[k], other_core).wait_send()
    else:
        for copy in crosses:
            copy.wait_recv()
    for copy in pending:
        copy.wait_send()


def exchange_call(step, groups, emb_width, tail, head, rel_grad, ent, state, rel, rel_state):
    vmem, hbm = pl.BlockSpec(memory_space=pltpu.VMEM), pl.BlockSpec(memory_space=pl.ANY)
    chunks = head.shape[0]
    wire = wire_rows(CHUNK)
    last = step == groups - 1
    like = lambda x: jax.ShapeDtypeStruct(x.shape, x.dtype)
    loss = jax.ShapeDtypeStruct((1, LANES), F32)
    out_wire = wire + (CHUNK // LEFT if last else 0)
    out_type = F32 if last else BF16
    gathered = jax.ShapeDtypeStruct((4 * chunks, out_wire, LANES), out_type)
    out_shape = (gathered, like(rel), loss) if last else (like(ent), like(state), like(rel), like(rel_state), loss, gathered)
    sems = lambda n: pltpu.SemaphoreType.DMA((n,))
    return pl.pallas_call(
        functools.partial(exchange_kernel, (step, groups, chunks, emb_width, last)),
        out_shape=out_shape,
        in_specs=[hbm] + [vmem] * 6,
        out_specs=tuple(vmem for _ in out_shape),
        scratch_shapes=[
            pltpu.VMEM((2 * chunks, wire, LANES), F32), pltpu.VMEM((2 * chunks, wire, LANES), F32),
            pltpu.VMEM((chunks, wire, LANES), F32), pltpu.VMEM((chunks, wire, LANES), F32),
            pltpu.VMEM((5, *rel_grad.shape), F32), pltpu.VMEM((5, *rel_grad.shape), F32),
            pltpu.VMEM((chunks, out_wire, LANES), out_type),
            sems(2 * chunks), sems(2 * chunks), sems(2 * chunks), sems(chunks), sems(chunks), sems(chunks), sems(chunks),
            sems(5), sems(5), sems(4 * chunks), sems(4 * chunks),
        ],
        compiler_params=pltpu.CompilerParams(vmem_limit_bytes=VMEM_LIMIT, collective_id=step, has_side_effects=True),
        name='exchange',
    )(tail, head, rel_grad, ent, state, rel, rel_state)


def solution(mesh):
    groups = mesh.shape['ent']
    data_reps = mesh.shape['data']
    row_spec = P(('sweep', 'ent'), None)
    edge_spec = P(('sweep', 'ent'), None, 'data')

    def device_fn(ent_table, ent_state, rel_table, head_idx, tail_idx, rel_idx, edge_mask, neg_idx):
        part_rows, emb_width = ent_table.shape
        rel_rows = rel_table.shape[0]
        bucket_edges = head_idx.shape[2] * data_reps
        shard = part_rows // 4
        tail_bits = (part_rows - 1).bit_length()
        head_bits = (shard - 1).bit_length()
        spare = 2**(REL_PAD - 1).bit_length() - 1
        y, ent = lax.axis_index('data'), lax.axis_index('ent')
        core, top, bot = ent % 2, y // 2, y % 2
        is_home = core == top

        packed = head_idx[0] | (tail_idx[0] << tail_bits) | (rel_idx[0] << (2 * tail_bits))
        packed = jnp.where(edge_mask[0] > 0, packed, spare << (2 * tail_bits))
        packed = lax.all_gather(packed, 'data', axis=1, tiled=True)
        own_tiles = columns_to_tiles(ent_table)
        own_table = tiles_to_wire(own_tiles.astype(BF16), CHUNK)
        to_core = lambda c: (lax.dynamic_slice_in_dim(own_tiles, (2 * bot + c) * shard, shard), lax.dynamic_slice_in_dim(ent_state, (2 * bot + c) * shard, shard))
        away = [(d * groups + 2 * (n // 2) + d // 2, d * groups + 2 * (n // 2) + 1 - d // 2) for d in range(data_reps) for n in range(0, groups, 2)]
        other_ent, other_state = to_core(1 - core)
        mine_ent, mine_state = to_core(core)
        pick = lambda here, sent: jnp.where(is_home, here, lax.ppermute(sent, ('data', 'ent'), away))
        packed = pick(packed, packed)
        neg = pick(neg_idx[0], neg_idx[0])
        table = pick(own_table, own_table)
        ent_now = pick(mine_ent, other_ent)
        state_now = pick(mine_state, other_state)[:, None]

        is_mine = ((packed >> head_bits) & 3 == 2 * bot + core) & (packed >> (2 * tail_bits) != spare)
        local = (packed & (shard - 1)) | (packed >> tail_bits << head_bits)
        keys = lax.sort(jnp.where(is_mine, local, spare << (head_bits + tail_bits)), dimension=1)
        counts = jnp.sum(is_mine, axis=1, dtype=jnp.int32)
        rel_ids = (keys >> (head_bits + tail_bits)).reshape(groups, -1, BLOCK)

        rel_now = jnp.pad(columns_to_tiles(rel_table), ((0, REL_PAD - rel_rows), (0, 0)))
        rel_state = jnp.zeros((REL_PAD, 1), F32)
        losses = []
        for step in range(groups):
            tail, head, rel_grad = bucket_call((head_bits, tail_bits), keys[step], counts[step:step + 1], neg[step], rel_ids[step], ent_now, rel_now, table)
            out = exchange_call(step, groups, emb_width, tail, head, rel_grad, ent_now, state_now, rel_now, rel_state)
            if step + 1 < groups:
                ent_now, state_now, rel_now, rel_state, loss, table = out
            else:
                wire, rel_now, loss = out
            losses.append(loss)
        ent_out = wire_to_columns(wire, CHUNK)
        state_out = wire[:, wire_rows(CHUNK):, :HALF:LEFT].transpose(0, 2, 1).reshape(part_rows)
        half = emb_width // 2
        cut = LANES + HALF
        rel_out = jnp.concatenate([rel_now[:, :LANES], rel_now[:, 2 * LANES:cut + LANES], rel_now[:, 3 * LANES:3 * LANES + half - cut],
                                   rel_now[:, LANES:2 * LANES], rel_now[:, cut + LANES:3 * LANES], rel_now[:, 3 * LANES + HALF:3 * LANES + HALF + half - cut]], axis=1)[:rel_rows]
        loss_rows = jnp.concatenate(losses, axis=0) / bucket_edges
        bucket_loss = lax.dynamic_slice_in_dim(loss_rows, ent, 1, axis=1).reshape(1, groups)
        return ent_out, state_out, rel_out, bucket_loss

    return jax.shard_map(device_fn, mesh=mesh, in_specs=(row_spec, P(('sweep', 'ent')), P('sweep', None), edge_spec, edge_spec, edge_spec, edge_spec, P(('sweep', 'ent'), None, None)), out_specs=(row_spec, P(('sweep', 'ent')), P('sweep', None), row_spec), check_vma=False)
```

time: 4080 us -> 1350 us (0.33)
  waiting for transfers between devices: 2510 us -> 0.01 us
  Pallas kernels: 0 us -> 1140 us
  other arithmetic: 737 us -> 22.2 us
  local copies, waits for them, and re-layouts: 687 us -> 152 us
  matrix products: 69 us -> 0 us
    psum x16 -> x0, waiting for transfers between devices: 1870 us -> none  [the longest x8 1190 us: device_fn(): ent_grad = lax.psum(ent_grad, 'data')]
    pallas_call x0 -> x16, Pallas kernels: none -> 1140 us  [the longest x8 857 us: exchange_call(): pl.pallas_call(functools.partial(exchange_kernel, (step, groups, chunks,...]
    ppermute x21 -> x5, waiting for transfers between devices: 636 us -> 0.01 us  [device_fn(): lax.ppermute(sent, ('data', 'ent'), away)]
    gather x56 -> x0, local copies, waits for them, and re-layouts: 440 us -> none  [the longest x16 147 us: device_fn(): head_rows = jnp.take(table_now, h_ids, axis=0)]
    scatter-add x16 -> x0, other arithmetic: 392 us -> none  [the longest x8 280 us: device_fn(): jax.ops.segment_sum(jnp.concatenate([g_head, sent_rows], axis=0), jnp.con...]
    concatenate x16 -> x5, local copies, waits for them, and re-layouts: 117 us -> 15.8 us  [the longest x2 15.6 us: columns_to_tiles(): jnp.concatenate([re[..., :LANES], im[..., :LANES], re[..., LANES:cut], im...]
    concatenate x38 -> x1, other arithmetic: 77.1 us -> 1.93 us  [tiles_to_wire(): return jnp.concatenate([main, last], axis=1)]
    dot_general x24 -> x0, matrix products: 69 us -> none  [the longest x8 32.5 us: bucket_terms(): jnp.einsum('...bn,...nd->...bd', d_neg, neg_bf, preferred_element_type=jn...]
  transfers between devices with their start and end apart: 37 -> 5, of which waited for: 23 -> 0; matrix products, arithmetic and copies ran while one was open for 15% -> 8% of each run, Pallas kernels for 0% -> 0%
where the time goes in v1:
time: 1350 us
  Pallas kernels  1140 us (84%)
  local copies, waits for them, and re-layouts  152 us (11%)
  other arithmetic  22.2 us (2%)
  between operations  14.9 us (1%)
  blocking collectives  14.7 us (1%)
    pallas_call x8, Pallas kernels, exchange_call(): pl.pallas_call(functools.partial(exchange_kernel, (step, groups, chunks,...  857 us
    pallas_call x8, Pallas kernels, bucket_call(): pl.pallas_call(functools.partial(bucket_kernel, bits), out_shape=(jax.Sha...  282 us
    unnamed x46, local copies, waits for them, and re-layouts  27.7 us
  transfers between devices with their start and end apart: 5, of which 0 were waited for; matrix products, arithmetic and copies ran while one was open for 8% of the time, Pallas kernels for 0%

profile of v1, /device:TPU:97, one launch (start us, length us, event | category | flops | bytes accessed | tf_op | source)
XLA Modules:
  0.0 1350.3 jit_solution(14822271711755973168)
XLA Ops:
  11.5 14.7 %all-gather = s32[1,8,8192]{2,1,0:T(8,128)S(1)} all-gather(s32[1,8,2048]{2,1,0:T(8,128)S(1)} %or_select_fusion.1), channel_id=2, replica_groups=mesh['sweep'=1,'data'=4,'ent'=8] {'data'}, dimensions={2}, use_global_device_ids=true | all-gather | bytes 327680 | tf_op jit(solution)/shard_map/all_gather | solution.py:505
  31.9 3.9 fusion.6
  40.6 3.2 copy.84
  50.6 13.7 %concatenate.18 = f32[4096,512]{1,0:T(8,128)} concatenate(f32[4096,128]{1,0:T(8,128)} %copy.81, f32[4096,128]{1,0:T(8,128)} %copy.82, f32[4096,64]{1,0:T(8,128)} %copy.83, f32[4096,64]{1,0:T(8,128)} %copy.84, f32[4096,8]{1,0:T(8,128)} %copy.60, f32[4096,56]{1,0:T(8,128)S(1)} %broadcast_in_dim.22, f32[4096,8]{1,0:T(8,128)} %copy.61, f32[4096,56]{1,0:T(8,128)S(1)} %broadcast_in_dim.22), dimensions={1} | concatenate | bytes 16777216 | tf_op jit(solution)/shard_map/concatenate | solution.py:33
  64.4 3.1 constant_dynamic-slice_fusion
  69.2 5.9 convert_element_type.13
  75.1 6.9 convert_element_type.14
  82.0 4.8 slice.301
  90.5 5.0 reshape_squeeze.3
  95.5 5.0 slice_bitcast_fusion.1
  100.5 5.8 copy.70
  131.2 18.2 %sort.9.cloned.1.call-done = s32[8,8192]{1,0:T(8,128)} async-done(((s32[8,8192]{1,0:T(8,128)}), s32[8,8192]{1,0:T(8,128)}) %sort.9.cloned.1.call-update) | async-done | bytes 262160 | tf_op jit(solution)/shard_map/sort | solution.py:521
  159.0 4.0 dynamic-slice_select_fusion.ent_ref.refs_3_
  163.0 4.4 broadcast_select_fusion.table_ref
  167.4 20.9 %bucket.8 = (f32[16,800,128]{2,1,0:T(8,128)}, f32[4,800,128]{2,1,0:T(8,128)}, f32[400,128]{1,0:T(8,128)}) custom-call(s32[8192]{0:T(1024)} %bitcast.72, s32[1]{0:T(128)} %get-tuple-element.203.count_ref, s32[1024]{0:T(1024)} %bitcast.81, s32[32,256]{1,0:T(8,128)} %squeeze.110.rel_id_ref, f32[1024,512]{1,0:T(8,128)} %dynamic-slice_select_fusion.ent_ref.refs_3_, ...), custom_call_target="tpu_custom_call" | custom-call | tf_op jit(solution)/shard_map/bucket/pallas_call | solution.py:241
  189.0 95.2 %exchange.8 = (f32[1024,512]{1,0:T(8,128)}, f32[1024,1]{1,0:T(8,128)}, f32[128,512]{1,0:T(8,128)}, f32[128,1]{1,0:T(8,128)}, f32[1,128]{1,0:T(1,128)}, /*index=5*/bf16[16,800,128]{2,1,0:T(8,128)(2,1)}) custom-call(f32[16,800,128]{2,1,0:T(8,128)} %get-tuple-element.73.refs_0_, f32[4,800,128]{2,1,0:T(8,128)} %get-tuple-element.74.refs_1_, ...), custom_call_target="tpu_custom_call" | custom-call | tf_op jit(solution)/shard_map/exchange/pallas_call | solution.py:467
  284.2 31.5 %bucket.9 = (f32[16,800,128]{2,1,0:T(8,128)}, f32[4,800,128]{2,1,0:T(8,128)}, f32[400,128]{1,0:T(8,128)}) custom-call(s32[8192]{0:T(1024)} %bitcast.71, s32[1]{0:T(128)} %get-tuple-element.204.count_ref, s32[1024]{0:T(1024)} %bitcast.80, s32[32,256]{1,0:T(8,128)} %squeeze.107.rel_id_ref, f32[1024,512]{1,0:T(8,128)} %get-tuple-element.76.ent_ref.refs_3_, ...), custom_call_target="tpu_custom_call" | custom-call | tf_op jit(solution)/shard_map/bucket/pallas_call | solution.py:241
  315.7 92.9 %exchange.9 = (f32[1024,512]{1,0:T(8,128)}, f32[1024,1]{1,0:T(8,128)}, f32[128,512]{1,0:T(8,128)}, f32[128,1]{1,0:T(8,128)}, f32[1,128]{1,0:T(1,128)}, /*index=5*/bf16[16,800,128]{2,1,0:T(8,128)(2,1)}) custom-call(f32[16,800,128]{2,1,0:T(8,128)} %get-tuple-element.79.refs_0_, f32[4,800,128]{2,1,0:T(8,128)} %get-tuple-element.80.refs_1_, ...), custom_call_target="tpu_custom_call" | custom-call | tf_op jit(solution)/shard_map/exchange/pallas_call | solution.py:467
  408.6 48.9 %bucket.10 = (f32[16,800,128]{2,1,0:T(8,128)}, f32[4,800,128]{2,1,0:T(8,128)}, f32[400,128]{1,0:T(8,128)}) custom-call(s32[8192]{0:T(1024)} %bitcast.70, s32[1]{0:T(128)} %get-tuple-element.205.count_ref, s32[1024]{0:T(1024)} %bitcast.79, s32[32,256]{1,0:T(8,128)} %squeeze.104.rel_id_ref, f32[1024,512]{1,0:T(8,128)} %get-tuple-element.84.ent_ref.refs_3_, ...), custom_call_target="tpu_custom_call" | custom-call | tf_op jit(solution)/shard_map/bucket/pallas_call | solution.py:241
  457.5 92.1 %exchange.10 = (f32[1024,512]{1,0:T(8,128)}, f32[1024,1]{1,0:T(8,128)}, f32[128,512]{1,0:T(8,128)}, f32[128,1]{1,0:T(8,128)}, f32[1,128]{1,0:T(1,128)}, /*index=5*/bf16[16,800,128]{2,1,0:T(8,128)(2,1)}) custom-call(f32[16,800,128]{2,1,0:T(8,128)} %get-tuple-element.87.refs_0_, f32[4,800,128]{2,1,0:T(8,128)} %get-tuple-element.88.refs_1_, ...), custom_call_target="tpu_custom_call" | custom-call | tf_op jit(solution)/shard_map/exchange/pallas_call | solution.py:467
  549.7 31.3 %bucket.11 = (f32[16,800,128]{2,1,0:T(8,128)}, f32[4,800,128]{2,1,0:T(8,128)}, f32[400,128]{1,0:T(8,128)}) custom-call(s32[8192]{0:T(1024)} %bitcast.69, s32[1]{0:T(128)} %get-tuple-element.206.count_ref, s32[1024]{0:T(1024)} %bitcast.78, s32[32,256]{1,0:T(8,128)} %squeeze.101.rel_id_ref, f32[1024,512]{1,0:T(8,128)} %get-tuple-element.92.ent_ref.refs_3_, ...), custom_call_target="tpu_custom_call" | custom-call | tf_op jit(solution)/shard_map/bucket/pallas_call | solution.py:241
  580.9 104.8 %exchange.11 = (f32[1024,512]{1,0:T(8,128)}, f32[1024,1]{1,0:T(8,128)}, f32[128,512]{1,0:T(8,128)}, f32[128,1]{1,0:T(8,128)}, f32[1,128]{1,0:T(1,128)}, /*index=5*/bf16[16,800,128]{2,1,0:T(8,128)(2,1)}) custom-call(f32[16,800,128]{2,1,0:T(8,128)} %get-tuple-element.95.refs_0_, f32[4,800,128]{2,1,0:T(8,128)} %get-tuple-element.96.refs_1_, ...), custom_call_target="tpu_custom_call" | custom-call | tf_op jit(solution)/shard_map/exchange/pallas_call | solution.py:467
  685.8 34.8 %bucket.12 = (f32[16,800,128]{2,1,0:T(8,128)}, f32[4,800,128]{2,1,0:T(8,128)}, f32[400,128]{1,0:T(8,128)}) custom-call(s32[8192]{0:T(1024)} %bitcast.68, s32[1]{0:T(128)} %get-tuple-element.207.count_ref, s32[1024]{0:T(1024)} %bitcast.77, s32[32,256]{1,0:T(8,128)} %squeeze.98.rel_id_ref, f32[1024,512]{1,0:T(8,128)} %get-tuple-element.100.ent_ref.refs_3_, ...), custom_call_target="tpu_custom_call" | custom-call | tf_op jit(solution)/shard_map/bucket/pallas_call | solution.py:241
  720.5 125.2 %exchange.12 = (f32[1024,512]{1,0:T(8,128)}, f32[1024,1]{1,0:T(8,128)}, f32[128,512]{1,0:T(8,128)}, f32[128,1]{1,0:T(8,128)}, f32[1,128]{1,0:T(1,128)}, /*index=5*/bf16[16,800,128]{2,1,0:T(8,128)(2,1)}) custom-call(f32[16,800,128]{2,1,0:T(8,128)} %get-tuple-element.103.refs_0_, f32[4,800,128]{2,1,0:T(8,128)} %get-tuple-element.104.refs_1_, ...), custom_call_target="tpu_custom_call" | custom-call | tf_op jit(solution)/shard_map/exchange/pallas_call | solution.py:467
  845.7 31.4 %bucket.13 = (f32[16,800,128]{2,1,0:T(8,128)}, f32[4,800,128]{2,1,0:T(8,128)}, f32[400,128]{1,0:T(8,128)}) custom-call(s32[8192]{0:T(1024)} %bitcast.67, s32[1]{0:T(128)} %get-tuple-element.208.count_ref, s32[1024]{0:T(1024)} %bitcast.76, s32[32,256]{1,0:T(8,128)} %squeeze.95.rel_id_ref, f32[1024,512]{1,0:T(8,128)} %get-tuple-element.108.ent_ref.refs_3_, ...), custom_call_target="tpu_custom_call" | custom-call | tf_op jit(solution)/shard_map/bucket/pallas_call | solution.py:241
  877.1 124.1 %exchange.13 = (f32[1024,512]{1,0:T(8,128)}, f32[1024,1]{1,0:T(8,128)}, f32[128,512]{1,0:T(8,128)}, f32[128,1]{1,0:T(8,128)}, f32[1,128]{1,0:T(1,128)}, /*index=5*/bf16[16,800,128]{2,1,0:T(8,128)(2,1)}) custom-call(f32[16,800,128]{2,1,0:T(8,128)} %get-tuple-element.111.refs_0_, f32[4,800,128]{2,1,0:T(8,128)} %get-tuple-element.112.refs_1_, ...), custom_call_target="tpu_custom_call" | custom-call | tf_op jit(solution)/shard_map/exchange/pallas_call | solution.py:467
  1001.2 41.3 %bucket.14 = (f32[16,800,128]{2,1,0:T(8,128)}, f32[4,800,128]{2,1,0:T(8,128)}, f32[400,128]{1,0:T(8,128)}) custom-call(s32[8192]{0:T(1024)} %bitcast.66, s32[1]{0:T(128)} %get-tuple-element.209.count_ref, s32[1024]{0:T(1024)} %bitcast.75, s32[32,256]{1,0:T(8,128)} %squeeze.92.rel_id_ref, f32[1024,512]{1,0:T(8,128)} %get-tuple-element.116.ent_ref.refs_3_, ...), custom_call_target="tpu_custom_call" | custom-call | tf_op jit(solution)/shard_map/bucket/pallas_call | solution.py:241
  1042.5 83.1 %exchange.14 = (f32[1024,512]{1,0:T(8,128)}, f32[1024,1]{1,0:T(8,128)}, f32[128,512]{1,0:T(8,128)}, f32[128,1]{1,0:T(8,128)}, f32[1,128]{1,0:T(1,128)}, /*index=5*/bf16[16,800,128]{2,1,0:T(8,128)(2,1)}) custom-call(f32[16,800,128]{2,1,0:T(8,128)} %get-tuple-element.119.refs_0_, f32[4,800,128]{2,1,0:T(8,128)} %get-tuple-element.120.refs_1_, ...), custom_call_target="tpu_custom_call" | custom-call | tf_op jit(solution)/shard_map/exchange/pallas_call | solution.py:467
  1125.6 41.6 %bucket.15 = (f32[16,800,128]{2,1,0:T(8,128)}, f32[4,800,128]{2,1,0:T(8,128)}, f32[400,128]{1,0:T(8,128)}) custom-call(s32[8192]{0:T(1024)} %bitcast.65, s32[1]{0:T(128)} %get-tuple-element.210.count_ref, s32[1024]{0:T(1024)} %bitcast.74, s32[32,256]{1,0:T(8,128)} %squeeze.89.rel_id_ref, f32[1024,512]{1,0:T(8,128)} %get-tuple-element.124.ent_ref.refs_3_, ...), custom_call_target="tpu_custom_call" | custom-call | tf_op jit(solution)/shard_map/bucket/pallas_call | solution.py:241
  1167.2 139.9 %exchange.15 = (f32[16,832,128]{2,1,0:T(8,128)}, f32[128,512]{1,0:T(8,128)}, f32[1,128]{1,0:T(1,128)}) custom-call(f32[16,800,128]{2,1,0:T(8,128)} %get-tuple-element.127.refs_0_, f32[4,800,128]{2,1,0:T(8,128)} %get-tuple-element.128.refs_1_, f32[400,128]{1,0:T(8,128)} %get-tuple-element.129.refs_2_, f32[1024,512]{1,0:T(8,128)} %get-tuple-element.124.ent_ref.refs_3_, ...), custom_call_target="tpu_custom_call" | custom-call | tf_op jit(solution)/shard_map/exchange/pallas_call | solution.py:467
  1313.4 5.6 fusion.3
  1334.9 3.2 copy.90
  (111 shorter events, 89.0 us)
Async XLA Ops:
  7.2 142.2 %sort.9.cloned.1.call-start = ((), (), s32[]{:S(2)}) async-start(), calls=%async_computation | async-start | bytes 786464 | tf_op jit(solution)/shard_map/sort | solution.py:521
  8.0 115.8 %collective-permute-start.4 = (f32[1024]{0:T(1024)S(1)}, f32[1024]{0:T(1024)S(1)}, u32[]{:S(2)}, u32[]{:S(2)}) collective-permute-start(f32[1024]{0:T(1024)S(1)} %dynamic_slice.18), channel_id=1, source_target_pairs={{0,1},{2,3},{4,5},{6,7},{8,9},{10,11},{12,13},{14,15},{17,16},{19,... | collective-permute-start | bytes 12296 | tf_op jit(solution)/shard_map/ppermute | solution.py:512
  9.3 116.3 %collective-permute-start.1 = (s32[8,1024]{1,0:T(8,128)}, s32[8,1024]{1,0:T(8,128)}, u32[]{:S(2)}, u32[]{:S(2)}) collective-permute-start(s32[8,1024]{1,0:T(8,128)} %bitcast.73), channel_id=1, source_target_pairs={{0,1},{2,3},{4,5},{6,7},{8,9},{10,11},{12,13},{14,15},{17,16},{19,... | collective-permute-start | bytes 98312 | tf_op jit(solution)/shard_map/ppermute | solution.py:512
  26.3 100.7 %collective-permute-start = (s32[8,8192]{1,0:T(8,128)S(1)}, s32[8,8192]{1,0:T(8,128)}, u32[]{:S(2)}, u32[]{:S(2)}) collective-permute-start(s32[8,8192]{1,0:T(8,128)S(1)} %bitcast.63), channel_id=1, source_target_pairs={{0,1},{2,3},{4,5},{6,7},{8,9},{10,11},{12,13},{14,15},{17,16},{19,... | collective-permute-start | bytes 786440 | tf_op jit(solution)/shard_map/ppermute | solution.py:512
  67.4 91.5 %collective-permute-start.2 = (f32[1024,512]{1,0:T(8,128)}, f32[1024,512]{1,0:T(8,128)}, u32[]{:S(2)}, u32[]{:S(2)}) collective-permute-start(f32[1024,512]{1,0:T(8,128)} %constant_dynamic-slice_fusion), channel_id=1, source_target_pairs={{0,1},{2,3},{4,5},{6,7},{8,9},{10,11},{12,13},{14,15},{17,16},{19,... | collective-permute-start | bytes 6291464 | tf_op jit(solution)/shard_map/ppermute | solution.py:512
  82.0 4.8 copy-start
  107.5 3.4 copy-start.5
  109.4 53.6 %collective-permute-start.3 = (bf16[16,800,128]{2,1,0:T(8,128)(2,1)}, bf16[16,800,128]{2,1,0:T(8,128)(2,1)}, u32[]{:S(2)}, u32[]{:S(2)}) collective-permute-start(bf16[16,800,128]{2,1,0:T(8,128)(2,1)} %pad_maximum_fusion), channel_id=1, source_target_pairs={{0,1},{2,3},{4,5},{6,7},{8,9},{10,11},{12,13},{14,15},{17,16},{19,... | collective-permute-start | bytes 9830408 | tf_op jit(solution)/shard_map/ppermute | solution.py:512
  1313.3 5.7 copy-start.6
  1313.3 5.6 copy-start.7
  1313.3 5.6 copy-start.8
  1313.3 5.6 copy-start.9
  1313.3 5.6 copy-start.10
  1313.3 5.6 copy-start.11
  1313.4 5.6 copy-start.12
  1313.4 5.6 copy-start.13
  1332.5 5.5 copy-start.2
  1338.0 1.2 copy-start.3
  1338.0 1.9 copy-start.1
  1340.2 2.8 copy-start.4
Sparse Core Ops, SparseCore 0:
  129.0 20.1 sort.11.cloned.1.call-done
  (1 shorter events, 0.0 us)

commit v2 on v1

v2 whole, which is shorter than its diff:
```python
import functools

import jax
import jax.numpy as jnp
from jax import lax
from jax.experimental import pallas as pl
from jax.experimental.pallas import tpu as pltpu
from jax.sharding import PartitionSpec as P

LR_SCALE = 0.2
EPSILON = 1e-8
LANES = 128
HALF = 64
LEFT = 8
BLOCK = 256
CHUNK = 128
UNROLL = 128
STRIP = 32
REL_PAD = 128
TILES = range(4)
ROW_COL, ROW_ROW, COL_COL = (((1,), (0,)), ((1,), (1,)), ((0,), (0,)))
F32 = jnp.float32
BF16 = jnp.bfloat16
VMEM_LIMIT = 60 * 2**20


def wire_rows(rows):
    return 3 * rows + rows // LEFT


def columns_to_tiles(x):
    lane = lax.broadcasted_iota(jnp.int32, (x.shape[0], LANES), 1)
    end = x.shape[1] - 3 * LANES
    t0, t1, t2 = (x[:, band(t, LANES)] for t in TILES[:-1])
    t3 = jnp.concatenate([x[:, 3 * LANES:], jnp.zeros((x.shape[0], LANES - end), x.dtype)], axis=1)
    im = x.shape[1] // 2 - LANES
    cut = LANES - im
    b = jnp.where(lane < cut, pltpu.roll(t1, cut, 1), pltpu.roll(t2, cut, 1))
    c = jnp.where(lane < HALF, t1, jnp.where(lane < LANES - LEFT, pltpu.roll(t2, LANES - LEFT, 1), pltpu.roll(t3, LANES - LEFT, 1)))
    low, high = pltpu.roll(t1, HALF, 1), pltpu.roll(t3, cut, 1)
    d = jnp.where(lane < LEFT, low, jnp.where((lane >= HALF) & (lane < HALF + LEFT), high, 0.0))
    return [t0, b, c, d]


def tiles_to_columns(tiles, width):
    a, b, c, d = tiles
    lane = lax.broadcasted_iota(jnp.int32, a.shape, 1)
    im = width // 2 - LANES
    b, c, low, high = pltpu.roll(b, im, 1), pltpu.roll(c, LEFT, 1), pltpu.roll(d, HALF, 1), pltpu.roll(d, im, 1)
    t1 = jnp.where(lane < HALF, tiles[2], jnp.where(lane < im, low, b))
    t2 = jnp.where(lane < im, b, c)
    t3 = jnp.where(lane < LEFT, c, high)
    return jnp.concatenate([a, t1, t2, t3[:, :width - 3 * LANES]], axis=1)


def each_row(count, body):
    for u in range(count):
        body(u)


def band(n, size):
    return slice(n * size, (n + 1) * size)


def where_here():
    y, ent = lax.axis_index('data'), lax.axis_index('ent')
    return y, ent // 2, ent % 2, y // 2, y % 2


def fold_last(tile):
    n = tile.shape[0] // LEFT
    out = tile[:n]
    for k in range(1, LEFT):
        out = out + pltpu.roll(tile[band(k, n)], LEFT * k, 1)
    return out


def unfold_last(packed):
    keep = lax.broadcasted_iota(jnp.int32, packed.shape, 1) % HALF < LEFT
    return [jnp.where(keep, packed if k == 0 else pltpu.roll(packed, LANES - LEFT * k, 1), 0.0) for k in range(LEFT)]


def tiles_of(x):
    return [x[:, band(t, LANES)] for t in TILES]


def times(x, y):
    out = [x[0] * y[0] - x[1] * y[1], x[0] * y[1] + x[1] * y[0]]
    for a, b in zip(x[2:], y[2:]):
        low = lax.broadcasted_iota(jnp.int32, a.shape, 1) < HALF
        a_swap, b_swap = pltpu.roll(a, HALF, 1), pltpu.roll(b, HALF, 1)
        out.append(jnp.where(low, a * b - a_swap * b_swap, a_swap * b + a * b_swap))
    return out


def times_conj(x, y):
    out = [x[0] * y[0] + x[1] * y[1], x[1] * y[0] - x[0] * y[1]]
    for a, b in zip(x[2:], y[2:]):
        low = lax.broadcasted_iota(jnp.int32, a.shape, 1) < HALF
        a_swap, b_swap = pltpu.roll(a, HALF, 1), pltpu.roll(b, HALF, 1)
        out.append(jnp.where(low, a * b + a_swap * b_swap, a * b_swap - a_swap * b))
    return out


def tiles_at(ref, row, rows):
    block = ref[pl.ds(row * 4, rows * 4), :].reshape(rows // 8, 32, LANES)
    return [block[:, 8 * t:8 * t + 8].reshape(rows, LANES) for t in TILES]


def stack_tiles(tiles):
    rows = tiles[0].shape[0]
    return jnp.concatenate([t.reshape(rows // 8, 8, LANES) for t in tiles], axis=1).reshape(rows * 4, LANES)


def row_at(address):
    return pl.ds(address, 4, stride=8)


def row_address(row):
    return (row >> 3 << 5) | (row & 7)


def in_three(x):
    pieces = []
    for _ in range(3):
        piece = x.astype(BF16)
        pieces.append(piece)
        x = x - piece.astype(F32)
    return pieces


def dot(x, y, dims):
    return lax.dot_general(x, y, (dims, ((), ())), preferred_element_type=F32)


def bucket_kernel(cfg, edges_hbm, count_ref, negs_hbm, rel_ids_hbm, ent_ref, rel_ref, table_ref, tail_out, head_out, rel_out,
                  tail_rows, head_next, tail_next, head_buf, tail_buf, gh_last, gt_last, rel_buf, query_buf, pos_buf, score_buf, d_neg_buf, grad_buf, piece_buf,
                  neg_rows, neg_grad, rel_three, tail_acc0, tail_acc1, head_acc0, head_acc1, rel_acc, loss_acc,
                  edge_ref, neg_ref, rel_id_ref, sems):
    step, tail_bits = cfg
    chunk = CHUNK
    part = chunk // LEFT
    tail_acc, head_acc = (tail_acc0, tail_acc1), (head_acc0, head_acc1)
    count = count_ref[step]
    negs = neg_ref.shape[0]
    loads = [
        pltpu.make_async_copy(negs_hbm.at[step, 0], neg_ref, sems.at[0]),
        pltpu.make_async_copy(edges_hbm.at[step, 0], edge_ref, sems.at[1]),
        pltpu.make_async_copy(rel_ids_hbm.at[step], rel_id_ref, sems.at[2]),
    ]
    for load in loads:
        load.start()

    def head_of(e):
        return row_at(e >> tail_bits)

    def tail_of(e):
        return row_at(e & (2**tail_bits - 1))

    def widen(n, carry):
        base = pl.multiple_of(n * chunk, chunk)
        tiles = [table_ref[n, band(t, chunk), :].astype(F32) for t in TILES[:-1]]
        tiles.append(jnp.concatenate(unfold_last(table_ref[n, 3 * chunk:, :].astype(F32)), axis=0))
        tail_rows[pl.ds(base * 4, chunk * 4), :] = stack_tiles(tiles)
        for acc in tail_acc:
            acc[pl.ds(base * 4, chunk * 4), :] = jnp.zeros((chunk * 4, LANES), F32)
        return carry

    lax.fori_loop(0, table_ref.shape[0], widen, 0)

    def clear(n, carry):
        base = pl.multiple_of(n * chunk * 4, chunk * 4)
        for acc in head_acc:
            acc[pl.ds(base, chunk * 4), :] = jnp.zeros((chunk * 4, LANES), F32)
        return carry

    lax.fori_loop(0, head_out.shape[0], clear, 0)
    neg_grad[...] = jnp.zeros_like(neg_grad)
    gh_last[...] = jnp.zeros_like(gh_last)
    gt_last[...] = jnp.zeros_like(gt_last)
    rel_acc[...] = jnp.zeros_like(rel_acc)
    loss_acc[...] = jnp.zeros_like(loss_acc)
    for n, piece in enumerate(in_three(rel_ref[...])):
        rel_three[band(n, REL_PAD), :] = piece
    for load in loads:
        load.wait()

    def take_negs(n, carry):
        base = pl.multiple_of(n * UNROLL, UNROLL)

        def take(u):
            head_buf[row_at(row_address(u)), :] = tail_rows[row_at(neg_ref[base + u]), :]

        each_row(UNROLL, take)
        for t, tile in enumerate(tiles_at(head_buf, 0, UNROLL)):
            neg_rows[pl.ds(base, UNROLL), band(t, LANES)] = tile.astype(BF16)
        return carry

    lax.fori_loop(0, negs // UNROLL, take_negs, 0)

    def take_edges(base):
        def take(u):
            e = edge_ref[base + u]
            head_next[row_at(row_address(u)), :] = ent_ref[head_of(e), :]
            tail_next[row_at(row_address(u)), :] = tail_rows[tail_of(e), :]

        return take

    def put_edges(base):
        def put(pair):
            for lane in range(2):
                u = 2 * pair + lane
                e = edge_ref[base + u]
                row = row_at(row_address(u))
                head_acc[lane][head_of(e), :] += gh_last[row, :]
                tail_acc[lane][tail_of(e), :] += gt_last[row, :]

        return put

    each_row(BLOCK, take_edges(BLOCK))
    spans = [slice(r, r + STRIP) for r in range(0, BLOCK, STRIP)]

    def block(n, carry):
        base = pl.multiple_of(n * BLOCK, BLOCK)
        hot = lax.broadcasted_iota(jnp.int32, (REL_PAD, BLOCK), 0) == rel_id_ref[pl.ds(n, 1), :]
        hot = jnp.where(hot, 1.0, 0.0).astype(BF16)
        rel_buf[...] = dot(jnp.concatenate([hot] * 3, axis=0), rel_three[...], COL_COL)
        for span in spans:
            head, tail, rel = tiles_at(head_next, span.start, STRIP), tiles_at(tail_next, span.start, STRIP), tiles_of(rel_buf[span, :])
            wide = slice(4 * span.start, 4 * span.stop)
            head_buf[wide, :], tail_buf[wide, :] = stack_tiles(head), stack_tiles(tail)
            total = None
            for t, q in enumerate(times(head, rel)):
                q = q.astype(BF16)
                query_buf[span, band(t, LANES)] = q
                product = q.astype(F32) * tail[t]
                total = product if total is None else total + product
            pos_buf[span, :] = jnp.sum(total, axis=1, keepdims=True)
        each_row(BLOCK, take_edges(base + 2 * BLOCK))
        each_row(BLOCK // 2, put_edges(base))
        score_buf[...] = dot(query_buf[...], neg_rows[...], ROW_ROW)
        for span in spans:
            weight = jnp.where(lax.broadcasted_iota(jnp.int32, (STRIP, 1), 0) + (base + span.start) < count, 1.0, 0.0)
            score, pos = score_buf[span, :], pos_buf[span, :]
            top = jnp.maximum(jnp.max(score, axis=1, keepdims=True), pos)
            pos_exp = jnp.exp(pos - top)
            neg_exp = jnp.exp(score - top)
            total = pos_exp + jnp.sum(neg_exp, axis=1, keepdims=True)
            loss_acc[...] += jnp.sum(weight * (top + jnp.log(total) - pos), axis=0, keepdims=True)
            pos_buf[span, :] = weight * (pos_exp / total - 1.0)
            d_neg_buf[span, :] = ((weight / total) * neg_exp).astype(BF16)
        grad_buf[...] = dot(d_neg_buf[...], neg_rows[...], ROW_COL)
        neg_grad[...] += dot(d_neg_buf[...], query_buf[...], COL_COL)
        for span in spans:
            wide = slice(4 * span.start, 4 * span.stop)
            d_pos = pos_buf[span, :]
            tail, rel = tiles_at(tail_buf, span.start, STRIP), tiles_of(rel_buf[span, :])
            grad_q = [d_pos * x + y for x, y in zip(tail, tiles_of(grad_buf[span, :]))]
            gt_last[wide, :] = stack_tiles([d_pos * q.astype(F32) for q in tiles_of(query_buf[span, :])])
            gh_last[wide, :] = stack_tiles(times_conj(grad_q, rel))
            for t, grad in enumerate(times_conj(grad_q, tiles_at(head_buf, span.start, STRIP))):
                for k, piece in enumerate(in_three(grad)):
                    piece_buf[k * BLOCK + span.start:k * BLOCK + span.stop, band(t, LANES)] = piece
        rel_acc[...] += dot(jnp.concatenate([hot] * 3, axis=1), piece_buf[...], ROW_COL)
        return carry

    blocks = pl.cdiv(count, BLOCK)
    lax.fori_loop(0, blocks, block, 0)
    each_row(BLOCK // 2, put_edges(pl.multiple_of(blocks * BLOCK, BLOCK)))

    def put_negs(n, carry):
        base = pl.multiple_of(n * UNROLL, UNROLL)
        gt_last[:4 * UNROLL, :] = stack_tiles(tiles_of(neg_grad[pl.ds(base, UNROLL), :]))

        def put(pair):
            for lane in range(2):
                u = 2 * pair + lane
                tail_acc[lane][row_at(neg_ref[base + u]), :] += gt_last[row_at(row_address(u)), :]

        each_row(UNROLL // 2, put)
        return carry

    lax.fori_loop(0, negs // UNROLL, put_negs, 0)

    def emit(out_ref, acc):
        def one(n, carry):
            base = pl.multiple_of(n * chunk, chunk)
            tiles = [a + b for a, b in zip(tiles_at(acc[0], base, chunk), tiles_at(acc[1], base, chunk))]
            for t in TILES[:-1]:
                out_ref[n, band(t, chunk), :] = tiles[t]
            out_ref[n, 3 * chunk:, :] = fold_last(tiles[3])
            return carry

        lax.fori_loop(0, out_ref.shape[0], one, 0)

    emit(tail_out, tail_acc)
    emit(head_out, head_acc)
    _, x, _, top, _ = where_here()
    group = 2 * x + top
    row = lax.broadcasted_iota(jnp.int32, (REL_PAD, LANES), 0)
    lane = lax.broadcasted_iota(jnp.int32, (REL_PAD, LANES), 1)
    loss = jnp.where(lane == group, loss_acc[...], 0.0)
    for t in TILES[:-1]:
        rows = rel_acc[:, band(t, LANES)]
        rel_out[band(t, REL_PAD), :] = jnp.where(row == REL_PAD - 1, loss, rows) if t == 0 else rows
    rel_out[3 * REL_PAD:, :] = fold_last(rel_acc[:, 3 * LANES:])


def bucket_call(step, tail_bits, edges, counts, negs, rel_ids, ent, rel, table):
    smem, vmem, hbm = (pl.BlockSpec(memory_space=m) for m in (pltpu.SMEM, pltpu.VMEM, pl.ANY))
    rows, neg_count, chunks = ent.shape[0] // 4, negs.shape[-1], table.shape[0]
    width = 4 * LANES
    wire = wire_rows(CHUNK)
    block = pltpu.VMEM((BLOCK * 4, LANES), F32)
    table_rows = pltpu.VMEM((chunks * CHUNK * 4, LANES), F32)
    head_rows = pltpu.VMEM((rows * 4, LANES), F32)
    return pl.pallas_call(
        functools.partial(bucket_kernel, (step, tail_bits)),
        out_shape=(
            jax.ShapeDtypeStruct((chunks, wire, LANES), F32),
            jax.ShapeDtypeStruct((rows // CHUNK, wire, LANES), F32),
            jax.ShapeDtypeStruct((wire_rows(REL_PAD), LANES), F32),
        ),
        in_specs=[hbm, smem, hbm, hbm, vmem, vmem, vmem],
        out_specs=(vmem, vmem, vmem),
        scratch_shapes=[
            table_rows, *[block] * 6, pltpu.VMEM((BLOCK, width), F32), pltpu.VMEM((BLOCK, width), BF16), pltpu.VMEM((BLOCK, 1), F32),
            pltpu.VMEM((BLOCK, neg_count), F32), pltpu.VMEM((BLOCK, neg_count), BF16), pltpu.VMEM((BLOCK, width), F32), pltpu.VMEM((3 * BLOCK, width), BF16),
            pltpu.VMEM((neg_count, width), BF16), pltpu.VMEM((neg_count, width), F32), pltpu.VMEM((3 * REL_PAD, width), BF16),
            table_rows, table_rows, head_rows, head_rows,
            pltpu.VMEM((REL_PAD, width), F32), pltpu.VMEM((1, 1), F32),
            pltpu.SMEM((edges.shape[-1],), jnp.int32), pltpu.SMEM((neg_count,), jnp.int32), pltpu.VMEM(rel_ids.shape[1:], jnp.int32), pltpu.SemaphoreType.DMA((3,)),
        ],
        compiler_params=pltpu.CompilerParams(vmem_limit_bytes=VMEM_LIMIT),
        name='bucket',
    )(edges, counts, negs, rel_ids, ent, rel, table)


def entry(peers):
    barrier = pltpu.get_barrier_semaphore()
    for peer in peers:
        pl.semaphore_signal(barrier, inc=1, device_id=peer, device_id_type=pl.DeviceIdType.MESH)
    pl.semaphore_wait(barrier, len(peers))


def remote(src, dst, send, recv, peer):
    return pltpu.make_async_remote_copy(src_ref=src, dst_ref=dst, send_sem=send, recv_sem=recv, device_id=peer, device_id_type=pl.DeviceIdType.MESH)


def adagrad(rows, state, grad, mean_of, learn_rate):
    square = grad[0] * grad[0] + grad[1] * grad[1] + grad[2] * grad[2] + grad[3] * grad[3]
    state = state + jnp.sum(square, axis=1, keepdims=True) / mean_of
    root = jnp.sqrt(state + EPSILON)
    return [r - learn_rate * (g / root) for r, g in zip(rows, grad)], state


def exchange_kernel(cfg, tail_ref, head_ref, rel_grad_ref, ent_ref, state_ref, rel_ref, rel_state_ref, *refs):
    step, groups, chunks, emb_width, last = cfg
    if last:
        ent_wire, rel_out, loss_out, *refs = refs
    else:
        ent_out, state_out, rel_out, rel_state_out, loss_out, table, *refs = refs
    (own, from_core, from_y, from_group, rel_sum, rel_from, send_buf,
     own_sem, core_send, core_recv, y_send, y_recv, group_send, group_recv, rel_send, rel_recv, out_send, out_recv) = refs
    learn_rate = LR_SCALE * emb_width ** -0.25
    chunk = CHUNK
    y, x, core, top, bot = where_here()
    mine = 2 * x + top
    x_size = groups // 2

    def place(group, low, c):
        return {'data': 2 * (group % 2) + low, 'ent': 2 * (group // 2) + c}

    def at(dy, dx, c):
        return {'data': dy, 'ent': 2 * dx + c}

    def turned(shift):
        return (bot + shift) % 2

    other_core = at(y, x, 1 - core)
    other_y = at(2 * top + 1 - bot, x, core)
    rel_peers = (other_core, other_y, at(3 - y, x, core), at(y, x + 1 - 2 * (x % 2), core), at(y, x_size - 1 - x, core))
    grad_to = place((mine + step) % groups, turned(step), core)
    grad_from = place((mine + groups - step) % groups, turned(step), core)
    nxt = step + 1
    table_to = place((mine + groups - nxt) % groups, turned(nxt), core)
    table_from = place((mine + nxt) % groups, turned(nxt), core)
    peers = list(rel_peers)
    if step:
        peers += [grad_to, grad_from]
    if last:
        for turn in range(4):
            peers.append(at((y + turn) % 4, x, top))
        senders = [at((2 * core + d), x, c) for d in range(2) for c in range(2)]
        peers += senders
    else:
        peers += [table_to, table_from]
    entry(peers)
    keep = turned(step)
    pending = []

    def start(copy):
        copy.start()
        pending.append(copy)
        return copy

    shards = [(1 - keep, k) for k in range(chunks)] + [(keep, k) for k in range(chunks)]
    loads, cores = [], []
    rel_copies = [start(remote(rel_grad_ref, rel_from.at[0], rel_send.at[0], rel_recv.at[0], rel_peers[0]))]
    for n, (low, k) in enumerate(shards):
        cores.append(start(remote(tail_ref.at[(low * 2 + 1 - core) * chunks + k], from_core.at[n], core_send.at[n], core_recv.at[n], other_core)))
        load = pltpu.make_async_copy(tail_ref.at[(low * 2 + core) * chunks + k], own.at[n], own_sem.at[n])
        load.start()
        loads.append(load)

    def rel_step(n):
        rel_copies[n].wait_recv()
        rel_sum[n] = (rel_grad_ref[...] if n == 0 else rel_sum[n - 1]) + rel_from[n]
        if n + 1 < len(rel_peers):
            rel_copies.append(start(remote(rel_sum.at[n], rel_from.at[n + 1], rel_send.at[n + 1], rel_recv.at[n + 1], rel_peers[n + 1])))

    rel_step(0)
    ys = []
    for k in range(chunks):
        loads[k].wait()
        cores[k].wait_recv()
        own[k] = own[k] + from_core[k]
        ys.append(start(remote(own.at[k], from_y.at[k], y_send.at[k], y_recv.at[k], other_y)))
    rel_step(1)
    for k in range(chunks, 2 * chunks):
        loads[k].wait()
        cores[k].wait_recv()
        own[k] = own[k] + from_core[k]
    rel_step(2)
    gs, outs, forwards, crosses = [], [], [], []

    def stage_group(k):
        ys[k].wait_recv()
        own[chunks + k] = own[chunks + k] + from_y[k]
        if step:
            gs.append(start(remote(own.at[chunks + k], from_group.at[k], group_send.at[k], group_recv.at[k], grad_to)))

    def stage_update(k):
        if step:
            gs[k].wait_recv()
        total = from_group if step else own
        base = k if step else chunks + k
        grad = [total[base, band(t, chunk), :] + head_ref[k, band(t, chunk), :] for t in TILES[:-1]]
        grad.append(jnp.concatenate(unfold_last(total[base, 3 * chunk:, :] + head_ref[k, 3 * chunk:, :]), axis=0))
        span = band(k, chunk)
        rows, state = adagrad(tiles_at(ent_ref, k * chunk, chunk), state_ref[span, :], grad, emb_width, learn_rate)
        wire = rows[:3] + [fold_last(rows[3])]
        if last:
            lane = lax.broadcasted_iota(jnp.int32, (chunk, LANES), 1)
            wire.append(fold_last(jnp.where(lane < 1, state, 0.0)))
        else:
            ent_out[band(k, 4 * chunk), :] = stack_tiles(rows)
            state_out[span, :] = state
        offset = 0
        for piece in wire:
            send_buf[k, offset:offset + piece.shape[0], :] = piece.astype(send_buf.dtype)
            offset += piece.shape[0]
        slot = (bot * 2 + core) * chunks + k
        if last:
            for turn in range(1, 4):
                start(remote(send_buf.at[k], ent_wire.at[slot], out_send.at[turn * chunks + k], out_recv.at[slot], at((y + turn) % 4, x, top)))

            @pl.when(core == top)
            def _():
                pltpu.make_async_copy(send_buf.at[k], ent_wire.at[slot], out_recv.at[slot]).start()

            @pl.when(core != top)
            def _():
                remote(send_buf.at[k], ent_wire.at[slot], out_send.at[k], out_recv.at[slot], other_core).start()
        else:
            outs.append(start(remote(send_buf.at[k], table.at[slot], out_send.at[k], out_recv.at[k], table_to)))

    def forward(n, low, k, peer):
        slot = (low * 2 + core) * chunks + k
        return start(remote(table.at[slot], table.at[slot], out_send.at[n * chunks + k], out_recv.at[n * chunks + k], peer))

    def stage_forward(k):
        if last:
            return
        outs[k].wait_recv()
        forwards.append(forward(1, turned(nxt), k, other_y))
        crosses.append(forward(2, turned(nxt), k, other_core))

    def stage_cross(k):
        if last:
            return
        forwards[k].wait_recv()
        crosses.append(forward(3, 1 - turned(nxt), k, other_core))

    stages = (stage_group, stage_update, stage_forward, stage_cross)
    for tick in range(chunks + len(stages) - 1):
        for lag, stage in enumerate(stages):
            if 0 <= tick - lag < chunks:
                stage(tick - lag)
        if tick in (0, 1):
            rel_step(3 + tick)

    summed = rel_sum[len(rel_peers) - 1]
    rel_grad = [summed[band(t, REL_PAD)] for t in TILES[:-1]] + [jnp.concatenate(unfold_last(summed[3 * REL_PAD:]), axis=0)]
    loss_out[...] = rel_grad[0][REL_PAD - 1:, :]
    row = lax.broadcasted_iota(jnp.int32, (REL_PAD, LANES), 0)
    rel_grad[0] = jnp.where(row < REL_PAD - 1, rel_grad[0], 0.0)
    rel_rows, rel_state = adagrad(tiles_of(rel_ref[...]), rel_state_ref[...], rel_grad, emb_width, learn_rate)
    for t in TILES:
        rel_out[:, band(t, LANES)] = rel_rows[t]
    if not last:
        rel_state_out[...] = rel_state

    if last:
        for slot in range(4 * chunks):
            remote(ent_wire.at[slot], ent_wire.at[slot], out_send.at[0], out_recv.at[slot], other_core).wait_recv()

        @pl.when(core != top)
        def _():
            for k in range(chunks):
                remote(send_buf.at[k], send_buf.at[k], out_send.at[k], out_recv.at[k], other_core).wait_send()
    else:
        for copy in crosses:
            copy.wait_recv()
    for copy in pending:
        copy.wait_send()


def exchange_call(step, groups, emb_width, tail, head, rel_grad, ent, state, rel, rel_state):
    vmem, hbm = pl.BlockSpec(memory_space=pltpu.VMEM), pl.BlockSpec(memory_space=pl.ANY)
    chunks = head.shape[0]
    wire = wire_rows(CHUNK)
    last = step == groups - 1
    like = lambda x: jax.ShapeDtypeStruct(x.shape, x.dtype)
    loss = jax.ShapeDtypeStruct((1, LANES), F32)
    out_wire = wire + (CHUNK // LEFT if last else 0)
    out_type = F32 if last else BF16
    gathered = jax.ShapeDtypeStruct((4 * chunks, out_wire, LANES), out_type)
    out_shape = (gathered, like(rel), loss) if last else (like(ent), like(state), like(rel), like(rel_state), loss, gathered)
    sems = lambda n: pltpu.SemaphoreType.DMA((n,))
    return pl.pallas_call(
        functools.partial(exchange_kernel, (step, groups, chunks, emb_width, last)),
        out_shape=out_shape,
        in_specs=[hbm] + [vmem] * 6,
        out_specs=tuple(vmem for _ in out_shape),
        scratch_shapes=[
            pltpu.VMEM((2 * chunks, wire, LANES), F32), pltpu.VMEM((2 * chunks, wire, LANES), F32),
            pltpu.VMEM((chunks, wire, LANES), F32), pltpu.VMEM((chunks, wire, LANES), F32),
            pltpu.VMEM((5, *rel_grad.shape), F32), pltpu.VMEM((5, *rel_grad.shape), F32),
            pltpu.VMEM((chunks, out_wire, LANES), out_type),
            sems(2 * chunks), sems(2 * chunks), sems(2 * chunks), sems(chunks), sems(chunks), sems(chunks), sems(chunks),
            sems(5), sems(5), sems(4 * chunks), sems(4 * chunks),
        ],
        compiler_params=pltpu.CompilerParams(vmem_limit_bytes=VMEM_LIMIT, collective_id=step, has_side_effects=True),
        name='exchange',
    )(tail, head, rel_grad, ent, state, rel, rel_state)


def index_kernel(cfg, head_ref, tail_ref, rel_ref, mask_ref, neg_ref, key_out, count_out, neg_out, packed, shares, neg_buf, send_sem, recv_sem, neg_send, neg_recv):
    head_bits, tail_bits, spare = cfg
    y, x, core, top, bot = where_here()
    own = 2 * x + core
    other_core = {'data': y, 'ent': 2 * x + 1 - core}
    users = [(c, 2 * core + d) for c in range(2) for d in range(2)]
    users = [({'data': row, 'ent': 2 * x + c}, (core == c) & (y == row)) for c, row in users]
    entry([peer for peer, _ in users] + [{'data': row, 'ent': 2 * x + top} for row in range(4)] + [other_core])
    edges = head_ref[...] | (tail_ref[...] << tail_bits) | (rel_ref[...] << (2 * tail_bits))
    packed[...] = jnp.where(mask_ref[...] > 0, edges, spare << (2 * tail_bits))
    neg_buf[...] = row_address(neg_ref[...])
    to_users = [remote(packed, shares.at[y], send_sem.at[n], recv_sem.at[y], peer) for n, (peer, _) in enumerate(users)]
    for copy, (_, here) in zip(to_users, users):
        @pl.when(jnp.logical_not(here))
        def _():
            copy.start()

    @pl.when(core == top)
    def _():
        pltpu.make_async_copy(packed, shares.at[y], recv_sem.at[y]).start()
        remote(neg_buf, neg_out, neg_send, neg_recv, other_core).start()
        neg_out[...] = neg_buf[...]

    count = jnp.zeros((packed.shape[0], 1), jnp.int32)
    width = packed.shape[1]
    for row in range(4):
        remote(packed, shares.at[row], send_sem.at[0], recv_sem.at[row], other_core).wait_recv()
        share = shares[row]
        mine = ((share >> head_bits) & 3 == 2 * bot + core) & (share >> (2 * tail_bits) != spare)
        local = (share & (2**head_bits - 1)) | (share >> tail_bits << head_bits)
        key_out[:, band(row, width)] = jnp.where(mine, local, spare << (head_bits + tail_bits))
        count = count + jnp.sum(jnp.where(mine, 1, 0), axis=1, keepdims=True)
    count_out[...] = jnp.broadcast_to(count, count_out.shape)
    for copy, (_, here) in zip(to_users, users):
        @pl.when(jnp.logical_not(here))
        def _():
            copy.wait_send()

    @pl.when(core == top)
    def _():
        remote(neg_buf, neg_out, neg_send, neg_recv, other_core).wait_send()

    @pl.when(core != top)
    def _():
        remote(neg_buf, neg_out, neg_send, neg_recv, other_core).wait_recv()


def index_call(cfg, head, tail, rel, mask, neg, reps):
    vmem = pl.BlockSpec(memory_space=pltpu.VMEM)
    groups, share = head.shape
    return pl.pallas_call(
        functools.partial(index_kernel, cfg),
        out_shape=(jax.ShapeDtypeStruct((groups, reps * share), jnp.int32), jax.ShapeDtypeStruct((groups, LANES), jnp.int32), jax.ShapeDtypeStruct(neg.shape, jnp.int32)),
        in_specs=[vmem] * 5,
        out_specs=(vmem,) * 3,
        scratch_shapes=[pltpu.VMEM(head.shape, jnp.int32), pltpu.VMEM((reps, *head.shape), jnp.int32), pltpu.VMEM(neg.shape, jnp.int32),
                        pltpu.SemaphoreType.DMA((4,)), pltpu.SemaphoreType.DMA((4,)), pltpu.SemaphoreType.DMA, pltpu.SemaphoreType.DMA],
        compiler_params=pltpu.CompilerParams(collective_id=20, has_side_effects=True),
        name='setup_index',
    )(head, tail, rel, mask, neg)


def rows_kernel(ent_hbm, rel_ref, table, ent_out, rel_out, rows_buf, away, load_sem, table_send, table_recv, ent_send, ent_recv):
    y, x, core, top, bot = where_here()
    other_core = {'data': y, 'ent': 2 * x + 1 - core}
    chunks, chunk = table.shape[0], CHUNK
    shard = chunks // 4
    entry([other_core])
    rel_rows = rel_ref.shape[0]
    pad = jnp.zeros((REL_PAD - rel_rows, rel_ref.shape[1]), F32)
    for t, tile in enumerate(columns_to_tiles(jnp.concatenate([rel_ref[...], pad], axis=0))):
        rel_out[:, band(t, LANES)] = tile

    def load(n):
        return pltpu.make_async_copy(ent_hbm.at[pl.ds(pl.multiple_of(n * chunk, chunk), chunk), :], rows_buf.at[n % 4], load_sem.at[n % 4])

    def table_copy(q):
        part = table.at[pl.ds(q * shard, shard)]
        return remote(part, part, table_send.at[q], table_recv.at[q], other_core)

    ent_copy = remote(away, ent_out, ent_send, ent_recv, other_core)

    @pl.when(core == top)
    def _():
        for n in range(3):
            load(n).start()
        for q in range(4):
            def one(k, carry):
                n = q * shard + k

                @pl.when(n + 3 < chunks)
                def _():
                    load(n + 3).start()

                load(n).wait()
                tiles = columns_to_tiles(rows_buf[n % 4])
                for t in TILES[:-1]:
                    table[n, band(t, chunk), :] = tiles[t].astype(BF16)
                table[n, 3 * chunk:, :] = fold_last(tiles[3]).astype(BF16)
                place = pl.ds(pl.multiple_of(k * chunk * 4, chunk * 4), chunk * 4)

                @pl.when(2 * bot + core == q)
                def _():
                    ent_out[place, :] = stack_tiles(tiles)

                @pl.when(2 * bot + 1 - core == q)
                def _():
                    away[place, :] = stack_tiles(tiles)

                return carry

            lax.fori_loop(0, shard, one, 0)
            table_copy(q).start()

            @pl.when(2 * bot + 1 - core == q)
            def _():
                ent_copy.start()

        for q in range(4):
            table_copy(q).wait_send()
        ent_copy.wait_send()

    @pl.when(core != top)
    def _():
        for q in range(4):
            table_copy(q).wait_recv()
        ent_copy.wait_recv()


def rows_call(ent, rel):
    vmem, hbm = pl.BlockSpec(memory_space=pltpu.VMEM), pl.BlockSpec(memory_space=pl.ANY)
    rows, width = ent.shape
    chunks = rows // CHUNK
    dma = pltpu.SemaphoreType.DMA
    return pl.pallas_call(
        rows_kernel,
        out_shape=(jax.ShapeDtypeStruct((chunks, wire_rows(CHUNK), LANES), BF16), jax.ShapeDtypeStruct((rows, LANES), F32), jax.ShapeDtypeStruct((REL_PAD, 4 * LANES), F32)),
        in_specs=[hbm, vmem],
        out_specs=(vmem,) * 3,
        scratch_shapes=[pltpu.VMEM((4, CHUNK, width), F32), pltpu.VMEM((rows, LANES), F32), dma((4,)), dma((4,)), dma((4,)), dma, dma],
        compiler_params=pltpu.CompilerParams(collective_id=21, has_side_effects=True),
        cost_estimate=pl.CostEstimate(flops=10**9, bytes_accessed=2 * 10**7, transcendentals=0),
        name='setup_rows',
    )(ent, rel)


def finish_kernel(width, rel_rows, wire_ref, rel_ref, ent_out, rel_out):
    chunk = CHUNK
    tiles = [wire_ref[0, band(t, chunk), :] for t in TILES[:-1]]
    tiles.append(jnp.concatenate(unfold_last(wire_ref[0, 3 * chunk:wire_rows(chunk), :]), axis=0))
    ent_out[...] = tiles_to_columns(tiles, width)

    @pl.when(pl.program_id(0) == 0)
    def _():
        rel_out[...] = tiles_to_columns(tiles_of(rel_ref[...]), width)[:rel_rows]


def finish_call(wire, rel, width, rel_rows):
    chunks = wire.shape[0]
    return pl.pallas_call(
        functools.partial(finish_kernel, width, rel_rows),
        out_shape=(jax.ShapeDtypeStruct((chunks * CHUNK, width), F32), jax.ShapeDtypeStruct((rel_rows, width), F32)),
        grid=(chunks,),
        in_specs=[pl.BlockSpec((1, *wire.shape[1:]), lambda n: (n, 0, 0)), pl.BlockSpec(rel.shape, lambda n: (0, 0))],
        out_specs=(pl.BlockSpec((CHUNK, width), lambda n: (n, 0)), pl.BlockSpec((rel_rows, width), lambda n: (0, 0))),
        name='finish',
    )(wire, rel)


def solution(mesh):
    groups = mesh.shape['ent']
    data_reps = mesh.shape['data']
    row_spec = P(('sweep', 'ent'), None)
    edge_spec = P(('sweep', 'ent'), None, 'data')

    def device_fn(ent_table, ent_state, rel_table, head_idx, tail_idx, rel_idx, edge_mask, neg_idx):
        part_rows, emb_width = ent_table.shape
        rel_rows = rel_table.shape[0]
        bucket_edges = head_idx.shape[2] * data_reps
        shard = part_rows // 4
        tail_bits = (part_rows - 1).bit_length()
        head_bits = (shard - 1).bit_length()
        spare = 2**(REL_PAD - 1).bit_length() - 1
        ent = lax.axis_index('ent')
        _, _, core, top, bot = where_here()

        keys, counts, neg = index_call((head_bits, tail_bits, spare), head_idx[0], tail_idx[0], rel_idx[0], edge_mask[0], neg_idx[0], data_reps)
        keys = lax.sort(keys, dimension=1)
        counts = counts[:, 0]
        neg = neg[:, None]
        rel_ids = (keys >> (head_bits + tail_bits)).reshape(groups, -1, BLOCK)
        words = (row_address(keys & (shard - 1)) << (tail_bits + 2)) | row_address((keys >> head_bits) & (part_rows - 1))
        words = jnp.pad(words, ((0, 0), (BLOCK, BLOCK)))[:, None]

        table, ent_now, rel_now = rows_call(ent_table, rel_table)
        to_core = lambda c: lax.dynamic_slice_in_dim(ent_state, (2 * bot + c) * shard, shard)
        away = [(d * groups + 2 * (n // 2) + d // 2, d * groups + 2 * (n // 2) + 1 - d // 2) for d in range(data_reps) for n in range(0, groups, 2)]
        state_now = jnp.where(core == top, to_core(core), lax.ppermute(to_core(1 - core), ('data', 'ent'), away))[:, None]
        rel_state = jnp.zeros((REL_PAD, 1), F32)
        losses = []
        for step in range(groups):
            tail, head, rel_grad = bucket_call(step, tail_bits + 2, words, counts, neg, rel_ids, ent_now, rel_now, table)
            out = exchange_call(step, groups, emb_width, tail, head, rel_grad, ent_now, state_now, rel_now, rel_state)
            if step + 1 < groups:
                ent_now, state_now, rel_now, rel_state, loss, table = out
            else:
                wire, rel_now, loss = out
            losses.append(loss)
        ent_out, rel_out = finish_call(wire, rel_now, emb_width, rel_rows)
        state_out = wire[:, wire_rows(CHUNK):, :HALF:LEFT].transpose(0, 2, 1).reshape(part_rows)
        loss_rows = jnp.concatenate(losses, axis=0) / bucket_edges
        bucket_loss = lax.dynamic_slice_in_dim(loss_rows, ent, 1, axis=1).reshape(1, groups)
        return ent_out, state_out, rel_out, bucket_loss

    return jax.shard_map(device_fn, mesh=mesh, in_specs=(row_spec, P(('sweep', 'ent')), P('sweep', None), edge_spec, edge_spec, edge_spec, edge_spec, P(('sweep', 'ent'), None, None)), out_specs=(row_spec, P(('sweep', 'ent')), P('sweep', None), row_spec), check_vma=False)
```

time: 1350 us -> 1210 us (0.90)
  local copies, waits for them, and re-layouts: 152 us -> 30.4 us
  other arithmetic: 22.2 us -> 1.77 us
  Pallas kernels: 1140 us -> 1160 us
  blocking collectives: 14.7 us -> 0 us
    slice x23 -> x1, local copies, waits for them, and re-layouts: 39 us -> 1.3 us  [device_fn(): counts = counts[:, 0]]
    sort x2, local copies, waits for them, and re-layouts: 18.2 us -> 0.06 us  [device_fn(): keys = lax.sort(keys, dimension=1)]
    pallas_call x8 -> x11, Pallas kernels: 282 us -> 300 us  [the longest x8 248 us: bucket_call(): pl.pallas_call(functools.partial(bucket_kernel, (step, tail_bits)), out_s...]
    concatenate x4 -> x0, local copies, waits for them, and re-layouts: 15.7 us -> none  [the longest x2 15.6 us: columns_to_tiles(): jnp.concatenate([re[..., :LANES], im[..., :LANES], re[..., LANES:cut], im...]
    all_gather x1 -> x0, blocking collectives: 14.7 us -> none  [device_fn(): packed = lax.all_gather(packed, 'data', axis=1, tiled=True)]
    transpose x5 -> x0, local copies, waits for them, and re-layouts: 14.3 us -> none  [the longest x2 10.7 us: tiles_to_wire(): last = last.transpose(0, 2, 3, 1, 4).reshape(n, size // LEFT, LANES)]
    unnamed x46 -> x24, local copies, waits for them, and re-layouts: 27.7 us -> 20.6 us
  transfers between devices with their start and end apart: 5 -> 1, of which waited for: 0 -> 0; matrix products, arithmetic and copies ran while one was open for 8% -> 1% of each run, Pallas kernels for 0% -> 3%
where the time goes in v2:
time: 1210 us
  Pallas kernels  1160 us (96%)
  local copies, waits for them, and re-layouts  30.4 us (3%)
  between operations  14.8 us (1%)
    pallas_call x8, Pallas kernels, exchange_call(): pl.pallas_call(functools.partial(exchange_kernel, (step, groups, chunks,...  860 us
    pallas_call x8, Pallas kernels, bucket_call(): pl.pallas_call(functools.partial(bucket_kernel, (step, tail_bits)), out_s...  248 us
  transfers between devices with their start and end apart: 1, of which 0 were waited for; matrix products, arithmetic and copies ran while one was open for 1% of the time, Pallas kernels for 3%

profile of v2, /device:TPU:97, one launch (start us, length us, event | category | flops | bytes accessed | tf_op | source)
XLA Modules:
  0.0 1207.6 jit_solution(13302029851804422504)
XLA Ops:
  8.0 1.3 collective-permute-start
  9.3 13.4 %setup_index.1 = (s32[8,8192]{1,0:T(8,128)}, s32[8,128]{1,0:T(8,128)}, s32[8,1024]{1,0:T(8,128)}) custom-call(s32[8,2048]{1,0:T(8,128)} %bitcast.22, s32[8,2048]{1,0:T(8,128)} %bitcast.23, s32[8,2048]{1,0:T(8,128)} %bitcast.24, s32[8,2048]{1,0:T(8,128)} %bitcast.25, s32[8,1024]{1,0:T(8,128)} %bitcast.26), custom_call_target="tpu_custom_call" | custom-call | tf_op jit(solution)/shard_map/setup_index/pallas_call | solution.py:609
  22.8 1.8 copy.17.rel_ref
  24.5 1.3 slice_reduce_fusion.count_ref
  25.8 8.6 copy.16.ent_hbm
  34.4 16.9 %setup_rows.1 = (bf16[32,400,128]{2,1,0:T(8,128)(2,1)}, f32[4096,128]{1,0:T(8,128)}, f32[128,512]{1,0:T(8,128)}) custom-call(f32[4096,400]{1,0:T(8,128)} %copy.16.ent_hbm, f32[107,400]{1,0:T(8,128)} %copy.17.rel_ref), custom_call_target="tpu_custom_call" | custom-call | flops 1000000000 | bytes 20000000 | tf_op jit(solution)/shard_map/setup_rows/pallas_call | solution.py:693
  52.7 1.0 copy.18.state_ref
  53.7 1.1 broadcast_shift-right-arithmetic_fusion
  54.8 0.8 copy.24
  55.6 0.9 broadcast_in_dim.12.edges_hbm
  56.5 32.1 %bucket.8 = (f32[32,400,128]{2,1,0:T(8,128)}, f32[8,400,128]{2,1,0:T(8,128)}, f32[400,128]{1,0:T(8,128)}) custom-call(s32[8,1,8704]{2,1,0:T(1,128)} %broadcast_in_dim.12.edges_hbm, s32[8]{0:T(128)} %slice_reduce_fusion.count_ref, s32[8,1,1024]{2,1,0:T(1,128)} %broadcast_in_dim.13.negs_hbm, s32[8,32,256]{2,1,0:T(8,128)} %bitcast.12, ...), custom_call_target="tpu_custom_call" | custom-call | tf_op jit(solution)/shard_map/bucket/pallas_call | solution.py:317
  89.2 83.8 %exchange.8 = (f32[4096,128]{1,0:T(8,128)}, f32[1024,1]{1,0:T(8,128)}, f32[128,512]{1,0:T(8,128)}, f32[128,1]{1,0:T(8,128)}, f32[1,128]{1,0:T(1,128)}, /*index=5*/bf16[32,400,128]{2,1,0:T(8,128)(2,1)}) custom-call(f32[32,400,128]{2,1,0:T(8,128)} %get-tuple-element.87.tail_ref, f32[8,400,128]{2,1,0:T(8,128)} %get-tuple-element.88.head_ref, ...), custom_call_target="tpu_custom_call" | custom-call | tf_op jit(solution)/shard_map/exchange/pallas_call | solution.py:541
  173.0 21.4 %bucket.9 = (f32[32,400,128]{2,1,0:T(8,128)}, f32[8,400,128]{2,1,0:T(8,128)}, f32[400,128]{1,0:T(8,128)}) custom-call(s32[8,1,8704]{2,1,0:T(1,128)} %broadcast_in_dim.12.edges_hbm, s32[8]{0:T(128)} %slice_reduce_fusion.count_ref, s32[8,1,1024]{2,1,0:T(1,128)} %broadcast_in_dim.13.negs_hbm, s32[8,32,256]{2,1,0:T(8,128)} %bitcast.13, ...), custom_call_target="tpu_custom_call" | custom-call | tf_op jit(solution)/shard_map/bucket/pallas_call | solution.py:317
  194.4 103.3 %exchange.9 = (f32[4096,128]{1,0:T(8,128)}, f32[1024,1]{1,0:T(8,128)}, f32[128,512]{1,0:T(8,128)}, f32[128,1]{1,0:T(8,128)}, f32[1,128]{1,0:T(1,128)}, /*index=5*/bf16[32,400,128]{2,1,0:T(8,128)(2,1)}) custom-call(f32[32,400,128]{2,1,0:T(8,128)} %get-tuple-element.93.tail_ref, f32[8,400,128]{2,1,0:T(8,128)} %get-tuple-element.94.head_ref, ...), custom_call_target="tpu_custom_call" | custom-call | tf_op jit(solution)/shard_map/exchange/pallas_call | solution.py:541
  297.7 32.6 %bucket.10 = (f32[32,400,128]{2,1,0:T(8,128)}, f32[8,400,128]{2,1,0:T(8,128)}, f32[400,128]{1,0:T(8,128)}) custom-call(s32[8,1,8704]{2,1,0:T(1,128)} %broadcast_in_dim.12.edges_hbm, s32[8]{0:T(128)} %slice_reduce_fusion.count_ref, s32[8,1,1024]{2,1,0:T(1,128)} %broadcast_in_dim.13.negs_hbm, s32[8,32,256]{2,1,0:T(8,128)} %bitcast.14, ...), custom_call_target="tpu_custom_call" | custom-call | tf_op jit(solution)/shard_map/bucket/pallas_call | solution.py:317
  330.4 97.9 %exchange.10 = (f32[4096,128]{1,0:T(8,128)}, f32[1024,1]{1,0:T(8,128)}, f32[128,512]{1,0:T(8,128)}, f32[128,1]{1,0:T(8,128)}, f32[1,128]{1,0:T(1,128)}, /*index=5*/bf16[32,400,128]{2,1,0:T(8,128)(2,1)}) custom-call(f32[32,400,128]{2,1,0:T(8,128)} %get-tuple-element.101.tail_ref, f32[8,400,128]{2,1,0:T(8,128)} %get-tuple-element.102.head_ref, ...), custom_call_target="tpu_custom_call" | custom-call | tf_op jit(solution)/shard_map/exchange/pallas_call | solution.py:541
  428.3 32.5 %bucket.11 = (f32[32,400,128]{2,1,0:T(8,128)}, f32[8,400,128]{2,1,0:T(8,128)}, f32[400,128]{1,0:T(8,128)}) custom-call(s32[8,1,8704]{2,1,0:T(1,128)} %broadcast_in_dim.12.edges_hbm, s32[8]{0:T(128)} %slice_reduce_fusion.count_ref, s32[8,1,1024]{2,1,0:T(1,128)} %broadcast_in_dim.13.negs_hbm, s32[8,32,256]{2,1,0:T(8,128)} %bitcast.15, ...), custom_call_target="tpu_custom_call" | custom-call | tf_op jit(solution)/shard_map/bucket/pallas_call | solution.py:317
  460.7 111.8 %exchange.11 = (f32[4096,128]{1,0:T(8,128)}, f32[1024,1]{1,0:T(8,128)}, f32[128,512]{1,0:T(8,128)}, f32[128,1]{1,0:T(8,128)}, f32[1,128]{1,0:T(1,128)}, /*index=5*/bf16[32,400,128]{2,1,0:T(8,128)(2,1)}) custom-call(f32[32,400,128]{2,1,0:T(8,128)} %get-tuple-element.109.tail_ref, f32[8,400,128]{2,1,0:T(8,128)} %get-tuple-element.110.head_ref, ...), custom_call_target="tpu_custom_call" | custom-call | tf_op jit(solution)/shard_map/exchange/pallas_call | solution.py:541
  572.5 38.0 %bucket.12 = (f32[32,400,128]{2,1,0:T(8,128)}, f32[8,400,128]{2,1,0:T(8,128)}, f32[400,128]{1,0:T(8,128)}) custom-call(s32[8,1,8704]{2,1,0:T(1,128)} %broadcast_in_dim.12.edges_hbm, s32[8]{0:T(128)} %slice_reduce_fusion.count_ref, s32[8,1,1024]{2,1,0:T(1,128)} %broadcast_in_dim.13.negs_hbm, s32[8,32,256]{2,1,0:T(8,128)} %bitcast.16, ...), custom_call_target="tpu_custom_call" | custom-call | tf_op jit(solution)/shard_map/bucket/pallas_call | solution.py:317
  610.5 102.8 %exchange.12 = (f32[4096,128]{1,0:T(8,128)}, f32[1024,1]{1,0:T(8,128)}, f32[128,512]{1,0:T(8,128)}, f32[128,1]{1,0:T(8,128)}, f32[1,128]{1,0:T(1,128)}, /*index=5*/bf16[32,400,128]{2,1,0:T(8,128)(2,1)}) custom-call(f32[32,400,128]{2,1,0:T(8,128)} %get-tuple-element.117.tail_ref, f32[8,400,128]{2,1,0:T(8,128)} %get-tuple-element.118.head_ref, ...), custom_call_target="tpu_custom_call" | custom-call | tf_op jit(solution)/shard_map/exchange/pallas_call | solution.py:541
  713.3 35.0 %bucket.13 = (f32[32,400,128]{2,1,0:T(8,128)}, f32[8,400,128]{2,1,0:T(8,128)}, f32[400,128]{1,0:T(8,128)}) custom-call(s32[8,1,8704]{2,1,0:T(1,128)} %broadcast_in_dim.12.edges_hbm, s32[8]{0:T(128)} %slice_reduce_fusion.count_ref, s32[8,1,1024]{2,1,0:T(1,128)} %broadcast_in_dim.13.negs_hbm, s32[8,32,256]{2,1,0:T(8,128)} %bitcast.17, ...), custom_call_target="tpu_custom_call" | custom-call | tf_op jit(solution)/shard_map/bucket/pallas_call | solution.py:317
  748.3 107.1 %exchange.13 = (f32[4096,128]{1,0:T(8,128)}, f32[1024,1]{1,0:T(8,128)}, f32[128,512]{1,0:T(8,128)}, f32[128,1]{1,0:T(8,128)}, f32[1,128]{1,0:T(1,128)}, /*index=5*/bf16[32,400,128]{2,1,0:T(8,128)(2,1)}) custom-call(f32[32,400,128]{2,1,0:T(8,128)} %get-tuple-element.125.tail_ref, f32[8,400,128]{2,1,0:T(8,128)} %get-tuple-element.126.head_ref, ...), custom_call_target="tpu_custom_call" | custom-call | tf_op jit(solution)/shard_map/exchange/pallas_call | solution.py:541
  855.4 24.2 %bucket.14 = (f32[32,400,128]{2,1,0:T(8,128)}, f32[8,400,128]{2,1,0:T(8,128)}, f32[400,128]{1,0:T(8,128)}) custom-call(s32[8,1,8704]{2,1,0:T(1,128)} %broadcast_in_dim.12.edges_hbm, s32[8]{0:T(128)} %slice_reduce_fusion.count_ref, s32[8,1,1024]{2,1,0:T(1,128)} %broadcast_in_dim.13.negs_hbm, s32[8,32,256]{2,1,0:T(8,128)} %bitcast.18, ...), custom_call_target="tpu_custom_call" | custom-call | tf_op jit(solution)/shard_map/bucket/pallas_call | solution.py:317
  879.6 105.8 %exchange.14 = (f32[4096,128]{1,0:T(8,128)}, f32[1024,1]{1,0:T(8,128)}, f32[128,512]{1,0:T(8,128)}, f32[128,1]{1,0:T(8,128)}, f32[1,128]{1,0:T(1,128)}, /*index=5*/bf16[32,400,128]{2,1,0:T(8,128)(2,1)}) custom-call(f32[32,400,128]{2,1,0:T(8,128)} %get-tuple-element.133.tail_ref, f32[8,400,128]{2,1,0:T(8,128)} %get-tuple-element.134.head_ref, ...), custom_call_target="tpu_custom_call" | custom-call | tf_op jit(solution)/shard_map/exchange/pallas_call | solution.py:541
  985.4 32.3 %bucket.15 = (f32[32,400,128]{2,1,0:T(8,128)}, f32[8,400,128]{2,1,0:T(8,128)}, f32[400,128]{1,0:T(8,128)}) custom-call(s32[8,1,8704]{2,1,0:T(1,128)} %broadcast_in_dim.12.edges_hbm, s32[8]{0:T(128)} %slice_reduce_fusion.count_ref, s32[8,1,1024]{2,1,0:T(1,128)} %broadcast_in_dim.13.negs_hbm, s32[8,32,256]{2,1,0:T(8,128)} %bitcast.19, ...), custom_call_target="tpu_custom_call" | custom-call | tf_op jit(solution)/shard_map/bucket/pallas_call | solution.py:317
  1017.8 147.1 %exchange.15 = (f32[32,416,128]{2,1,0:T(8,128)}, f32[128,512]{1,0:T(8,128)}, f32[1,128]{1,0:T(1,128)}) custom-call(f32[32,400,128]{2,1,0:T(8,128)} %get-tuple-element.141.tail_ref, f32[8,400,128]{2,1,0:T(8,128)} %get-tuple-element.142.head_ref, f32[400,128]{1,0:T(8,128)} %get-tuple-element.143.rel_grad_ref, f32[4096,128]{1,0:T(8,128)} %get-tuple-element.138.ent_ref, ...), custom_call_target="tpu_custom_call" | custom-call | tf_op jit(solution)/shard_map/exchange/pallas_call | solution.py:541
  1165.6 2.3 slice.7
  1168.1 0.7 reshape.18
  1168.8 21.3 %finish.1 = (f32[4096,400]{1,0:T(8,128)}, f32[107,400]{1,0:T(8,128)}) custom-call(f32[32,416,128]{2,1,0:T(8,128)} %get-tuple-element.146.wire_ref, f32[128,512]{1,0:T(8,128)} %get-tuple-element.147.rel_ref), custom_call_target="tpu_custom_call" | custom-call | tf_op jit(solution)/shard_map/finish/pallas_call | solution.py:718
  1190.1 8.6 copy.20
  1198.7 0.8 copy.21
  1199.6 0.7 dynamic-slice_reduce_fusion
  (30 shorter events, 3.6 us)
Async XLA Ops:
  7.2 46.5 %sort.9.cloned.1.call-start = ((), (), s32[]{:S(2)}) async-start(), calls=%async_computation | async-start | bytes 786464 | tf_op jit(solution)/shard_map/sort | solution.py:746
  8.0 44.0 %collective-permute-start = (f32[1024]{0:T(1024)S(1)}, f32[1024]{0:T(1024)S(1)}, u32[]{:S(2)}, u32[]{:S(2)}) collective-permute-start(f32[1024]{0:T(1024)S(1)} %dynamic_slice.10), channel_id=1, source_target_pairs={{0,1},{2,3},{4,5},{6,7},{8,9},{10,11},{12,13},{14,15},{17,16},{19,... | collective-permute-start | bytes 12296 | tf_op jit(solution)/shard_map/ppermute | solution.py:756
  34.4 16.9 %copy-start.1 = (s32[8,1024]{1,0:T(8,128)S(1)}, s32[8,1024]{1,0:T(8,128)}, u32[]{:S(2)}) copy-start(s32[8,1024]{1,0:T(8,128)} %get-tuple-element.83) | copy-start | bytes 98308
  1017.7 147.2 %copy-start.2 = (f32[1,128]{1,0:T(1,128)S(1)}, f32[1,128]{1,0:T(1,128)}, u32[]{:S(2)}) copy-start(f32[1,128]{1,0:T(1,128)} %get-tuple-element.150) | copy-start | bytes 1540
  1017.7 147.2 %copy-start.3 = (f32[1,128]{1,0:T(1,128)S(1)}, f32[1,128]{1,0:T(1,128)}, u32[]{:S(2)}) copy-start(f32[1,128]{1,0:T(1,128)} %get-tuple-element.151) | copy-start | bytes 1540
  1017.7 147.2 %copy-start.4 = (f32[1,128]{1,0:T(1,128)S(1)}, f32[1,128]{1,0:T(1,128)}, u32[]{:S(2)}) copy-start(f32[1,128]{1,0:T(1,128)} %get-tuple-element.152) | copy-start | bytes 1540
  1017.7 147.2 %copy-start.5 = (f32[1,128]{1,0:T(1,128)S(1)}, f32[1,128]{1,0:T(1,128)}, u32[]{:S(2)}) copy-start(f32[1,128]{1,0:T(1,128)} %get-tuple-element.153) | copy-start | bytes 1540
  1017.8 147.2 %copy-start.6 = (f32[1,128]{1,0:T(1,128)S(1)}, f32[1,128]{1,0:T(1,128)}, u32[]{:S(2)}) copy-start(f32[1,128]{1,0:T(1,128)} %get-tuple-element.154) | copy-start | bytes 1540
  1017.8 147.2 %copy-start.7 = (f32[1,128]{1,0:T(1,128)S(1)}, f32[1,128]{1,0:T(1,128)}, u32[]{:S(2)}) copy-start(f32[1,128]{1,0:T(1,128)} %get-tuple-element.155) | copy-start | bytes 1540
  1017.8 147.2 %copy-start.8 = (f32[1,128]{1,0:T(1,128)S(1)}, f32[1,128]{1,0:T(1,128)}, u32[]{:S(2)}) copy-start(f32[1,128]{1,0:T(1,128)} %get-tuple-element.156) | copy-start | bytes 1540
  1190.1 8.6 copy-start
Sparse Core Ops, SparseCore 0:
  22.9 20.1 sort.11.cloned.1.call-done
  (1 shorter events, 0.0 us)

commit v3 on v2

--- a/solution.py
+++ b/solution.py
@@ -15,9 +15,12 @@
 BLOCK = 256
 CHUNK = 128
 UNROLL = 128
+LAG = 2
+REL_HOPS = 6
 STRIP = 32
 REL_PAD = 128
 TILES = range(4)
+CORES = range(2)
 ROW_COL, ROW_ROW, COL_COL = (((1,), (0,)), ((1,), (1,)), ((0,), (0,)))
 F32 = jnp.float32
 BF16 = jnp.bfloat16
@@ -29,28 +32,17 @@
 
 
 def columns_to_tiles(x):
-    lane = lax.broadcasted_iota(jnp.int32, (x.shape[0], LANES), 1)
-    end = x.shape[1] - 3 * LANES
-    t0, t1, t2 = (x[:, band(t, LANES)] for t in TILES[:-1])
-    t3 = jnp.concatenate([x[:, 3 * LANES:], jnp.zeros((x.shape[0], LANES - end), x.dtype)], axis=1)
-    im = x.shape[1] // 2 - LANES
-    cut = LANES - im
-    b = jnp.where(lane < cut, pltpu.roll(t1, cut, 1), pltpu.roll(t2, cut, 1))
-    c = jnp.where(lane < HALF, t1, jnp.where(lane < LANES - LEFT, pltpu.roll(t2, LANES - LEFT, 1), pltpu.roll(t3, LANES - LEFT, 1)))
-    low, high = pltpu.roll(t1, HALF, 1), pltpu.roll(t3, cut, 1)
-    d = jnp.where(lane < LEFT, low, jnp.where((lane >= HALF) & (lane < HALF + LEFT), high, 0.0))
-    return [t0, b, c, d]
-
-
-def tiles_to_columns(tiles, width):
-    a, b, c, d = tiles
-    lane = lax.broadcasted_iota(jnp.int32, a.shape, 1)
-    im = width // 2 - LANES
-    b, c, low, high = pltpu.roll(b, im, 1), pltpu.roll(c, LEFT, 1), pltpu.roll(d, HALF, 1), pltpu.roll(d, im, 1)
-    t1 = jnp.where(lane < HALF, tiles[2], jnp.where(lane < im, low, b))
-    t2 = jnp.where(lane < im, b, c)
-    t3 = jnp.where(lane < LEFT, c, high)
-    return jnp.concatenate([a, t1, t2, t3[:, :width - 3 * LANES]], axis=1)
+    half = x.shape[0] // 2
+    a, c, d = slice(0, LANES), slice(LANES, LANES + HALF), slice(LANES + HALF, half)
+    re, im = x[:half], x[half:]
+    zero = jnp.zeros((HALF - LEFT, x.shape[1]), x.dtype)
+    return [t.T for t in (re[a], im[a], jnp.concatenate([re[c], im[c]], axis=0), jnp.concatenate([re[d], zero, im[d], zero], axis=0))]
+
+
+def tiles_to_columns(tiles):
+    a, b, c, d = (t.T for t in tiles)
+    high = slice(HALF, HALF + LEFT)
+    return jnp.concatenate([a, c[:HALF], d[:LEFT], b, c[HALF:], d[high]], axis=0)
 
 
 def each_row(count, body):
@@ -379,7 +371,7 @@
 
     other_core = at(y, x, 1 - core)
     other_y = at(2 * top + 1 - bot, x, core)
-    rel_peers = (other_core, other_y, at(3 - y, x, core), at(y, x + 1 - 2 * (x % 2), core), at(y, x_size - 1 - x, core))
+    rel_peers = (other_core, other_y, at(3 - y, x, core), at(y, x + 1 - 2 * (x % 2), core), at(y, x_size - 1 - x, core), other_core)
     grad_to = place((mine + step) % groups, turned(step), core)
     grad_from = place((mine + groups - step) % groups, turned(step), core)
     nxt = step + 1
@@ -406,7 +398,7 @@
 
     shards = [(1 - keep, k) for k in range(chunks)] + [(keep, k) for k in range(chunks)]
     loads, cores = [], []
-    rel_copies = [start(remote(rel_grad_ref, rel_from.at[0], rel_send.at[0], rel_recv.at[0], rel_peers[0]))]
+    rel_copies = [start(remote(rel_grad_ref.at[1 - core], rel_from.at[0], rel_send.at[0], rel_recv.at[0], rel_peers[0]))]
     for n, (low, k) in enumerate(shards):
         cores.append(start(remote(tail_ref.at[(low * 2 + 1 - core) * chunks + k], from_core.at[n], core_send.at[n], core_recv.at[n], other_core)))
         load = pltpu.make_async_copy(tail_ref.at[(low * 2 + core) * chunks + k], own.at[n], own_sem.at[n])
@@ -415,23 +407,21 @@
 
     def rel_step(n):
         rel_copies[n].wait_recv()
-        rel_sum[n] = (rel_grad_ref[...] if n == 0 else rel_sum[n - 1]) + rel_from[n]
-        if n + 1 < len(rel_peers):
-            rel_copies.append(start(remote(rel_sum.at[n], rel_from.at[n + 1], rel_send.at[n + 1], rel_recv.at[n + 1], rel_peers[n + 1])))
-
-    rel_step(0)
+        rel_sum[n] = (rel_grad_ref[core] if n == 0 else rel_sum[n - 1]) + rel_from[n]
+        rel_copies.append(start(remote(rel_sum.at[n], rel_from.at[n + 1], rel_send.at[n + 1], rel_recv.at[n + 1], rel_peers[n + 1])))
+
     ys = []
     for k in range(chunks):
         loads[k].wait()
         cores[k].wait_recv()
         own[k] = own[k] + from_core[k]
         ys.append(start(remote(own.at[k], from_y.at[k], y_send.at[k], y_recv.at[k], other_y)))
-    rel_step(1)
+        if k == 1:
+            rel_step(0)
     for k in range(chunks, 2 * chunks):
         loads[k].wait()
         cores[k].wait_recv()
         own[k] = own[k] + from_core[k]
-    rel_step(2)
     gs, outs, forwards, crosses = [], [], [], []
 
     def stage_group(k):
@@ -439,6 +429,27 @@
         own[chunks + k] = own[chunks + k] + from_y[k]
         if step:
             gs.append(start(remote(own.at[chunks + k], from_group.at[k], group_send.at[k], group_recv.at[k], grad_to)))
+
+    def cross_copy(k):
+        return remote(send_buf.at[k], ent_wire.at[(bot * 2 + core) * chunks + k], out_send.at[2 * chunks + k], out_recv.at[(bot * 2 + core) * chunks + k], other_core)
+
+    turn = (y + 4 - 2 * core) % 4
+    near = 1 - turn % 2
+    back = jnp.where((turn == 1) | (turn == 2), 0, 1)
+    onward = at((y + 1 + 2 * back) % 4, x, core)
+
+    def landed(low, c, k):
+        slot = (low * 2 + c) * chunks + k
+        remote(ent_wire.at[slot], ent_wire.at[slot], out_send.at[0], out_recv.at[slot], other_core).wait_recv()
+
+    def stage_relay(k):
+        if k % 2 == 0:
+            return
+        for c in CORES:
+            landed(near, c, k - 1)
+            landed(near, c, k)
+            slot = (near * 2 + c) * chunks + k - 1 + back
+            start(remote(ent_wire.at[slot], ent_wire.at[slot], out_send.at[(3 + c) * chunks + k], out_recv.at[slot], onward))
 
     def stage_update(k):
         if step:
@@ -462,8 +473,8 @@
             offset += piece.shape[0]
         slot = (bot * 2 + core) * chunks + k
         if last:
-            for turn in range(1, 4):
-                start(remote(send_buf.at[k], ent_wire.at[slot], out_send.at[turn * chunks + k], out_recv.at[slot], at((y + turn) % 4, x, top)))
+            for n, turn in enumerate((1, 3)):
+                start(remote(send_buf.at[k], ent_wire.at[slot], out_send.at[n * chunks + k], out_recv.at[slot], at((y + turn) % 4, x, top)))
 
             @pl.when(core == top)
             def _():
@@ -471,7 +482,7 @@
 
             @pl.when(core != top)
             def _():
-                remote(send_buf.at[k], ent_wire.at[slot], out_send.at[k], out_recv.at[slot], other_core).start()
+                cross_copy(k).start()
         else:
             outs.append(start(remote(send_buf.at[k], table.at[slot], out_send.at[k], out_recv.at[k], table_to)))
 
@@ -480,27 +491,26 @@
         return start(remote(table.at[slot], table.at[slot], out_send.at[n * chunks + k], out_recv.at[n * chunks + k], peer))
 
     def stage_forward(k):
-        if last:
-            return
         outs[k].wait_recv()
         forwards.append(forward(1, turned(nxt), k, other_y))
         crosses.append(forward(2, turned(nxt), k, other_core))
 
     def stage_cross(k):
-        if last:
-            return
         forwards[k].wait_recv()
         crosses.append(forward(3, 1 - turned(nxt), k, other_core))
 
-    stages = (stage_group, stage_update, stage_forward, stage_cross)
-    for tick in range(chunks + len(stages) - 1):
-        for lag, stage in enumerate(stages):
-            if 0 <= tick - lag < chunks:
-                stage(tick - lag)
-        if tick in (0, 1):
-            rel_step(3 + tick)
-
-    summed = rel_sum[len(rel_peers) - 1]
+    stages = (stage_group, stage_update, stage_relay) if last else (stage_group, stage_update, stage_forward, stage_cross)
+    rel_steps = len(rel_peers) - 1
+    for tick in range(chunks + LAG * (len(stages) - 1)):
+        for n, stage in enumerate(stages):
+            if 0 <= tick - LAG * n < chunks:
+                stage(tick - LAG * n)
+        if tick % 2 == 1 and tick < 2 * rel_steps - 1:
+            rel_step(tick // 2 + 1)
+
+    rel_copies[rel_steps].wait_recv()
+    halves = rel_sum[rel_steps - 1], rel_from[rel_steps]
+    summed = jnp.concatenate([jnp.where(core == n, halves[0], halves[1]) for n in CORES], axis=0)
     rel_grad = [summed[band(t, REL_PAD)] for t in TILES[:-1]] + [jnp.concatenate(unfold_last(summed[3 * REL_PAD:]), axis=0)]
     loss_out[...] = rel_grad[0][REL_PAD - 1:, :]
     row = lax.broadcasted_iota(jnp.int32, (REL_PAD, LANES), 0)
@@ -512,13 +522,14 @@
         rel_state_out[...] = rel_state
 
     if last:
-        for slot in range(4 * chunks):
-            remote(ent_wire.at[slot], ent_wire.at[slot], out_send.at[0], out_recv.at[slot], other_core).wait_recv()
+        for c in CORES:
+            for k in range(chunks):
+                landed(1 - near, c, k)
 
         @pl.when(core != top)
         def _():
             for k in range(chunks):
-                remote(send_buf.at[k], send_buf.at[k], out_send.at[k], out_recv.at[k], other_core).wait_send()
+                cross_copy(k).wait_send()
     else:
         for copy in crosses:
             copy.wait_recv()
@@ -529,6 +540,7 @@
 def exchange_call(step, groups, emb_width, tail, head, rel_grad, ent, state, rel, rel_state):
     vmem, hbm = pl.BlockSpec(memory_space=pltpu.VMEM), pl.BlockSpec(memory_space=pl.ANY)
     chunks = head.shape[0]
+    rel_grad = rel_grad.reshape(2, -1, LANES)
     wire = wire_rows(CHUNK)
     last = step == groups - 1
     like = lambda x: jax.ShapeDtypeStruct(x.shape, x.dtype)
@@ -546,10 +558,10 @@
         scratch_shapes=[
             pltpu.VMEM((2 * chunks, wire, LANES), F32), pltpu.VMEM((2 * chunks, wire, LANES), F32),
             pltpu.VMEM((chunks, wire, LANES), F32), pltpu.VMEM((chunks, wire, LANES), F32),
-            pltpu.VMEM((5, *rel_grad.shape), F32), pltpu.VMEM((5, *rel_grad.shape), F32),
+            pltpu.VMEM((REL_HOPS - 1, *rel_grad.shape[1:]), F32), pltpu.VMEM((REL_HOPS, *rel_grad.shape[1:]), F32),
             pltpu.VMEM((chunks, out_wire, LANES), out_type),
             sems(2 * chunks), sems(2 * chunks), sems(2 * chunks), sems(chunks), sems(chunks), sems(chunks), sems(chunks),
-            sems(5), sems(5), sems(4 * chunks), sems(4 * chunks),
+            sems(REL_HOPS), sems(REL_HOPS), sems(5 * chunks), sems(4 * chunks),
         ],
         compiler_params=pltpu.CompilerParams(vmem_limit_bytes=VMEM_LIMIT, collective_id=step, has_side_effects=True),
         name='exchange',
@@ -624,13 +636,11 @@
     chunks, chunk = table.shape[0], CHUNK
     shard = chunks // 4
     entry([other_core])
-    rel_rows = rel_ref.shape[0]
-    pad = jnp.zeros((REL_PAD - rel_rows, rel_ref.shape[1]), F32)
-    for t, tile in enumerate(columns_to_tiles(jnp.concatenate([rel_ref[...], pad], axis=0))):
+    for t, tile in enumerate(columns_to_tiles(rel_ref[...])):
         rel_out[:, band(t, LANES)] = tile
 
     def load(n):
-        return pltpu.make_async_copy(ent_hbm.at[pl.ds(pl.multiple_of(n * chunk, chunk), chunk), :], rows_buf.at[n % 4], load_sem.at[n % 4])
+        return pltpu.make_async_copy(ent_hbm.at[:, pl.ds(pl.multiple_of(n * chunk, chunk), chunk)], rows_buf.at[n % 4], load_sem.at[n % 4])
 
     def table_copy(q):
         part = table.at[pl.ds(q * shard, shard)]
@@ -687,7 +697,7 @@
 
 def rows_call(ent, rel):
     vmem, hbm = pl.BlockSpec(memory_space=pltpu.VMEM), pl.BlockSpec(memory_space=pl.ANY)
-    rows, width = ent.shape
+    width, rows = ent.shape
     chunks = rows // CHUNK
     dma = pltpu.SemaphoreType.DMA
     return pl.pallas_call(
@@ -695,32 +705,35 @@
         out_shape=(jax.ShapeDtypeStruct((chunks, wire_rows(CHUNK), LANES), BF16), jax.ShapeDtypeStruct((rows, LANES), F32), jax.ShapeDtypeStruct((REL_PAD, 4 * LANES), F32)),
         in_specs=[hbm, vmem],
         out_specs=(vmem,) * 3,
-        scratch_shapes=[pltpu.VMEM((4, CHUNK, width), F32), pltpu.VMEM((rows, LANES), F32), dma((4,)), dma((4,)), dma((4,)), dma, dma],
+        scratch_shapes=[pltpu.VMEM((4, width, CHUNK), F32), pltpu.VMEM((rows, LANES), F32), dma((4,)), dma((4,)), dma((4,)), dma, dma],
         compiler_params=pltpu.CompilerParams(collective_id=21, has_side_effects=True),
         cost_estimate=pl.CostEstimate(flops=10**9, bytes_accessed=2 * 10**7, transcendentals=0),
         name='setup_rows',
     )(ent, rel)
 
 
-def finish_kernel(width, rel_rows, wire_ref, rel_ref, ent_out, rel_out):
+def finish_kernel(wire_ref, rel_ref, ent_out, rel_out):
     chunk = CHUNK
-    tiles = [wire_ref[0, band(t, chunk), :] for t in TILES[:-1]]
-    tiles.append(jnp.concatenate(unfold_last(wire_ref[0, 3 * chunk:wire_rows(chunk), :]), axis=0))
-    ent_out[...] = tiles_to_columns(tiles, width)
+    for n in range(wire_ref.shape[0]):
+        tiles = [wire_ref[n, band(t, chunk), :] for t in TILES[:-1]]
+        tiles.append(jnp.concatenate(unfold_last(wire_ref[n, 3 * chunk:wire_rows(chunk), :]), axis=0))
+        ent_out[:, band(n, chunk)] = tiles_to_columns(tiles)
 
     @pl.when(pl.program_id(0) == 0)
     def _():
-        rel_out[...] = tiles_to_columns(tiles_of(rel_ref[...]), width)[:rel_rows]
-
-
-def finish_call(wire, rel, width, rel_rows):
+        rel_out[...] = tiles_to_columns(tiles_of(rel_ref[...]))
+
+
+def finish_call(wire, rel, width):
     chunks = wire.shape[0]
+    size = chunks // 8
+    whole = lambda n: (0, 0)
     return pl.pallas_call(
-        functools.partial(finish_kernel, width, rel_rows),
-        out_shape=(jax.ShapeDtypeStruct((chunks * CHUNK, width), F32), jax.ShapeDtypeStruct((rel_rows, width), F32)),
-        grid=(chunks,),
-        in_specs=[pl.BlockSpec((1, *wire.shape[1:]), lambda n: (n, 0, 0)), pl.BlockSpec(rel.shape, lambda n: (0, 0))],
-        out_specs=(pl.BlockSpec((CHUNK, width), lambda n: (n, 0)), pl.BlockSpec((rel_rows, width), lambda n: (0, 0))),
+        finish_kernel,
+        out_shape=(jax.ShapeDtypeStruct((width, chunks * CHUNK), F32), jax.ShapeDtypeStruct((width, REL_PAD), F32)),
+        grid=(chunks // size,),
+        in_specs=[pl.BlockSpec((size, *wire.shape[1:]), lambda n: (n, 0, 0)), pl.BlockSpec(rel.shape, whole)],
+        out_specs=(pl.BlockSpec((width, size * CHUNK), lambda n: (0, n)), pl.BlockSpec((width, REL_PAD), whole)),
         name='finish',
     )(wire, rel)
 
@@ -750,7 +763,7 @@
         words = (row_address(keys & (shard - 1)) << (tail_bits + 2)) | row_address((keys >> head_bits) & (part_rows - 1))
         words = jnp.pad(words, ((0, 0), (BLOCK, BLOCK)))[:, None]
 
-        table, ent_now, rel_now = rows_call(ent_table, rel_table)
+        table, ent_now, rel_now = rows_call(ent_table.T, jnp.pad(rel_table.T, ((0, 0), (0, REL_PAD - rel_rows))))
         to_core = lambda c: lax.dynamic_slice_in_dim(ent_state, (2 * bot + c) * shard, shard)
         away = [(d * groups + 2 * (n // 2) + d // 2, d * groups + 2 * (n // 2) + 1 - d // 2) for d in range(data_reps) for n in range(0, groups, 2)]
         state_now = jnp.where(core == top, to_core(core), lax.ppermute(to_core(1 - core), ('data', 'ent'), away))[:, None]
@@ -764,10 +777,10 @@
             else:
                 wire, rel_now, loss = out
             losses.append(loss)
-        ent_out, rel_out = finish_call(wire, rel_now, emb_width, rel_rows)
+        ent_out, rel_out = finish_call(wire, rel_now, emb_width)
         state_out = wire[:, wire_rows(CHUNK):, :HALF:LEFT].transpose(0, 2, 1).reshape(part_rows)
         loss_rows = jnp.concatenate(losses, axis=0) / bucket_edges
         bucket_loss = lax.dynamic_slice_in_dim(loss_rows, ent, 1, axis=1).reshape(1, groups)
-        return ent_out, state_out, rel_out, bucket_loss
+        return ent_out.T, state_out, rel_out[:, :rel_rows].T, bucket_loss
 
     return jax.shard_map(device_fn, mesh=mesh, in_specs=(row_spec, P(('sweep', 'ent')), P('sweep', None), edge_spec, edge_spec, edge_spec, edge_spec, P(('sweep', 'ent'), None, None)), out_specs=(row_spec, P(('sweep', 'ent')), P('sweep', None), row_spec), check_vma=False)

time: 1210 us -> 1060 us (0.88)
  Pallas kernels: 1160 us -> 1030 us
  local copies, waits for them, and re-layouts: 30.4 us -> 13.9 us
    pallas_call x8, Pallas kernels: 860 us -> 742 us  [exchange_call(): pl.pallas_call(functools.partial(exchange_kernel, (step, groups, chunks,...]
    unnamed x24 -> x18, local copies, waits for them, and re-layouts: 20.6 us -> 0.87 us
  transfers between devices with their start and end apart: 1 -> 1, of which waited for: 0 -> 0; matrix products, arithmetic and copies ran while one was open for 1% -> 0% of each run, Pallas kernels for 3% -> 3%
where the time goes in v3:
time: 1060 us
  Pallas kernels  1030 us (97%)
  between operations  14.6 us (1%)
  local copies, waits for them, and re-layouts  13.9 us (1%)
    pallas_call x8, Pallas kernels, exchange_call(): pl.pallas_call(functools.partial(exchange_kernel, (step, groups, chunks,...  742 us
    pallas_call x8, Pallas kernels, bucket_call(): pl.pallas_call(functools.partial(bucket_kernel, (step, tail_bits)), out_s...  249 us
  transfers between devices with their start and end apart: 1, of which 0 were waited for; matrix products, arithmetic and copies ran while one was open for 0% of the time, Pallas kernels for 3%

profile of v3, /device:TPU:97, one launch (start us, length us, event | category | flops | bytes accessed | tf_op | source)
XLA Modules:
  0.0 1061.6 jit_solution(17022034266521455048)
XLA Ops:
  7.3 0.7 dynamic_slice.10
  8.0 1.3 collective-permute-start
  9.3 13.4 %setup_index.1 = (s32[8,8192]{1,0:T(8,128)}, s32[8,128]{1,0:T(8,128)}, s32[8,1024]{1,0:T(8,128)}) custom-call(s32[8,2048]{1,0:T(8,128)} %bitcast.45, s32[8,2048]{1,0:T(8,128)} %bitcast.46, s32[8,2048]{1,0:T(8,128)} %bitcast.47, s32[8,2048]{1,0:T(8,128)} %bitcast.48, s32[8,1024]{1,0:T(8,128)} %bitcast.49), custom_call_target="tpu_custom_call" | custom-call | tf_op jit(solution)/shard_map/setup_index/pallas_call | solution.py:621
  22.8 1.3 slice_reduce_fusion.count_ref
  24.1 1.6 pad.9.rel_ref
  25.7 16.6 %setup_rows.1 = (bf16[32,400,128]{2,1,0:T(8,128)(2,1)}, f32[4096,128]{1,0:T(8,128)}, f32[128,512]{1,0:T(8,128)}) custom-call(f32[400,4096]{1,0:T(8,128)} %bitcast.33, f32[400,128]{1,0:T(8,128)} %pad.9.rel_ref), custom_call_target="tpu_custom_call" | custom-call | flops 1000000000 | bytes 20000000 | tf_op jit(solution)/shard_map/setup_rows/pallas_call | solution.py:703
  43.0 0.7 dynamic-slice_select_fusion
  43.7 1.0 copy.12.state_ref
  44.7 1.1 broadcast_shift-right-arithmetic_fusion
  45.8 0.8 copy.16
  46.6 0.9 broadcast_in_dim.12.edges_hbm
  47.5 32.3 %bucket.8 = (f32[32,400,128]{2,1,0:T(8,128)}, f32[8,400,128]{2,1,0:T(8,128)}, f32[400,128]{1,0:T(8,128)}) custom-call(s32[8,1,8704]{2,1,0:T(1,128)} %broadcast_in_dim.12.edges_hbm, s32[8]{0:T(128)} %slice_reduce_fusion.count_ref, s32[8,1,1024]{2,1,0:T(1,128)} %broadcast_in_dim.13.negs_hbm, s32[8,32,256]{2,1,0:T(8,128)} %bitcast.25, ...), custom_call_target="tpu_custom_call" | custom-call | tf_op jit(solution)/shard_map/bucket/pallas_call | solution.py:309
  80.4 80.6 %exchange.8 = (f32[4096,128]{1,0:T(8,128)}, f32[1024,1]{1,0:T(8,128)}, f32[128,512]{1,0:T(8,128)}, f32[128,1]{1,0:T(8,128)}, f32[1,128]{1,0:T(1,128)}, /*index=5*/bf16[32,400,128]{2,1,0:T(8,128)(2,1)}) custom-call(f32[32,400,128]{2,1,0:T(8,128)} %get-tuple-element.87.tail_ref, f32[8,400,128]{2,1,0:T(8,128)} %get-tuple-element.88.head_ref, ...), custom_call_target="tpu_custom_call" | custom-call | tf_op jit(solution)/shard_map/exchange/pallas_call | solution.py:553
  161.0 27.1 %bucket.9 = (f32[32,400,128]{2,1,0:T(8,128)}, f32[8,400,128]{2,1,0:T(8,128)}, f32[400,128]{1,0:T(8,128)}) custom-call(s32[8,1,8704]{2,1,0:T(1,128)} %broadcast_in_dim.12.edges_hbm, s32[8]{0:T(128)} %slice_reduce_fusion.count_ref, s32[8,1,1024]{2,1,0:T(1,128)} %broadcast_in_dim.13.negs_hbm, s32[8,32,256]{2,1,0:T(8,128)} %bitcast.26, ...), custom_call_target="tpu_custom_call" | custom-call | tf_op jit(solution)/shard_map/bucket/pallas_call | solution.py:309
  188.1 83.4 %exchange.9 = (f32[4096,128]{1,0:T(8,128)}, f32[1024,1]{1,0:T(8,128)}, f32[128,512]{1,0:T(8,128)}, f32[128,1]{1,0:T(8,128)}, f32[1,128]{1,0:T(1,128)}, /*index=5*/bf16[32,400,128]{2,1,0:T(8,128)(2,1)}) custom-call(f32[32,400,128]{2,1,0:T(8,128)} %get-tuple-element.93.tail_ref, f32[8,400,128]{2,1,0:T(8,128)} %get-tuple-element.94.head_ref, ...), custom_call_target="tpu_custom_call" | custom-call | tf_op jit(solution)/shard_map/exchange/pallas_call | solution.py:553
  271.5 29.7 %bucket.10 = (f32[32,400,128]{2,1,0:T(8,128)}, f32[8,400,128]{2,1,0:T(8,128)}, f32[400,128]{1,0:T(8,128)}) custom-call(s32[8,1,8704]{2,1,0:T(1,128)} %broadcast_in_dim.12.edges_hbm, s32[8]{0:T(128)} %slice_reduce_fusion.count_ref, s32[8,1,1024]{2,1,0:T(1,128)} %broadcast_in_dim.13.negs_hbm, s32[8,32,256]{2,1,0:T(8,128)} %bitcast.27, ...), custom_call_target="tpu_custom_call" | custom-call | tf_op jit(solution)/shard_map/bucket/pallas_call | solution.py:309
  301.2 95.1 %exchange.10 = (f32[4096,128]{1,0:T(8,128)}, f32[1024,1]{1,0:T(8,128)}, f32[128,512]{1,0:T(8,128)}, f32[128,1]{1,0:T(8,128)}, f32[1,128]{1,0:T(1,128)}, /*index=5*/bf16[32,400,128]{2,1,0:T(8,128)(2,1)}) custom-call(f32[32,400,128]{2,1,0:T(8,128)} %get-tuple-element.101.tail_ref, f32[8,400,128]{2,1,0:T(8,128)} %get-tuple-element.102.head_ref, ...), custom_call_target="tpu_custom_call" | custom-call | tf_op jit(solution)/shard_map/exchange/pallas_call | solution.py:553
  396.4 32.5 %bucket.11 = (f32[32,400,128]{2,1,0:T(8,128)}, f32[8,400,128]{2,1,0:T(8,128)}, f32[400,128]{1,0:T(8,128)}) custom-call(s32[8,1,8704]{2,1,0:T(1,128)} %broadcast_in_dim.12.edges_hbm, s32[8]{0:T(128)} %slice_reduce_fusion.count_ref, s32[8,1,1024]{2,1,0:T(1,128)} %broadcast_in_dim.13.negs_hbm, s32[8,32,256]{2,1,0:T(8,128)} %bitcast.28, ...), custom_call_target="tpu_custom_call" | custom-call | tf_op jit(solution)/shard_map/bucket/pallas_call | solution.py:309
  428.9 97.3 %exchange.11 = (f32[4096,128]{1,0:T(8,128)}, f32[1024,1]{1,0:T(8,128)}, f32[128,512]{1,0:T(8,128)}, f32[128,1]{1,0:T(8,128)}, f32[1,128]{1,0:T(1,128)}, /*index=5*/bf16[32,400,128]{2,1,0:T(8,128)(2,1)}) custom-call(f32[32,400,128]{2,1,0:T(8,128)} %get-tuple-element.109.tail_ref, f32[8,400,128]{2,1,0:T(8,128)} %get-tuple-element.110.head_ref, ...), custom_call_target="tpu_custom_call" | custom-call | tf_op jit(solution)/shard_map/exchange/pallas_call | solution.py:553
  526.2 32.8 %bucket.12 = (f32[32,400,128]{2,1,0:T(8,128)}, f32[8,400,128]{2,1,0:T(8,128)}, f32[400,128]{1,0:T(8,128)}) custom-call(s32[8,1,8704]{2,1,0:T(1,128)} %broadcast_in_dim.12.edges_hbm, s32[8]{0:T(128)} %slice_reduce_fusion.count_ref, s32[8,1,1024]{2,1,0:T(1,128)} %broadcast_in_dim.13.negs_hbm, s32[8,32,256]{2,1,0:T(8,128)} %bitcast.29, ...), custom_call_target="tpu_custom_call" | custom-call | tf_op jit(solution)/shard_map/bucket/pallas_call | solution.py:309
  558.9 99.4 %exchange.12 = (f32[4096,128]{1,0:T(8,128)}, f32[1024,1]{1,0:T(8,128)}, f32[128,512]{1,0:T(8,128)}, f32[128,1]{1,0:T(8,128)}, f32[1,128]{1,0:T(1,128)}, /*index=5*/bf16[32,400,128]{2,1,0:T(8,128)(2,1)}) custom-call(f32[32,400,128]{2,1,0:T(8,128)} %get-tuple-element.117.tail_ref, f32[8,400,128]{2,1,0:T(8,128)} %get-tuple-element.118.head_ref, ...), custom_call_target="tpu_custom_call" | custom-call | tf_op jit(solution)/shard_map/exchange/pallas_call | solution.py:553
  658.4 37.8 %bucket.13 = (f32[32,400,128]{2,1,0:T(8,128)}, f32[8,400,128]{2,1,0:T(8,128)}, f32[400,128]{1,0:T(8,128)}) custom-call(s32[8,1,8704]{2,1,0:T(1,128)} %broadcast_in_dim.12.edges_hbm, s32[8]{0:T(128)} %slice_reduce_fusion.count_ref, s32[8,1,1024]{2,1,0:T(1,128)} %broadcast_in_dim.13.negs_hbm, s32[8,32,256]{2,1,0:T(8,128)} %bitcast.30, ...), custom_call_target="tpu_custom_call" | custom-call | tf_op jit(solution)/shard_map/bucket/pallas_call | solution.py:309
  696.2 80.1 %exchange.13 = (f32[4096,128]{1,0:T(8,128)}, f32[1024,1]{1,0:T(8,128)}, f32[128,512]{1,0:T(8,128)}, f32[128,1]{1,0:T(8,128)}, f32[1,128]{1,0:T(1,128)}, /*index=5*/bf16[32,400,128]{2,1,0:T(8,128)(2,1)}) custom-call(f32[32,400,128]{2,1,0:T(8,128)} %get-tuple-element.125.tail_ref, f32[8,400,128]{2,1,0:T(8,128)} %get-tuple-element.126.head_ref, ...), custom_call_target="tpu_custom_call" | custom-call | tf_op jit(solution)/shard_map/exchange/pallas_call | solution.py:553
  776.3 26.9 %bucket.14 = (f32[32,400,128]{2,1,0:T(8,128)}, f32[8,400,128]{2,1,0:T(8,128)}, f32[400,128]{1,0:T(8,128)}) custom-call(s32[8,1,8704]{2,1,0:T(1,128)} %broadcast_in_dim.12.edges_hbm, s32[8]{0:T(128)} %slice_reduce_fusion.count_ref, s32[8,1,1024]{2,1,0:T(1,128)} %broadcast_in_dim.13.negs_hbm, s32[8,32,256]{2,1,0:T(8,128)} %bitcast.31, ...), custom_call_target="tpu_custom_call" | custom-call | tf_op jit(solution)/shard_map/bucket/pallas_call | solution.py:309
  803.2 83.0 %exchange.14 = (f32[4096,128]{1,0:T(8,128)}, f32[1024,1]{1,0:T(8,128)}, f32[128,512]{1,0:T(8,128)}, f32[128,1]{1,0:T(8,128)}, f32[1,128]{1,0:T(1,128)}, /*index=5*/bf16[32,400,128]{2,1,0:T(8,128)(2,1)}) custom-call(f32[32,400,128]{2,1,0:T(8,128)} %get-tuple-element.133.tail_ref, f32[8,400,128]{2,1,0:T(8,128)} %get-tuple-element.134.head_ref, ...), custom_call_target="tpu_custom_call" | custom-call | tf_op jit(solution)/shard_map/exchange/pallas_call | solution.py:553
  886.2 29.5 %bucket.15 = (f32[32,400,128]{2,1,0:T(8,128)}, f32[8,400,128]{2,1,0:T(8,128)}, f32[400,128]{1,0:T(8,128)}) custom-call(s32[8,1,8704]{2,1,0:T(1,128)} %broadcast_in_dim.12.edges_hbm, s32[8]{0:T(128)} %slice_reduce_fusion.count_ref, s32[8,1,1024]{2,1,0:T(1,128)} %broadcast_in_dim.13.negs_hbm, s32[8,32,256]{2,1,0:T(8,128)} %bitcast.32, ...), custom_call_target="tpu_custom_call" | custom-call | tf_op jit(solution)/shard_map/bucket/pallas_call | solution.py:309
  915.8 123.0 %exchange.15 = (f32[32,416,128]{2,1,0:T(8,128)}, f32[128,512]{1,0:T(8,128)}, f32[1,128]{1,0:T(1,128)}) custom-call(f32[32,400,128]{2,1,0:T(8,128)} %get-tuple-element.141.tail_ref, f32[8,400,128]{2,1,0:T(8,128)} %get-tuple-element.142.head_ref, f32[2,200,128]{2,1,0:T(8,128)} %bitcast.37, f32[4096,128]{1,0:T(8,128)} %get-tuple-element.138.ent_ref, ...), custom_call_target="tpu_custom_call" | custom-call | tf_op jit(solution)/shard_map/exchange/pallas_call | solution.py:553
  1039.5 2.3 slice.10
  1041.8 9.6 finish.1
  1051.5 0.7 reshape.50
  1052.2 1.6 slice_bitcast_fusion
  1053.8 0.7 dynamic-slice_reduce_fusion
  (26 shorter events, 2.2 us)
Async XLA Ops:
  7.2 37.5 %sort.9.cloned.1.call-start = ((), (), s32[]{:S(2)}) async-start(), calls=%async_computation | async-start | bytes 786464 | tf_op jit(solution)/shard_map/sort | solution.py:759
  8.0 35.0 %collective-permute-start = (f32[1024]{0:T(1024)S(1)}, f32[1024]{0:T(1024)S(1)}, u32[]{:S(2)}, u32[]{:S(2)}) collective-permute-start(f32[1024]{0:T(1024)S(1)} %dynamic_slice.10), channel_id=1, source_target_pairs={{0,1},{2,3},{4,5},{6,7},{8,9},{10,11},{12,13},{14,15},{17,16},{19,... | collective-permute-start | bytes 12296 | tf_op jit(solution)/shard_map/ppermute | solution.py:769
  25.7 16.7 %copy-start = (s32[8,1024]{1,0:T(8,128)S(1)}, s32[8,1024]{1,0:T(8,128)}, u32[]{:S(2)}) copy-start(s32[8,1024]{1,0:T(8,128)} %get-tuple-element.83) | copy-start | bytes 98308
  915.7 123.0 %copy-start.1 = (f32[1,128]{1,0:T(1,128)S(1)}, f32[1,128]{1,0:T(1,128)}, u32[]{:S(2)}) copy-start(f32[1,128]{1,0:T(1,128)} %get-tuple-element.150) | copy-start | bytes 1540
  915.7 123.0 %copy-start.2 = (f32[1,128]{1,0:T(1,128)S(1)}, f32[1,128]{1,0:T(1,128)}, u32[]{:S(2)}) copy-start(f32[1,128]{1,0:T(1,128)} %get-tuple-element.151) | copy-start | bytes 1540
  915.7 123.0 %copy-start.3 = (f32[1,128]{1,0:T(1,128)S(1)}, f32[1,128]{1,0:T(1,128)}, u32[]{:S(2)}) copy-start(f32[1,128]{1,0:T(1,128)} %get-tuple-element.152) | copy-start | bytes 1540
  915.7 123.0 %copy-start.4 = (f32[1,128]{1,0:T(1,128)S(1)}, f32[1,128]{1,0:T(1,128)}, u32[]{:S(2)}) copy-start(f32[1,128]{1,0:T(1,128)} %get-tuple-element.153) | copy-start | bytes 1540
  915.7 123.0 %copy-start.5 = (f32[1,128]{1,0:T(1,128)S(1)}, f32[1,128]{1,0:T(1,128)}, u32[]{:S(2)}) copy-start(f32[1,128]{1,0:T(1,128)} %get-tuple-element.154) | copy-start | bytes 1540
  915.7 123.0 %copy-start.6 = (f32[1,128]{1,0:T(1,128)S(1)}, f32[1,128]{1,0:T(1,128)}, u32[]{:S(2)}) copy-start(f32[1,128]{1,0:T(1,128)} %get-tuple-element.155) | copy-start | bytes 1540
  915.8 123.0 %copy-start.7 = (f32[1,128]{1,0:T(1,128)S(1)}, f32[1,128]{1,0:T(1,128)}, u32[]{:S(2)}) copy-start(f32[1,128]{1,0:T(1,128)} %get-tuple-element.156) | copy-start | bytes 1540
Sparse Core Ops, SparseCore 0:
  22.9 20.1 sort.11.cloned.1.call-done
  (1 shorter events, 0.0 us)

commit v4 on v3

--- a/solution.py
+++ b/solution.py
@@ -16,6 +16,7 @@
 CHUNK = 128
 UNROLL = 128
 LAG = 2
+PARTS = 4
 REL_HOPS = 6
 STRIP = 32
 REL_PAD = 128
@@ -27,6 +28,30 @@
 VMEM_LIMIT = 60 * 2**20
 
 
+def roll(x, by):
+    return pltpu.roll(x, by, 1)
+
+
+def beside(parts):
+    return jnp.concatenate(parts, axis=1)
+
+
+def below(parts):
+    return jnp.concatenate(parts, axis=0)
+
+
+def lanes(shape):
+    return lax.broadcasted_iota(jnp.int32, shape, 1)
+
+
+def sublanes(shape):
+    return lax.broadcasted_iota(jnp.int32, shape, 0)
+
+
+def row_sum(x):
+    return jnp.sum(x, axis=1, keepdims=True)
+
+
 def wire_rows(rows):
     return 3 * rows + rows // LEFT
 
@@ -36,13 +61,13 @@
     a, c, d = slice(0, LANES), slice(LANES, LANES + HALF), slice(LANES + HALF, half)
     re, im = x[:half], x[half:]
     zero = jnp.zeros((HALF - LEFT, x.shape[1]), x.dtype)
-    return [t.T for t in (re[a], im[a], jnp.concatenate([re[c], im[c]], axis=0), jnp.concatenate([re[d], zero, im[d], zero], axis=0))]
+    return [t.T for t in (re[a], im[a], below([re[c], im[c]]), below([re[d], zero, im[d], zero]))]
 
 
 def tiles_to_columns(tiles):
     a, b, c, d = (t.T for t in tiles)
     high = slice(HALF, HALF + LEFT)
-    return jnp.concatenate([a, c[:HALF], d[:LEFT], b, c[HALF:], d[high]], axis=0)
+    return below([a, c[:HALF], d[:LEFT], b, c[HALF:], d[high]])
 
 
 def each_row(count, body):
@@ -63,13 +88,13 @@
     n = tile.shape[0] // LEFT
     out = tile[:n]
     for k in range(1, LEFT):
-        out = out + pltpu.roll(tile[band(k, n)], LEFT * k, 1)
+        out = out + roll(tile[band(k, n)], LEFT * k)
     return out
 
 
 def unfold_last(packed):
-    keep = lax.broadcasted_iota(jnp.int32, packed.shape, 1) % HALF < LEFT
-    return [jnp.where(keep, packed if k == 0 else pltpu.roll(packed, LANES - LEFT * k, 1), 0.0) for k in range(LEFT)]
+    keep = lanes(packed.shape) % HALF < LEFT
+    return [jnp.where(keep, packed if k == 0 else roll(packed, LANES - LEFT * k), 0.0) for k in range(LEFT)]
 
 
 def tiles_of(x):
@@ -79,8 +104,8 @@
 def times(x, y):
     out = [x[0] * y[0] - x[1] * y[1], x[0] * y[1] + x[1] * y[0]]
     for a, b in zip(x[2:], y[2:]):
-        low = lax.broadcasted_iota(jnp.int32, a.shape, 1) < HALF
-        a_swap, b_swap = pltpu.roll(a, HALF, 1), pltpu.roll(b, HALF, 1)
+        low = lanes(a.shape) < HALF
+        a_swap, b_swap = roll(a, HALF), roll(b, HALF)
         out.append(jnp.where(low, a * b - a_swap * b_swap, a_swap * b + a * b_swap))
     return out
 
@@ -88,8 +113,8 @@
 def times_conj(x, y):
     out = [x[0] * y[0] + x[1] * y[1], x[1] * y[0] - x[0] * y[1]]
     for a, b in zip(x[2:], y[2:]):
-        low = lax.broadcasted_iota(jnp.int32, a.shape, 1) < HALF
-        a_swap, b_swap = pltpu.roll(a, HALF, 1), pltpu.roll(b, HALF, 1)
+        low = lanes(a.shape) < HALF
+        a_swap, b_swap = roll(a, HALF), roll(b, HALF)
         out.append(jnp.where(low, a * b + a_swap * b_swap, a * b_swap - a_swap * b))
     return out
 
@@ -101,7 +126,7 @@
 
 def stack_tiles(tiles):
     rows = tiles[0].shape[0]
-    return jnp.concatenate([t.reshape(rows // 8, 8, LANES) for t in tiles], axis=1).reshape(rows * 4, LANES)
+    return beside([t.reshape(rows // 8, 8, LANES) for t in tiles]).reshape(rows * 4, LANES)
 
 
 def row_at(address):
@@ -125,10 +150,10 @@
     return lax.dot_general(x, y, (dims, ((), ())), preferred_element_type=F32)
 
 
-def bucket_kernel(cfg, edges_hbm, count_ref, negs_hbm, rel_ids_hbm, ent_ref, rel_ref, table_ref, tail_out, head_out, rel_out,
+def bucket_kernel(cfg, edges_hbm, count_ref, negs_hbm, rel_ids_hbm, ent_hbm, rel_ref, table_hbm, tail_hbm, head_hbm, rel_out,
                   tail_rows, head_next, tail_next, head_buf, tail_buf, gh_last, gt_last, rel_buf, query_buf, pos_buf, score_buf, d_neg_buf, grad_buf, piece_buf,
                   neg_rows, neg_grad, rel_three, tail_acc0, tail_acc1, head_acc0, head_acc1, rel_acc, loss_acc,
-                  edge_ref, neg_ref, rel_id_ref, sems):
+                  edge_ref, neg_ref, rel_id_ref, ent_ref, table_ref, tail_out, head_out, sems, table_sems, tail_sems):
     step, tail_bits = cfg
     chunk = CHUNK
     part = chunk // LEFT
@@ -139,8 +164,12 @@
         pltpu.make_async_copy(negs_hbm.at[step, 0], neg_ref, sems.at[0]),
         pltpu.make_async_copy(edges_hbm.at[step, 0], edge_ref, sems.at[1]),
         pltpu.make_async_copy(rel_ids_hbm.at[step], rel_id_ref, sems.at[2]),
+        pltpu.make_async_copy(ent_hbm, ent_ref, sems.at[3]),
     ]
-    for load in loads:
+    parts = table_sems.shape[0]
+    size = table_ref.shape[0] // parts
+    tables = [pltpu.make_async_copy(table_hbm.at[band(n, size)], table_ref.at[band(n, size)], table_sems.at[n]) for n in range(parts)]
+    for load in tables + loads:
         load.start()
 
     def head_of(e):
@@ -149,24 +178,13 @@
     def tail_of(e):
         return row_at(e & (2**tail_bits - 1))
 
-    def widen(n, carry):
-        base = pl.multiple_of(n * chunk, chunk)
-        tiles = [table_ref[n, band(t, chunk), :].astype(F32) for t in TILES[:-1]]
-        tiles.append(jnp.concatenate(unfold_last(table_ref[n, 3 * chunk:, :].astype(F32)), axis=0))
-        tail_rows[pl.ds(base * 4, chunk * 4), :] = stack_tiles(tiles)
-        for acc in tail_acc:
-            acc[pl.ds(base * 4, chunk * 4), :] = jnp.zeros((chunk * 4, LANES), F32)
+    def clear(accs, n, carry):
+        for acc in accs:
+            acc[pl.ds(pl.multiple_of(n * chunk * 4, chunk * 4), chunk * 4), :] = jnp.zeros((chunk * 4, LANES), F32)
         return carry
 
-    lax.fori_loop(0, table_ref.shape[0], widen, 0)
-
-    def clear(n, carry):
-        base = pl.multiple_of(n * chunk * 4, chunk * 4)
-        for acc in head_acc:
-            acc[pl.ds(base, chunk * 4), :] = jnp.zeros((chunk * 4, LANES), F32)
-        return carry
-
-    lax.fori_loop(0, head_out.shape[0], clear, 0)
+    lax.fori_loop(0, table_ref.shape[0], functools.partial(clear, tail_acc), 0)
+    lax.fori_loop(0, head_out.shape[0], functools.partial(clear, head_acc), 0)
     neg_grad[...] = jnp.zeros_like(neg_grad)
     gh_last[...] = jnp.zeros_like(gh_last)
     gt_last[...] = jnp.zeros_like(gt_last)
@@ -177,6 +195,17 @@
     for load in loads:
         load.wait()
 
+    def widen(n, carry):
+        base = pl.multiple_of(n * chunk, chunk)
+        tiles = [table_ref[n, band(t, chunk), :].astype(F32) for t in TILES[:-1]]
+        tiles.append(below(unfold_last(table_ref[n, 3 * chunk:, :].astype(F32))))
+        tail_rows[pl.ds(base * 4, chunk * 4), :] = stack_tiles(tiles)
+        return carry
+
+    for n, load in enumerate(tables):
+        load.wait()
+        lax.fori_loop(n * size, (n + 1) * size, widen, 0)
+
     def take_negs(n, carry):
         base = pl.multiple_of(n * UNROLL, UNROLL)
 
@@ -214,9 +243,9 @@
 
     def block(n, carry):
         base = pl.multiple_of(n * BLOCK, BLOCK)
-        hot = lax.broadcasted_iota(jnp.int32, (REL_PAD, BLOCK), 0) == rel_id_ref[pl.ds(n, 1), :]
+        hot = sublanes((REL_PAD, BLOCK)) == rel_id_ref[pl.ds(n, 1), :]
         hot = jnp.where(hot, 1.0, 0.0).astype(BF16)
-        rel_buf[...] = dot(jnp.concatenate([hot] * 3, axis=0), rel_three[...], COL_COL)
+        rel_buf[...] = dot(below([hot] * 3), rel_three[...], COL_COL)
         for span in spans:
             head, tail, rel = tiles_at(head_next, span.start, STRIP), tiles_at(tail_next, span.start, STRIP), tiles_of(rel_buf[span, :])
             wide = slice(4 * span.start, 4 * span.stop)
@@ -227,17 +256,17 @@
                 query_buf[span, band(t, LANES)] = q
                 product = q.astype(F32) * tail[t]
                 total = product if total is None else total + product
-            pos_buf[span, :] = jnp.sum(total, axis=1, keepdims=True)
+            pos_buf[span, :] = row_sum(total)
         each_row(BLOCK, take_edges(base + 2 * BLOCK))
         each_row(BLOCK // 2, put_edges(base))
         score_buf[...] = dot(query_buf[...], neg_rows[...], ROW_ROW)
         for span in spans:
-            weight = jnp.where(lax.broadcasted_iota(jnp.int32, (STRIP, 1), 0) + (base + span.start) < count, 1.0, 0.0)
+            weight = jnp.where(sublanes((STRIP, 1)) + (base + span.start) < count, 1.0, 0.0)
             score, pos = score_buf[span, :], pos_buf[span, :]
             top = jnp.maximum(jnp.max(score, axis=1, keepdims=True), pos)
             pos_exp = jnp.exp(pos - top)
             neg_exp = jnp.exp(score - top)
-            total = pos_exp + jnp.sum(neg_exp, axis=1, keepdims=True)
+            total = pos_exp + row_sum(neg_exp)
             loss_acc[...] += jnp.sum(weight * (top + jnp.log(total) - pos), axis=0, keepdims=True)
             pos_buf[span, :] = weight * (pos_exp / total - 1.0)
             d_neg_buf[span, :] = ((weight / total) * neg_exp).astype(BF16)
@@ -253,7 +282,7 @@
             for t, grad in enumerate(times_conj(grad_q, tiles_at(head_buf, span.start, STRIP))):
                 for k, piece in enumerate(in_three(grad)):
                     piece_buf[k * BLOCK + span.start:k * BLOCK + span.stop, band(t, LANES)] = piece
-        rel_acc[...] += dot(jnp.concatenate([hot] * 3, axis=1), piece_buf[...], ROW_COL)
+        rel_acc[...] += dot(beside([hot] * 3), piece_buf[...], ROW_COL)
         return carry
 
     blocks = pl.cdiv(count, BLOCK)
@@ -274,28 +303,36 @@
 
     lax.fori_loop(0, negs // UNROLL, put_negs, 0)
 
-    def emit(out_ref, acc):
-        def one(n, carry):
-            base = pl.multiple_of(n * chunk, chunk)
-            tiles = [a + b for a, b in zip(tiles_at(acc[0], base, chunk), tiles_at(acc[1], base, chunk))]
-            for t in TILES[:-1]:
-                out_ref[n, band(t, chunk), :] = tiles[t]
-            out_ref[n, 3 * chunk:, :] = fold_last(tiles[3])
-            return carry
-
-        lax.fori_loop(0, out_ref.shape[0], one, 0)
-
-    emit(tail_out, tail_acc)
-    emit(head_out, head_acc)
+    def emit(out_ref, acc, n, carry):
+        base = pl.multiple_of(n * chunk, chunk)
+        tiles = [a + b for a, b in zip(tiles_at(acc[0], base, chunk), tiles_at(acc[1], base, chunk))]
+        for t in TILES[:-1]:
+            out_ref[n, band(t, chunk), :] = tiles[t]
+        out_ref[n, 3 * chunk:, :] = fold_last(tiles[3])
+        return carry
+
+    stores = []
+    for n in range(tail_sems.shape[0]):
+        out, dst, acc, span = (head_out, head_hbm, head_acc, range(head_out.shape[0])) if n == parts else (tail_out, tail_hbm, tail_acc, range(n * size, (n + 1) * size))
+        lax.fori_loop(span.start, span.stop, functools.partial(emit, out, acc), 0)
+        part_of = pl.ds(span.start, len(span))
+        stores.append(pltpu.make_async_copy(out.at[part_of], dst.at[part_of], tail_sems.at[n]))
+        stores[-1].start()
     _, x, _, top, _ = where_here()
     group = 2 * x + top
-    row = lax.broadcasted_iota(jnp.int32, (REL_PAD, LANES), 0)
-    lane = lax.broadcasted_iota(jnp.int32, (REL_PAD, LANES), 1)
+    row = sublanes((REL_PAD, LANES))
+    lane = lanes((REL_PAD, LANES))
     loss = jnp.where(lane == group, loss_acc[...], 0.0)
     for t in TILES[:-1]:
         rows = rel_acc[:, band(t, LANES)]
         rel_out[band(t, REL_PAD), :] = jnp.where(row == REL_PAD - 1, loss, rows) if t == 0 else rows
     rel_out[3 * REL_PAD:, :] = fold_last(rel_acc[:, 3 * LANES:])
+    for store in stores:
+        store.wait()
+
+
+def dma_sems(n):
+    return pltpu.SemaphoreType.DMA((n,))
 
 
 def bucket_call(step, tail_bits, edges, counts, negs, rel_ids, ent, rel, table):
@@ -313,15 +350,17 @@
             jax.ShapeDtypeStruct((rows // CHUNK, wire, LANES), F32),
             jax.ShapeDtypeStruct((wire_rows(REL_PAD), LANES), F32),
         ),
-        in_specs=[hbm, smem, hbm, hbm, vmem, vmem, vmem],
-        out_specs=(vmem, vmem, vmem),
+        in_specs=[hbm, smem, hbm, hbm, hbm, vmem, hbm],
+        out_specs=(hbm, hbm, vmem),
         scratch_shapes=[
             table_rows, *[block] * 6, pltpu.VMEM((BLOCK, width), F32), pltpu.VMEM((BLOCK, width), BF16), pltpu.VMEM((BLOCK, 1), F32),
             pltpu.VMEM((BLOCK, neg_count), F32), pltpu.VMEM((BLOCK, neg_count), BF16), pltpu.VMEM((BLOCK, width), F32), pltpu.VMEM((3 * BLOCK, width), BF16),
             pltpu.VMEM((neg_count, width), BF16), pltpu.VMEM((neg_count, width), F32), pltpu.VMEM((3 * REL_PAD, width), BF16),
             table_rows, table_rows, head_rows, head_rows,
             pltpu.VMEM((REL_PAD, width), F32), pltpu.VMEM((1, 1), F32),
-            pltpu.SMEM((edges.shape[-1],), jnp.int32), pltpu.SMEM((neg_count,), jnp.int32), pltpu.VMEM(rel_ids.shape[1:], jnp.int32), pltpu.SemaphoreType.DMA((3,)),
+            pltpu.SMEM((edges.shape[-1],), jnp.int32), pltpu.SMEM((neg_count,), jnp.int32), pltpu.VMEM(rel_ids.shape[1:], jnp.int32),
+            pltpu.VMEM(ent.shape, F32), pltpu.VMEM(table.shape, BF16), pltpu.VMEM((chunks, wire, LANES), F32), pltpu.VMEM((rows // CHUNK, wire, LANES), F32),
+            dma_sems(4), dma_sems(PARTS), dma_sems(PARTS + 1),
         ],
         compiler_params=pltpu.CompilerParams(vmem_limit_bytes=VMEM_LIMIT),
         name='bucket',
@@ -341,19 +380,19 @@
 
 def adagrad(rows, state, grad, mean_of, learn_rate):
     square = grad[0] * grad[0] + grad[1] * grad[1] + grad[2] * grad[2] + grad[3] * grad[3]
-    state = state + jnp.sum(square, axis=1, keepdims=True) / mean_of
+    state = state + row_sum(square) / mean_of
     root = jnp.sqrt(state + EPSILON)
     return [r - learn_rate * (g / root) for r, g in zip(rows, grad)], state
 
 
-def exchange_kernel(cfg, tail_ref, head_ref, rel_grad_ref, ent_ref, state_ref, rel_ref, rel_state_ref, *refs):
+def exchange_kernel(cfg, tail_ref, head_hbm, rel_grad_ref, ent_hbm, state_ref, rel_ref, rel_state_ref, *refs):
     step, groups, chunks, emb_width, last = cfg
     if last:
         ent_wire, rel_out, loss_out, *refs = refs
     else:
-        ent_out, state_out, rel_out, rel_state_out, loss_out, table, *refs = refs
+        ent_out, state_out, rel_out, rel_state_out, loss_out, table_hbm, *refs, table, store_sem = refs
     (own, from_core, from_y, from_group, rel_sum, rel_from, send_buf,
-     own_sem, core_send, core_recv, y_send, y_recv, group_send, group_recv, rel_send, rel_recv, out_send, out_recv) = refs
+     own_sem, core_send, core_recv, y_send, y_recv, group_send, group_recv, rel_send, rel_recv, out_send, out_recv, head_ref, ent_ref, row_sem) = refs
     learn_rate = LR_SCALE * emb_width ** -0.25
     chunk = CHUNK
     y, x, core, top, bot = where_here()
@@ -365,6 +404,9 @@
 
     def at(dy, dx, c):
         return {'data': dy, 'ent': 2 * dx + c}
+
+    def slot_of(low, c, k):
+        return (low * 2 + c) * chunks + k
 
     def turned(shift):
         return (bot + shift) % 2
@@ -398,10 +440,24 @@
 
     shards = [(1 - keep, k) for k in range(chunks)] + [(keep, k) for k in range(chunks)]
     loads, cores = [], []
+    row_loads = [pltpu.make_async_copy(src, dst, row_sem.at[n]) for n, (src, dst) in enumerate(((head_hbm, head_ref), (ent_hbm, ent_ref)))]
+    for load in row_loads:
+        load.start()
+    stores = []
+
+    def store(n, src, dst):
+        copy = pltpu.make_async_copy(src, dst, store_sem.at[n])
+        copy.start()
+        stores.append(copy)
+
+    def store_table(low, c, k):
+        slot = slot_of(low, c, k)
+        store(slot, table.at[slot], table_hbm.at[slot])
+
     rel_copies = [start(remote(rel_grad_ref.at[1 - core], rel_from.at[0], rel_send.at[0], rel_recv.at[0], rel_peers[0]))]
     for n, (low, k) in enumerate(shards):
-        cores.append(start(remote(tail_ref.at[(low * 2 + 1 - core) * chunks + k], from_core.at[n], core_send.at[n], core_recv.at[n], other_core)))
-        load = pltpu.make_async_copy(tail_ref.at[(low * 2 + core) * chunks + k], own.at[n], own_sem.at[n])
+        cores.append(start(remote(tail_ref.at[slot_of(low, 1 - core, k)], from_core.at[n], core_send.at[n], core_recv.at[n], other_core)))
+        load = pltpu.make_async_copy(tail_ref.at[slot_of(low, core, k)], own.at[n], own_sem.at[n])
         load.start()
         loads.append(load)
 
@@ -431,7 +487,7 @@
             gs.append(start(remote(own.at[chunks + k], from_group.at[k], group_send.at[k], group_recv.at[k], grad_to)))
 
     def cross_copy(k):
-        return remote(send_buf.at[k], ent_wire.at[(bot * 2 + core) * chunks + k], out_send.at[2 * chunks + k], out_recv.at[(bot * 2 + core) * chunks + k], other_core)
+        return remote(send_buf.at[k], ent_wire.at[slot_of(bot, core, k)], out_send.at[2 * chunks + k], out_recv.at[slot_of(bot, core, k)], other_core)
 
     turn = (y + 4 - 2 * core) % 4
     near = 1 - turn % 2
@@ -439,7 +495,7 @@
     onward = at((y + 1 + 2 * back) % 4, x, core)
 
     def landed(low, c, k):
-        slot = (low * 2 + c) * chunks + k
+        slot = slot_of(low, c, k)
         remote(ent_wire.at[slot], ent_wire.at[slot], out_send.at[0], out_recv.at[slot], other_core).wait_recv()
 
     def stage_relay(k):
@@ -448,30 +504,35 @@
         for c in CORES:
             landed(near, c, k - 1)
             landed(near, c, k)
-            slot = (near * 2 + c) * chunks + k - 1 + back
+            slot = slot_of(near, c, k) - 1 + back
             start(remote(ent_wire.at[slot], ent_wire.at[slot], out_send.at[(3 + c) * chunks + k], out_recv.at[slot], onward))
 
     def stage_update(k):
+        if k == 0:
+            for load in row_loads:
+                load.wait()
         if step:
             gs[k].wait_recv()
         total = from_group if step else own
         base = k if step else chunks + k
         grad = [total[base, band(t, chunk), :] + head_ref[k, band(t, chunk), :] for t in TILES[:-1]]
-        grad.append(jnp.concatenate(unfold_last(total[base, 3 * chunk:, :] + head_ref[k, 3 * chunk:, :]), axis=0))
+        grad.append(below(unfold_last(total[base, 3 * chunk:, :] + head_ref[k, 3 * chunk:, :])))
         span = band(k, chunk)
         rows, state = adagrad(tiles_at(ent_ref, k * chunk, chunk), state_ref[span, :], grad, emb_width, learn_rate)
         wire = rows[:3] + [fold_last(rows[3])]
         if last:
-            lane = lax.broadcasted_iota(jnp.int32, (chunk, LANES), 1)
+            lane = lanes((chunk, LANES))
             wire.append(fold_last(jnp.where(lane < 1, state, 0.0)))
         else:
-            ent_out[band(k, 4 * chunk), :] = stack_tiles(rows)
+            wide = band(k, 4 * chunk)
+            ent_ref[wide, :] = stack_tiles(rows)
+            store(4 * chunks + k, ent_ref.at[wide], ent_out.at[wide])
             state_out[span, :] = state
         offset = 0
         for piece in wire:
             send_buf[k, offset:offset + piece.shape[0], :] = piece.astype(send_buf.dtype)
             offset += piece.shape[0]
-        slot = (bot * 2 + core) * chunks + k
+        slot = slot_of(bot, core, k)
         if last:
             for n, turn in enumerate((1, 3)):
                 start(remote(send_buf.at[k], ent_wire.at[slot], out_send.at[n * chunks + k], out_recv.at[slot], at((y + turn) % 4, x, top)))
@@ -487,16 +548,18 @@
             outs.append(start(remote(send_buf.at[k], table.at[slot], out_send.at[k], out_recv.at[k], table_to)))
 
     def forward(n, low, k, peer):
-        slot = (low * 2 + core) * chunks + k
+        slot = slot_of(low, core, k)
         return start(remote(table.at[slot], table.at[slot], out_send.at[n * chunks + k], out_recv.at[n * chunks + k], peer))
 
     def stage_forward(k):
         outs[k].wait_recv()
+        store_table(turned(nxt), core, k)
         forwards.append(forward(1, turned(nxt), k, other_y))
         crosses.append(forward(2, turned(nxt), k, other_core))
 
     def stage_cross(k):
         forwards[k].wait_recv()
+        store_table(1 - turned(nxt), core, k)
         crosses.append(forward(3, 1 - turned(nxt), k, other_core))
 
     stages = (stage_group, stage_update, stage_relay) if last else (stage_group, stage_update, stage_forward, stage_cross)
@@ -510,10 +573,10 @@
 
     rel_copies[rel_steps].wait_recv()
     halves = rel_sum[rel_steps - 1], rel_from[rel_steps]
-    summed = jnp.concatenate([jnp.where(core == n, halves[0], halves[1]) for n in CORES], axis=0)
-    rel_grad = [summed[band(t, REL_PAD)] for t in TILES[:-1]] + [jnp.concatenate(unfold_last(summed[3 * REL_PAD:]), axis=0)]
+    summed = below([jnp.where(core == n, halves[0], halves[1]) for n in CORES])
+    rel_grad = [summed[band(t, REL_PAD)] for t in TILES[:-1]] + [below(unfold_last(summed[3 * REL_PAD:]))]
     loss_out[...] = rel_grad[0][REL_PAD - 1:, :]
-    row = lax.broadcasted_iota(jnp.int32, (REL_PAD, LANES), 0)
+    row = sublanes((REL_PAD, LANES))
     rel_grad[0] = jnp.where(row < REL_PAD - 1, rel_grad[0], 0.0)
     rel_rows, rel_state = adagrad(tiles_of(rel_ref[...]), rel_state_ref[...], rel_grad, emb_width, learn_rate)
     for t in TILES:
@@ -531,8 +594,13 @@
             for k in range(chunks):
                 cross_copy(k).wait_send()
     else:
-        for copy in crosses:
+        for n, copy in enumerate(crosses):
             copy.wait_recv()
+        for low in CORES:
+            for k in range(chunks):
+                store_table(low, 1 - core, k)
+        for copy in stores:
+            copy.wait()
     for copy in pending:
         copy.wait_send()
 
@@ -549,26 +617,27 @@
     out_type = F32 if last else BF16
     gathered = jax.ShapeDtypeStruct((4 * chunks, out_wire, LANES), out_type)
     out_shape = (gathered, like(rel), loss) if last else (like(ent), like(state), like(rel), like(rel_state), loss, gathered)
-    sems = lambda n: pltpu.SemaphoreType.DMA((n,))
     return pl.pallas_call(
         functools.partial(exchange_kernel, (step, groups, chunks, emb_width, last)),
         out_shape=out_shape,
-        in_specs=[hbm] + [vmem] * 6,
-        out_specs=tuple(vmem for _ in out_shape),
+        in_specs=[hbm, hbm, vmem, hbm, vmem, vmem, vmem],
+        out_specs=(vmem,) * 3 if last else (hbm, vmem, vmem, vmem, vmem, hbm),
         scratch_shapes=[
             pltpu.VMEM((2 * chunks, wire, LANES), F32), pltpu.VMEM((2 * chunks, wire, LANES), F32),
             pltpu.VMEM((chunks, wire, LANES), F32), pltpu.VMEM((chunks, wire, LANES), F32),
             pltpu.VMEM((REL_HOPS - 1, *rel_grad.shape[1:]), F32), pltpu.VMEM((REL_HOPS, *rel_grad.shape[1:]), F32),
             pltpu.VMEM((chunks, out_wire, LANES), out_type),
-            sems(2 * chunks), sems(2 * chunks), sems(2 * chunks), sems(chunks), sems(chunks), sems(chunks), sems(chunks),
-            sems(REL_HOPS), sems(REL_HOPS), sems(5 * chunks), sems(4 * chunks),
+            *[dma_sems(2 * chunks)] * 3, *[dma_sems(chunks)] * 4,
+            dma_sems(REL_HOPS), dma_sems(REL_HOPS), dma_sems(5 * chunks), dma_sems(4 * chunks),
+            pltpu.VMEM(head.shape, F32), pltpu.VMEM(ent.shape, F32), dma_sems(2),
+            *(() if last else (pltpu.VMEM(gathered.shape, BF16), dma_sems(5 * chunks))),
         ],
         compiler_params=pltpu.CompilerParams(vmem_limit_bytes=VMEM_LIMIT, collective_id=step, has_side_effects=True),
         name='exchange',
     )(tail, head, rel_grad, ent, state, rel, rel_state)
 
 
-def index_kernel(cfg, head_ref, tail_ref, rel_ref, mask_ref, neg_ref, key_out, count_out, neg_out, packed, shares, neg_buf, send_sem, recv_sem, neg_send, neg_recv):
+def index_kernel(cfg, head_ref, tail_ref, rel_ref, mask_ref, neg_ref, word_out, rel_id_out, count_out, neg_out, packed, shares, neg_buf, send_sem, recv_sem, neg_send, neg_recv):
     head_bits, tail_bits, spare = cfg
     y, x, core, top, bot = where_here()
     own = 2 * x + core
@@ -591,16 +660,31 @@
         remote(neg_buf, neg_out, neg_send, neg_recv, other_core).start()
         neg_out[...] = neg_buf[...]
 
-    count = jnp.zeros((packed.shape[0], 1), jnp.int32)
-    width = packed.shape[1]
-    for row in range(4):
+    for row in TILES:
         remote(packed, shares.at[row], send_sem.at[0], recv_sem.at[row], other_core).wait_recv()
-        share = shares[row]
-        mine = ((share >> head_bits) & 3 == 2 * bot + core) & (share >> (2 * tail_bits) != spare)
-        local = (share & (2**head_bits - 1)) | (share >> tail_bits << head_bits)
-        key_out[:, band(row, width)] = jnp.where(mine, local, spare << (head_bits + tail_bits))
-        count = count + jnp.sum(jnp.where(mine, 1, 0), axis=1, keepdims=True)
-    count_out[...] = jnp.broadcast_to(count, count_out.shape)
+    share = beside([shares[row] for row in TILES])
+    mine = ((share >> head_bits) & 3 == 2 * bot + core) & (share >> (2 * tail_bits) != spare)
+    lane = lanes(share.shape)
+    width = share.shape[1]
+    steps = (width - 1).bit_length()
+    other = jnp.where(mine, 0, 1)
+    before = other
+    for bit in range(steps):
+        before = before + jnp.where(lane < 2**bit, 0, roll(before, 2**bit))
+    count_out[...] = jnp.broadcast_to(width - before[:, width - 1:], count_out.shape)
+    none = spare << (head_bits + tail_bits)
+    edge = jnp.where(mine, (share & (2**head_bits - 1)) | (share >> tail_bits << head_bits), none)
+    shift = jnp.where(mine, before - other, 0)
+    for bit in range(steps):
+        here = (shift >> bit) & 1 == 1
+        edge_in, shift_in = roll(edge, width - 2**bit), roll(shift, width - 2**bit)
+        there = (shift_in >> bit) & 1 == 1
+        edge = jnp.where(there, edge_in, jnp.where(here, none, edge))
+        shift = jnp.where(there, shift_in, jnp.where(here, 0, shift))
+    rel_id_out[...] = edge >> (head_bits + tail_bits)
+    head, tail = edge & (2**head_bits - 1), (edge >> head_bits) & (2**tail_bits - 1)
+    margin = jnp.zeros((share.shape[0], BLOCK), jnp.int32)
+    word_out[...] = beside([margin, (row_address(head) << (tail_bits + 2)) | row_address(tail), margin])
     for copy, (_, here) in zip(to_users, users):
         @pl.when(jnp.logical_not(here))
         def _():
@@ -620,9 +704,9 @@
     groups, share = head.shape
     return pl.pallas_call(
         functools.partial(index_kernel, cfg),
-        out_shape=(jax.ShapeDtypeStruct((groups, reps * share), jnp.int32), jax.ShapeDtypeStruct((groups, LANES), jnp.int32), jax.ShapeDtypeStruct(neg.shape, jnp.int32)),
+        out_shape=tuple(jax.ShapeDtypeStruct((groups, n), jnp.int32) for n in (reps * share + 2 * BLOCK, reps * share, LANES, neg.shape[1])),
         in_specs=[vmem] * 5,
-        out_specs=(vmem,) * 3,
+        out_specs=(vmem,) * 4,
         scratch_shapes=[pltpu.VMEM(head.shape, jnp.int32), pltpu.VMEM((reps, *head.shape), jnp.int32), pltpu.VMEM(neg.shape, jnp.int32),
                         pltpu.SemaphoreType.DMA((4,)), pltpu.SemaphoreType.DMA((4,)), pltpu.SemaphoreType.DMA, pltpu.SemaphoreType.DMA],
         compiler_params=pltpu.CompilerParams(collective_id=20, has_side_effects=True),
@@ -716,7 +800,7 @@
     chunk = CHUNK
     for n in range(wire_ref.shape[0]):
         tiles = [wire_ref[n, band(t, chunk), :] for t in TILES[:-1]]
-        tiles.append(jnp.concatenate(unfold_last(wire_ref[n, 3 * chunk:wire_rows(chunk), :]), axis=0))
+        tiles.append(below(unfold_last(wire_ref[n, 3 * chunk:wire_rows(chunk), :])))
         ent_out[:, band(n, chunk)] = tiles_to_columns(tiles)
 
     @pl.when(pl.program_id(0) == 0)
@@ -755,13 +839,9 @@
         ent = lax.axis_index('ent')
         _, _, core, top, bot = where_here()
 
-        keys, counts, neg = index_call((head_bits, tail_bits, spare), head_idx[0], tail_idx[0], rel_idx[0], edge_mask[0], neg_idx[0], data_reps)
-        keys = lax.sort(keys, dimension=1)
-        counts = counts[:, 0]
-        neg = neg[:, None]
-        rel_ids = (keys >> (head_bits + tail_bits)).reshape(groups, -1, BLOCK)
-        words = (row_address(keys & (shard - 1)) << (tail_bits + 2)) | row_address((keys >> head_bits) & (part_rows - 1))
-        words = jnp.pad(words, ((0, 0), (BLOCK, BLOCK)))[:, None]
+        words, rel_ids, counts, neg = index_call((head_bits, tail_bits, spare), head_idx[0], tail_idx[0], rel_idx[0], edge_mask[0], neg_idx[0], data_reps)
+        words, neg, counts = words[:, None], neg[:, None], counts[:, 0]
+        rel_ids = rel_ids.reshape(groups, -1, BLOCK)
 
         table, ent_now, rel_now = rows_call(ent_table.T, jnp.pad(rel_table.T, ((0, 0), (0, REL_PAD - rel_rows))))
         to_core = lambda c: lax.dynamic_slice_in_dim(ent_state, (2 * bot + c) * shard, shard)
@@ -779,7 +859,7 @@
             losses.append(loss)
         ent_out, rel_out = finish_call(wire, rel_now, emb_width)
         state_out = wire[:, wire_rows(CHUNK):, :HALF:LEFT].transpose(0, 2, 1).reshape(part_rows)
-        loss_rows = jnp.concatenate(losses, axis=0) / bucket_edges
+        loss_rows = below(losses) / bucket_edges
         bucket_loss = lax.dynamic_slice_in_dim(loss_rows, ent, 1, axis=1).reshape(1, groups)
         return ent_out.T, state_out, rel_out[:, :rel_rows].T, bucket_loss
 

time: 1060 us -> 1040 us (0.981)
  between operations: 14.6 us -> 1.48 us
    pallas_call x8, Pallas kernels: 742 us -> 718 us  [exchange_call(): pl.pallas_call(functools.partial(exchange_kernel, (step, groups, chunks,...]
  transfers between devices with their start and end apart: 1 -> 1, of which waited for: 0 -> 0; matrix products, arithmetic and copies ran while one was open for 0% -> 1% of each run, Pallas kernels for 3% -> 7%
where the time goes in v4:
time: 1040 us
  Pallas kernels  1020 us (98%)
  local copies, waits for them, and re-layouts  13.8 us (1%)
    pallas_call x8, Pallas kernels, exchange_call(): pl.pallas_call(functools.partial(exchange_kernel, (step, groups, chunks,...  718 us
    pallas_call x8, Pallas kernels, bucket_call(): pl.pallas_call(functools.partial(bucket_kernel, (step, tail_bits)), out_s...  258 us
  transfers between devices with their start and end apart: 1, of which 0 were waited for; matrix products, arithmetic and copies ran while one was open for 1% of the time, Pallas kernels for 7%

profile of v4, /device:TPU:97, one launch (start us, length us, event | category | flops | bytes accessed | tf_op | source)
XLA Modules:
  0.0 1036.1 jit_solution(11105356693574790811)
XLA Ops:
  0.7 0.7 dynamic_slice.10
  1.4 1.3 collective-permute-start
  2.7 15.7 %setup_index.1 = (s32[8,8704]{1,0:T(8,128)}, s32[8,8192]{1,0:T(8,128)}, s32[8,128]{1,0:T(8,128)}, s32[8,1024]{1,0:T(8,128)}) custom-call(s32[8,2048]{1,0:T(8,128)} %bitcast.45, s32[8,2048]{1,0:T(8,128)} %bitcast.46, s32[8,2048]{1,0:T(8,128)} %bitcast.47, s32[8,2048]{1,0:T(8,128)} %bitcast.48, s32[8,1024]{1,0:T(8,128)} %bitcast.49), custom_call_target="tpu_custom_call" | custom-call | tf_op jit(solution)/shard_map/setup_index/pallas_call | solution.py:705
  18.3 1.3 slice_reduce_fusion.count_ref
  19.6 1.6 pad.4.rel_ref
  21.3 16.6 %setup_rows.1 = (bf16[32,400,128]{2,1,0:T(8,128)(2,1)}, f32[4096,128]{1,0:T(8,128)}, f32[128,512]{1,0:T(8,128)}) custom-call(f32[400,4096]{1,0:T(8,128)} %bitcast.33, f32[400,128]{1,0:T(8,128)} %pad.4.rel_ref), custom_call_target="tpu_custom_call" | custom-call | flops 1000000000 | bytes 20000000 | tf_op jit(solution)/shard_map/setup_rows/pallas_call | solution.py:787
  38.0 0.9 broadcast_in_dim.12.edges_hbm
  39.5 0.8 copy.16
  40.3 36.7 %bucket.8 = (f32[32,400,128]{2,1,0:T(8,128)}, f32[8,400,128]{2,1,0:T(8,128)}, f32[400,128]{1,0:T(8,128)}) custom-call(s32[8,1,8704]{2,1,0:T(1,128)} %broadcast_in_dim.12.edges_hbm, s32[8]{0:T(128)} %slice_reduce_fusion.count_ref, s32[8,1,1024]{2,1,0:T(1,128)} %broadcast_in_dim.13.negs_hbm, s32[8,32,256]{2,1,0:T(8,128)} %bitcast.25, ...), custom_call_target="tpu_custom_call" | custom-call | tf_op jit(solution)/shard_map/bucket/pallas_call | solution.py:346
  77.0 0.7 dynamic-slice_select_fusion
  77.7 1.0 copy.12.state_ref
  79.4 69.7 %exchange.8 = (f32[4096,128]{1,0:T(8,128)}, f32[1024,1]{1,0:T(8,128)}, f32[128,512]{1,0:T(8,128)}, f32[128,1]{1,0:T(8,128)}, f32[1,128]{1,0:T(1,128)}, /*index=5*/bf16[32,400,128]{2,1,0:T(8,128)(2,1)}) custom-call(f32[32,400,128]{2,1,0:T(8,128)} %get-tuple-element.89.tail_ref, f32[8,400,128]{2,1,0:T(8,128)} %get-tuple-element.90.head_hbm, ...), custom_call_target="tpu_custom_call" | custom-call | tf_op jit(solution)/shard_map/exchange/pallas_call | solution.py:620
  149.1 34.2 %bucket.9 = (f32[32,400,128]{2,1,0:T(8,128)}, f32[8,400,128]{2,1,0:T(8,128)}, f32[400,128]{1,0:T(8,128)}) custom-call(s32[8,1,8704]{2,1,0:T(1,128)} %broadcast_in_dim.12.edges_hbm, s32[8]{0:T(128)} %slice_reduce_fusion.count_ref, s32[8,1,1024]{2,1,0:T(1,128)} %broadcast_in_dim.13.negs_hbm, s32[8,32,256]{2,1,0:T(8,128)} %bitcast.26, ...), custom_call_target="tpu_custom_call" | custom-call | tf_op jit(solution)/shard_map/bucket/pallas_call | solution.py:346
  183.3 76.5 %exchange.9 = (f32[4096,128]{1,0:T(8,128)}, f32[1024,1]{1,0:T(8,128)}, f32[128,512]{1,0:T(8,128)}, f32[128,1]{1,0:T(8,128)}, f32[1,128]{1,0:T(1,128)}, /*index=5*/bf16[32,400,128]{2,1,0:T(8,128)(2,1)}) custom-call(f32[32,400,128]{2,1,0:T(8,128)} %get-tuple-element.95.tail_ref, f32[8,400,128]{2,1,0:T(8,128)} %get-tuple-element.96.head_hbm, ...), custom_call_target="tpu_custom_call" | custom-call | tf_op jit(solution)/shard_map/exchange/pallas_call | solution.py:620
  259.7 23.1 %bucket.10 = (f32[32,400,128]{2,1,0:T(8,128)}, f32[8,400,128]{2,1,0:T(8,128)}, f32[400,128]{1,0:T(8,128)}) custom-call(s32[8,1,8704]{2,1,0:T(1,128)} %broadcast_in_dim.12.edges_hbm, s32[8]{0:T(128)} %slice_reduce_fusion.count_ref, s32[8,1,1024]{2,1,0:T(1,128)} %broadcast_in_dim.13.negs_hbm, s32[8,32,256]{2,1,0:T(8,128)} %bitcast.27, ...), custom_call_target="tpu_custom_call" | custom-call | tf_op jit(solution)/shard_map/bucket/pallas_call | solution.py:346
  282.8 94.8 %exchange.10 = (f32[4096,128]{1,0:T(8,128)}, f32[1024,1]{1,0:T(8,128)}, f32[128,512]{1,0:T(8,128)}, f32[128,1]{1,0:T(8,128)}, f32[1,128]{1,0:T(1,128)}, /*index=5*/bf16[32,400,128]{2,1,0:T(8,128)(2,1)}) custom-call(f32[32,400,128]{2,1,0:T(8,128)} %get-tuple-element.103.tail_ref, f32[8,400,128]{2,1,0:T(8,128)} %get-tuple-element.104.head_hbm, ...), custom_call_target="tpu_custom_call" | custom-call | tf_op jit(solution)/shard_map/exchange/pallas_call | solution.py:620
  377.6 26.2 %bucket.11 = (f32[32,400,128]{2,1,0:T(8,128)}, f32[8,400,128]{2,1,0:T(8,128)}, f32[400,128]{1,0:T(8,128)}) custom-call(s32[8,1,8704]{2,1,0:T(1,128)} %broadcast_in_dim.12.edges_hbm, s32[8]{0:T(128)} %slice_reduce_fusion.count_ref, s32[8,1,1024]{2,1,0:T(1,128)} %broadcast_in_dim.13.negs_hbm, s32[8,32,256]{2,1,0:T(8,128)} %bitcast.28, ...), custom_call_target="tpu_custom_call" | custom-call | tf_op jit(solution)/shard_map/bucket/pallas_call | solution.py:346
  403.8 100.7 %exchange.11 = (f32[4096,128]{1,0:T(8,128)}, f32[1024,1]{1,0:T(8,128)}, f32[128,512]{1,0:T(8,128)}, f32[128,1]{1,0:T(8,128)}, f32[1,128]{1,0:T(1,128)}, /*index=5*/bf16[32,400,128]{2,1,0:T(8,128)(2,1)}) custom-call(f32[32,400,128]{2,1,0:T(8,128)} %get-tuple-element.111.tail_ref, f32[8,400,128]{2,1,0:T(8,128)} %get-tuple-element.112.head_hbm, ...), custom_call_target="tpu_custom_call" | custom-call | tf_op jit(solution)/shard_map/exchange/pallas_call | solution.py:620
  504.6 33.9 %bucket.12 = (f32[32,400,128]{2,1,0:T(8,128)}, f32[8,400,128]{2,1,0:T(8,128)}, f32[400,128]{1,0:T(8,128)}) custom-call(s32[8,1,8704]{2,1,0:T(1,128)} %broadcast_in_dim.12.edges_hbm, s32[8]{0:T(128)} %slice_reduce_fusion.count_ref, s32[8,1,1024]{2,1,0:T(1,128)} %broadcast_in_dim.13.negs_hbm, s32[8,32,256]{2,1,0:T(8,128)} %bitcast.29, ...), custom_call_target="tpu_custom_call" | custom-call | tf_op jit(solution)/shard_map/bucket/pallas_call | solution.py:346
  538.5 100.3 %exchange.12 = (f32[4096,128]{1,0:T(8,128)}, f32[1024,1]{1,0:T(8,128)}, f32[128,512]{1,0:T(8,128)}, f32[128,1]{1,0:T(8,128)}, f32[1,128]{1,0:T(1,128)}, /*index=5*/bf16[32,400,128]{2,1,0:T(8,128)(2,1)}) custom-call(f32[32,400,128]{2,1,0:T(8,128)} %get-tuple-element.119.tail_ref, f32[8,400,128]{2,1,0:T(8,128)} %get-tuple-element.120.head_hbm, ...), custom_call_target="tpu_custom_call" | custom-call | tf_op jit(solution)/shard_map/exchange/pallas_call | solution.py:620
  638.8 39.3 %bucket.13 = (f32[32,400,128]{2,1,0:T(8,128)}, f32[8,400,128]{2,1,0:T(8,128)}, f32[400,128]{1,0:T(8,128)}) custom-call(s32[8,1,8704]{2,1,0:T(1,128)} %broadcast_in_dim.12.edges_hbm, s32[8]{0:T(128)} %slice_reduce_fusion.count_ref, s32[8,1,1024]{2,1,0:T(1,128)} %broadcast_in_dim.13.negs_hbm, s32[8,32,256]{2,1,0:T(8,128)} %bitcast.30, ...), custom_call_target="tpu_custom_call" | custom-call | tf_op jit(solution)/shard_map/bucket/pallas_call | solution.py:346
  678.1 87.2 %exchange.13 = (f32[4096,128]{1,0:T(8,128)}, f32[1024,1]{1,0:T(8,128)}, f32[128,512]{1,0:T(8,128)}, f32[128,1]{1,0:T(8,128)}, f32[1,128]{1,0:T(1,128)}, /*index=5*/bf16[32,400,128]{2,1,0:T(8,128)(2,1)}) custom-call(f32[32,400,128]{2,1,0:T(8,128)} %get-tuple-element.127.tail_ref, f32[8,400,128]{2,1,0:T(8,128)} %get-tuple-element.128.head_hbm, ...), custom_call_target="tpu_custom_call" | custom-call | tf_op jit(solution)/shard_map/exchange/pallas_call | solution.py:620
  765.3 31.2 %bucket.14 = (f32[32,400,128]{2,1,0:T(8,128)}, f32[8,400,128]{2,1,0:T(8,128)}, f32[400,128]{1,0:T(8,128)}) custom-call(s32[8,1,8704]{2,1,0:T(1,128)} %broadcast_in_dim.12.edges_hbm, s32[8]{0:T(128)} %slice_reduce_fusion.count_ref, s32[8,1,1024]{2,1,0:T(1,128)} %broadcast_in_dim.13.negs_hbm, s32[8,32,256]{2,1,0:T(8,128)} %bitcast.31, ...), custom_call_target="tpu_custom_call" | custom-call | tf_op jit(solution)/shard_map/bucket/pallas_call | solution.py:346
  796.5 73.5 %exchange.14 = (f32[4096,128]{1,0:T(8,128)}, f32[1024,1]{1,0:T(8,128)}, f32[128,512]{1,0:T(8,128)}, f32[128,1]{1,0:T(8,128)}, f32[1,128]{1,0:T(1,128)}, /*index=5*/bf16[32,400,128]{2,1,0:T(8,128)(2,1)}) custom-call(f32[32,400,128]{2,1,0:T(8,128)} %get-tuple-element.135.tail_ref, f32[8,400,128]{2,1,0:T(8,128)} %get-tuple-element.136.head_hbm, ...), custom_call_target="tpu_custom_call" | custom-call | tf_op jit(solution)/shard_map/exchange/pallas_call | solution.py:620
  870.0 33.8 %bucket.15 = (f32[32,400,128]{2,1,0:T(8,128)}, f32[8,400,128]{2,1,0:T(8,128)}, f32[400,128]{1,0:T(8,128)}) custom-call(s32[8,1,8704]{2,1,0:T(1,128)} %broadcast_in_dim.12.edges_hbm, s32[8]{0:T(128)} %slice_reduce_fusion.count_ref, s32[8,1,1024]{2,1,0:T(1,128)} %broadcast_in_dim.13.negs_hbm, s32[8,32,256]{2,1,0:T(8,128)} %bitcast.32, ...), custom_call_target="tpu_custom_call" | custom-call | tf_op jit(solution)/shard_map/bucket/pallas_call | solution.py:346
  903.9 115.9 %exchange.15 = (f32[32,416,128]{2,1,0:T(8,128)}, f32[128,512]{1,0:T(8,128)}, f32[1,128]{1,0:T(1,128)}) custom-call(f32[32,400,128]{2,1,0:T(8,128)} %get-tuple-element.143.tail_ref, f32[8,400,128]{2,1,0:T(8,128)} %get-tuple-element.144.head_hbm, f32[2,200,128]{2,1,0:T(8,128)} %bitcast.37, f32[4096,128]{1,0:T(8,128)} %get-tuple-element.140.ent_hbm, ...), custom_call_target="tpu_custom_call" | custom-call | tf_op jit(solution)/shard_map/exchange/pallas_call | solution.py:620
  1019.8 0.7 concatenate.3
  1020.5 2.3 slice.10
  1022.8 9.6 finish.1
  1032.5 0.7 reshape.50
  1033.2 1.6 slice_bitcast_fusion
  1034.9 0.7 dynamic-slice_reduce_fusion
  (25 shorter events, 1.4 us)
Async XLA Ops:
  1.4 75.7 %collective-permute-start = (f32[1024]{0:T(1024)S(1)}, f32[1024]{0:T(1024)S(1)}, u32[]{:S(2)}, u32[]{:S(2)}) collective-permute-start(f32[1024]{0:T(1024)S(1)} %dynamic_slice.10), channel_id=1, source_target_pairs={{0,1},{2,3},{4,5},{6,7},{8,9},{10,11},{12,13},{14,15},{17,16},{19,... | collective-permute-start | bytes 12296 | tf_op jit(solution)/shard_map/ppermute | solution.py:849
  21.3 16.7 %copy-start = (s32[8,8704]{1,0:T(8,128)S(1)}, s32[8,8704]{1,0:T(8,128)}, u32[]{:S(2)}) copy-start(s32[8,8704]{1,0:T(8,128)} %get-tuple-element.82) | copy-start | bytes 835588
  21.3 17.6 %copy-start.2 = (s32[8,1024]{1,0:T(8,128)S(1)}, s32[8,1024]{1,0:T(8,128)}, u32[]{:S(2)}) copy-start(s32[8,1024]{1,0:T(8,128)} %get-tuple-element.84) | copy-start | bytes 98308
  21.3 18.2 %copy-start.1 = (s32[8,8192]{1,0:T(8,128)S(1)}, s32[8,8192]{1,0:T(8,128)}, u32[]{:S(2)}) copy-start(s32[8,8192]{1,0:T(8,128)} %get-tuple-element.85) | copy-start | bytes 786436
  903.8 115.9 %copy-start.3 = (f32[1,128]{1,0:T(1,128)S(1)}, f32[1,128]{1,0:T(1,128)}, u32[]{:S(2)}) copy-start(f32[1,128]{1,0:T(1,128)} %get-tuple-element.152) | copy-start | bytes 1540
  903.8 115.9 %copy-start.4 = (f32[1,128]{1,0:T(1,128)S(1)}, f32[1,128]{1,0:T(1,128)}, u32[]{:S(2)}) copy-start(f32[1,128]{1,0:T(1,128)} %get-tuple-element.153) | copy-start | bytes 1540
  903.8 115.9 %copy-start.5 = (f32[1,128]{1,0:T(1,128)S(1)}, f32[1,128]{1,0:T(1,128)}, u32[]{:S(2)}) copy-start(f32[1,128]{1,0:T(1,128)} %get-tuple-element.154) | copy-start | bytes 1540
  903.8 115.9 %copy-start.6 = (f32[1,128]{1,0:T(1,128)S(1)}, f32[1,128]{1,0:T(1,128)}, u32[]{:S(2)}) copy-start(f32[1,128]{1,0:T(1,128)} %get-tuple-element.155) | copy-start | bytes 1540
  903.8 115.9 %copy-start.7 = (f32[1,128]{1,0:T(1,128)S(1)}, f32[1,128]{1,0:T(1,128)}, u32[]{:S(2)}) copy-start(f32[1,128]{1,0:T(1,128)} %get-tuple-element.156) | copy-start | bytes 1540
  903.8 115.9 %copy-start.8 = (f32[1,128]{1,0:T(1,128)S(1)}, f32[1,128]{1,0:T(1,128)}, u32[]{:S(2)}) copy-start(f32[1,128]{1,0:T(1,128)} %get-tuple-element.157) | copy-start | bytes 1540
  903.8 115.9 %copy-start.9 = (f32[1,128]{1,0:T(1,128)S(1)}, f32[1,128]{1,0:T(1,128)}, u32[]{:S(2)}) copy-start(f32[1,128]{1,0:T(1,128)} %get-tuple-element.158) | copy-start | bytes 1540
